TPU v7x, 8 devices: a whole 2x2x1 slice. The times are simulated.
8 devices in a mesh: part: 1 (over z), dp: 2 (over y), tp: 4 (over x, core).
Axes of the slice: x: 2, y: 2, z: 1, core: 2. Of those that a mesh axis runs over, the one named last changes fastest.
Arguments:
- hidden: bfloat16 [4, 256, 1280], P(('part', 'dp'))
- weight: bfloat16 [1280, 65536], P(None, 'tp')
- labels: int32 [4, 32], P(('part', 'dp'))
- in_len: int32 [4], P(('part', 'dp'))
- lab_len: int32 [4], P(('part', 'dp'))
Outputs:
- output 1: float32 [4], P(('part', 'dp'))
- output 2: float32 [1280, 65536], P(('part', 'dp'), 'tp')
- output 3: float32 [4, 256, 1280], P(('part', 'dp'))
All inputs are finite; a program needn't handle non-finite values.
Results may differ from a plain program's by a relative error of at most 0.00238044.
Values are sent between devices in bfloat16 or wider.
A program may use at most 1 GiB of HBM per device.

v0:
```python
import functools

import jax
import jax.numpy as jnp
from jax import lax
from jax.experimental import pallas as pl
from jax.experimental.pallas import tpu as pltpu
from jax.sharding import PartitionSpec as P

NEG_BIG = -1.0e30
LOG2E = 1.4426950408889634
F32 = jnp.float32
BF16 = jnp.bfloat16
TILE = 512
LANES = 128
MIB = 1 << 20


def vmem_spec():
    return pl.BlockSpec(memory_space=pltpu.VMEM)


def smem_spec():
    return pl.BlockSpec(memory_space=pltpu.SMEM)


def any_spec():
    return pl.BlockSpec(memory_space=pl.ANY)


def kernel_call(*args, **kw):
    return pl.pallas_call(*args, **kw)


def params():
    return pltpu.CompilerParams(vmem_limit_bytes=56 * MIB)


def label_col(meta_refs, i):
    n_slots = meta_refs[0].shape[1] - 1
    seq, item = i // n_slots, lax.rem(i, n_slots)
    n_seq = meta_refs[0].shape[0]
    at = lax.max(item - 1, 0)
    col = meta_refs[0][lax.rem(seq, n_seq), at]
    for k in range(1, len(meta_refs)):
        col = jnp.where(seq >= k * n_seq, meta_refs[k][lax.rem(seq, n_seq), at], col)
    return jnp.where(item == 0, 0, col)


def build_lists(meta_refs, vocab_loc, head, nxt):
    n_items = len(meta_refs) * meta_refs[0].shape[0] * (meta_refs[0].shape[1] - 1)
    col_start = lax.axis_index("tp") * vocab_loc
    n_tiles = vocab_loc // TILE

    def clear(i, c):
        head[i] = -1
        return c

    lax.fori_loop(0, n_tiles, clear, 0)

    def insert(i, c):
        loc = label_col(meta_refs, i) - col_start
        tile = lax.max(loc, 0) // TILE

        @pl.when((loc >= 0) & (loc < vocab_loc))
        def _():
            nxt[i] = head[tile]
            head[tile] = i

        return c

    lax.fori_loop(0, n_items, insert, 0)
    return col_start


def walk_list(head, nxt, tile, visit):
    def body(i):
        visit(i)
        return nxt[i]

    lax.while_loop(lambda i: i >= 0, body, head[tile])


class TileStream:
    def __init__(self, src, buf, sem, depth, n_tiles, view):
        self.src, self.buf, self.sem, self.depth, self.n, self.view = src, buf, sem, depth, n_tiles, view

    def copy(self, j):
        slot = lax.rem(j, self.depth)
        return pltpu.make_async_copy(self.view(self.src, j), self.buf.at[slot], self.sem.at[slot])

    def prime(self):
        for j in range(min(self.depth - 1, self.n)):
            self.copy(j).start()

    def get(self, j):
        self.copy(j).wait()

        @pl.when(j + self.depth - 1 < self.n)
        def _():
            self.copy(j + self.depth - 1).start()

        return lax.rem(j, self.depth)


def w_view(src, j, n=1):
    return src.at[:, pl.ds(pl.multiple_of(j * n * TILE, TILE), n * TILE)]


def z_view(src, j, n):
    return src.at[pl.ds(j * n, n)]


def exact_zero(total):
    return jnp.minimum(total[0:16] + total[16:32], 0.0).astype(BF16)


def after(lhs, zero):
    if zero is None:
        return lhs
    corner = lhs[0:16, 0:LANES] + zero
    return jnp.concatenate([jnp.concatenate([corner, lhs[0:16, LANES:]], axis=1), lhs[16:]], axis=0)


def unit_stats(z, m_ref, s_ref, r0):
    n_chunks = z.shape[1] // LANES
    total = None
    for b in range(z.shape[0] // 32):
        zb = [z[32 * b:32 * (b + 1), k * LANES:(k + 1) * LANES] for k in range(n_chunks)]
        rows = slice(r0 + 32 * b, r0 + 32 * (b + 1))
        m_old = m_ref[rows, :]
        m_new = functools.reduce(jnp.maximum, zb, m_old)
        s_new = s_ref[rows, :] * jnp.exp(m_old - m_new)
        for part in zb:
            s_new = s_new + jnp.exp(part - m_new)
        m_ref[rows, :] = m_new
        s_ref[rows, :] = s_new
        total = s_new if total is None else total + s_new
    return exact_zero(total)


def z_group(h_ref, w, z_out, m_ref, s_ref):
    n_tiles = z_out.shape[0]
    n = h_ref.shape[0] // 2
    zeros = []
    for t in range(n_tiles):
        for r in range(2):
            rows = slice(r * n, (r + 1) * n)
            lhs = after(h_ref[rows, :], zeros[-2] if len(zeros) >= 2 else None)
            z = jnp.dot(lhs, w[:, t * TILE:(t + 1) * TILE], preferred_element_type=F32)
            z_out[t, rows, :] = z
            zeros.append(unit_stats(z, m_ref, s_ref, r * n))


def emit_stats(m_ref, s_ref, out_ref, base):
    row_m = jnp.max(m_ref[...], axis=1, keepdims=True)
    row_s = jnp.sum(s_ref[...] * jnp.exp(m_ref[...] - row_m), axis=1, keepdims=True)
    rows = m_ref.shape[0]
    for k, v in enumerate((row_m, row_s)):
        flat = jnp.broadcast_to(v, (rows, LANES)).T
        for p in range(rows // LANES):
            at = base + 8 * k + p
            out_ref[at:at + 1, :] = flat[0:1, p * LANES:(p + 1) * LANES]


def z_own_kernel(n_slots, h_ref, w_hbm, labels_ref, in_len_ref, lab_len_ref, z_hbm, pick_ref, meta_ref, wbuf, wsem, zbuf, zsem, m_ref, s_ref, head, nxt):
    n_tiles = z_hbm.shape[0]
    rows = h_ref.shape[0]
    n_seq = meta_ref.shape[0]
    frames = rows // n_seq
    n_lab = n_slots - 1
    for q in range(n_seq):
        def put(k, c, q=q):
            meta_ref[q, k] = labels_ref[q, k]
            return c

        lax.fori_loop(0, n_lab, put, 0)
        meta_ref[q, n_lab] = in_len_ref[q]
        meta_ref[q, n_lab + 1] = lab_len_ref[q]
    group = zbuf.shape[1]
    stream = TileStream(w_hbm, wbuf, wsem, wbuf.shape[0], n_tiles // group, lambda src, j: w_view(src, j, group))
    stream.prime()
    col_start = build_lists([meta_ref], n_tiles * TILE, head, nxt)
    m_ref[...] = jnp.full(m_ref.shape, NEG_BIG, F32)
    s_ref[...] = jnp.zeros(s_ref.shape, F32)
    pick_ref[...] = jnp.zeros(pick_ref.shape, F32)
    lane = lax.broadcasted_iota(jnp.int32, (frames, LANES), 1)

    def out_copy(j):
        slot = lax.rem(j, zbuf.shape[0])
        return pltpu.make_async_copy(zbuf.at[slot], z_view(z_hbm, j, group), zsem.at[slot])

    def step(j, c):
        slot = stream.get(j)

        @pl.when(j >= 3)
        def _():
            out_copy(j - 3).wait()

        zslot = lax.rem(j, zbuf.shape[0])
        z_group(h_ref, wbuf.at[slot], zbuf.at[zslot], m_ref, s_ref)
        out_copy(j).start()

        for t in range(group):
            def visit(i, t=t):
                seq, item = i // n_slots, lax.rem(i, n_slots)
                off = label_col([meta_ref], i) - col_start - (j * group + t) * TILE
                blk = off // LANES
                r0 = pl.multiple_of(seq * frames, frames)
                zb = zbuf[zslot, t, pl.ds(r0, frames), pl.ds(pl.multiple_of(blk * LANES, LANES), LANES)]
                at = item + 64 * seq
                moved = pltpu.roll(zb, lax.rem(at - (off - blk * LANES) + 2 * LANES, LANES), 1)
                pick_ref[0:frames, :] = jnp.where(lane == at, moved, pick_ref[0:frames, :])

            walk_list(head, nxt, j * group + t, visit)
        return c

    n_groups = n_tiles // group
    lax.fori_loop(0, n_groups, step, 0)
    emit_stats(m_ref, s_ref, pick_ref, frames)
    for j in range(n_groups - 3, n_groups):
        out_copy(j).wait()


def z_oth_loop(lo, hi, h_ref, w_hbm, z_hbm, wbuf, wsem, zbuf, zsem, m_ref, s_ref, sections):
    group = zbuf.shape[1]
    lo, n_groups = lo // group, (hi - lo) // group
    stream = TileStream(w_hbm, wbuf, wsem, wbuf.shape[0], n_groups, lambda src, j: w_view(src, lo + j, group))
    stream.prime()

    def out_copy(j):
        slot = lax.rem(j, zbuf.shape[0])
        return pltpu.make_async_copy(zbuf.at[slot], z_view(z_hbm, lo + j, group), zsem.at[slot])

    base = 0
    for n, side, make_carry in sections:
        carry = make_carry()

        def step(k, c, base=base, side=side):
            j = base + k
            slot = stream.get(j)

            @pl.when(j >= 3)
            def _():
                out_copy(j - 3).wait()

            z_group(h_ref, wbuf.at[slot], zbuf.at[lax.rem(j, zbuf.shape[0])], m_ref, s_ref)
            c = side(k, c)
            out_copy(j).start()
            return c

        last = lax.fori_loop(0, n, step, carry)
        yield last
        base += n
    for j in range(max(n_groups - 3, 0), n_groups):
        out_copy(j).wait()


def join_rows(h_got, h_core, h_ref):
    n = h_got.shape[0]
    core = lax.rem(lax.axis_index("tp"), 2)
    h_ref[pl.ds(pl.multiple_of(core * n, n), n), :] = h_got[...]
    h_ref[pl.ds(pl.multiple_of((1 - core) * n, n), n), :] = h_core[...]


def z_first_kernel(lo, hi, h_got, h_core, w_hbm, z_hbm, m_ref, s_ref, h_ref, wbuf, wsem, zbuf, zsem):
    join_rows(h_got, h_core, h_ref)
    m_ref[...] = jnp.full(m_ref.shape, NEG_BIG, F32)
    s_ref[...] = jnp.zeros(s_ref.shape, F32)
    for _ in z_oth_loop(lo, hi, h_ref, w_hbm, z_hbm, wbuf, wsem, zbuf, zsem, m_ref, s_ref, [((hi - lo) // zbuf.shape[1], lambda k, c: c, lambda: 0)]):
        pass


def z_lattice_kernel(lo, hi, n_lat, n_lab, h_ref, w_hbm, m_in, s_in, p0, p1, p2, p3, meta_ref, z_in,
                     z_hbm, stats_ref, occ_ref, loss_ref, m_ref, s_ref,
                     wbuf, wsem, zbuf, zsem, e_lab, e_blk, a_lab, a_blk, b_lab, b_blk, o_t):
    n_blk = e_lab.shape[0]
    frames = n_blk * 64
    m_ref[...] = m_in[...]
    s_ref[...] = s_in[...]
    lane128 = lax.broadcasted_iota(jnp.int32, (LANES, LANES), 1)
    row32 = lax.broadcasted_iota(jnp.int32, (n_lab, LANES), 0)
    row8 = lax.broadcasted_iota(jnp.int32, (8, LANES), 0)
    lane32 = lax.broadcasted_iota(jnp.int32, (n_lab, LANES), 1)
    lane8 = lax.broadcasted_iota(jnp.int32, (8, LANES), 1)
    n_seq = meta_ref.shape[0]
    labs = jnp.zeros((n_lab, LANES), jnp.int32)
    lab_row = jnp.zeros((8, LANES), jnp.int32)
    live8 = jnp.zeros((8, LANES), jnp.int32)
    used8 = jnp.zeros((8, LANES), jnp.int32)
    for s in range(n_seq):
        for k in range(n_lab):
            labs = jnp.where((row32 == k) & (lane32 == s), meta_ref[s, k], labs)
            lab_row = jnp.where((row8 == s) & (lane8 == k), meta_ref[s, k], lab_row)
        live8 = jnp.where(lane8 == s, meta_ref[s, n_lab], live8)
        used8 = jnp.where(lane8 == s, meta_ref[s, n_lab + 1], used8)
    live32 = jnp.broadcast_to(live8[0:1], (n_lab, LANES))
    used32 = jnp.broadcast_to(used8[0:1], (n_lab, LANES))
    skip_dn = labs != pltpu.roll(labs, 1, 0)
    skip_up = labs != pltpu.roll(labs, n_lab - 1, 0)
    end_lab = row32 == used32 - 1
    end_blk = row32 == used32
    end_top = (row8 == 0) & (used8 == n_lab)
    shift0 = jnp.zeros((1, LANES), F32)
    seq1 = lane8[0:1] >= 64
    half_len = jnp.where(seq1, meta_ref[1, n_lab], meta_ref[0, n_lab])
    for j in range(n_blk):
        part = functools.reduce(jnp.add, [p[pl.ds(64 * j, 64), :] for p in (p0, p1, p2, p3)])
        blk = jnp.concatenate([part, pltpu.roll(part, 64, 1)], axis=0)
        blk = jnp.where(lane128 <= n_lab, blk, NEG_BIG)
        x = blk.T
        top = jnp.max(x[0:n_lab + 8], axis=0, keepdims=True)
        e_blk[j] = jnp.broadcast_to((x[0:1] - top) * LOG2E, (8, LANES))
        e_lab[j] = (pltpu.roll(x, LANES - 1, 0)[0:n_lab] - top) * LOG2E
        shift0 = shift0 + jnp.where(lax.rem(lane8[0:1], 64) + 64 * j < half_len, top, 0.0)
    shift_seq0 = jnp.sum(jnp.where(seq1, 0.0, shift0), axis=1, keepdims=True)
    shift_seq1 = jnp.sum(jnp.where(seq1, shift0, 0.0), axis=1, keepdims=True)

    def lse2(a, b):
        hi_v = jnp.maximum(a, b)
        return hi_v + jnp.log2(1.0 + jnp.exp2(jnp.minimum(a, b) - hi_v))

    def lse3(a, b, c):
        hi_v = jnp.maximum(a, b)
        lo_v = jnp.minimum(a, b)
        top = jnp.maximum(hi_v, c)
        mid = jnp.minimum(hi_v, c)
        return top + jnp.log2(1.0 + (jnp.exp2(lo_v - top) + jnp.exp2(mid - top)))

    def emission(t):
        j, u = t // 64, lax.rem(t, 64)
        idx32 = jnp.where(lane32 == 1, 64 + u, u)
        idx8 = jnp.where(lane8 == 1, 64 + u, u)
        el = jnp.take_along_axis(e_lab[j], idx32, axis=1)
        eb = jnp.take_along_axis(e_blk[j], idx8, axis=1)
        return el, eb

    neg32 = jnp.full((n_lab, LANES), NEG_BIG, F32)
    neg8 = jnp.full((8, LANES), NEG_BIG, F32)
    start32 = jnp.where(row32 == 0, 0.0, NEG_BIG)
    fin_b = jnp.where(end_blk, 0.0, NEG_BIG)
    fin_t = jnp.where(end_top, 0.0, NEG_BIG)
    skip_dn = skip_dn & (row32 > 0)
    skip_up = skip_up & (row32 < n_lab - 1)

    def lat_step(i, carry):
        al, ab, at, bl, bb, bt = carry
        el, eb = emission(i)
        eb32 = jnp.broadcast_to(eb[0:1], (n_lab, LANES))
        rolled = pltpu.roll(al, 1, 0)
        prev = jnp.where(row32 == 0, NEG_BIG, rolled)
        prev_t = jnp.where(row8 == 0, rolled[0:8], NEG_BIG)
        nl = lse3(al, ab, jnp.where(skip_dn, rolled, NEG_BIG))
        nb = lse2(ab, prev)
        nt = lse2(at, prev_t)
        a_lab[i] = nl
        a_blk[i, 0:n_lab] = nb
        a_blk[i, n_lab:n_lab + 8] = nt
        al = jnp.where(i < live32, el + nl, al)
        ab = jnp.where(i < live32, eb32 + nb, ab)
        at = jnp.where(i < live8, eb + nt, at)
        t = frames - 1 - i
        fl, fb = emission(t)
        fb32 = jnp.broadcast_to(fb[0:1], (n_lab, LANES))
        last = row32 == n_lab - 1
        up_l = jnp.where(skip_up, pltpu.roll(bl, n_lab - 1, 0), NEG_BIG)
        up_b = jnp.where(last, jnp.broadcast_to(bt[0:1], (n_lab, LANES)), pltpu.roll(bb, n_lab - 1, 0))
        ml = fl + lse3(bl, up_b, up_l)
        mb = fb32 + lse2(bb, bl)
        mt = fb + bt
        bl = jnp.where(t < live32, ml, bl)
        bb = jnp.where(t < live32, mb, bb)
        bt = jnp.where(t < live8, mt, bt)
        b_lab[t] = bl
        b_blk[t, 0:n_lab] = bb
        b_blk[t, n_lab:n_lab + 8] = bt
        return al, ab, at, bl, bb, bt

    group = zbuf.shape[1]
    n_lat_groups = n_lat // group
    per_tile = frames // n_lat_groups

    def lattice_side(k, carry):
        for u in range(per_tile):
            carry = lat_step(k * per_tile + u, carry)
        return carry

    n_occ = (hi - lo - n_lat) // group
    occ_group = frames // n_occ // 64
    back32 = jnp.where(lane32 >= 64, 1, 0)
    back8 = jnp.where(lane8 >= 64, 1, 0)
    run = z_oth_loop(lo, hi, h_ref, w_hbm, z_hbm, wbuf, wsem, zbuf, zsem, m_ref, s_ref,
                     [(n_lat_groups, lattice_side, lambda: (neg32, start32, neg8, neg32, fin_b, fin_t)),
                      (n_occ, lambda k, c: occ_side(k, c), lambda: 0)])
    al, ab, at, _, _, _ = next(run)

    lasts = [jnp.where(end, v, NEG_BIG) for end, v in ((end_lab, al), (end_blk, ab), (end_top, at))]
    top = functools.reduce(jnp.maximum, [jnp.max(v, axis=0, keepdims=True) for v in lasts])
    total = functools.reduce(jnp.add, [jnp.sum(jnp.exp2(v - top), axis=0, keepdims=True) for v in lasts])
    loss = -(top + jnp.log2(total))
    loss32 = jnp.broadcast_to(loss, (n_lab, LANES))
    loss8 = jnp.broadcast_to(loss, (8, LANES))
    lane1 = lane8[0:1]
    loss_ref[...] = jnp.broadcast_to(loss * (1.0 / LOG2E) - jnp.where(lane1 == 0, shift_seq0, jnp.where(lane1 == 1, shift_seq1, 0.0)), (8, LANES))

    def occ_frame(i, u, acc_l, acc_b):
        occ_l = jnp.where(i < live32, jnp.exp2(a_lab[i] + b_lab[i] + loss32), 0.0)
        occ_b = jnp.exp2(a_blk[i, 0:n_lab] + b_blk[i, 0:n_lab] + loss32)
        occ_u = jnp.exp2(a_blk[i, n_lab:n_lab + 8] + b_blk[i, n_lab:n_lab + 8] + loss8)
        blank = jnp.sum(occ_b, axis=0, keepdims=True) + occ_u[0:1]
        blank = jnp.where(i < live8, jnp.broadcast_to(blank, (8, LANES)), 0.0)
        acc_l = jnp.where(lax.rem(lane32, 64) == u, jnp.take_along_axis(occ_l, back32, axis=1), acc_l)
        acc_b = jnp.where(lax.rem(lane8, 64) == u, jnp.take_along_axis(blank, back8, axis=1), acc_b)
        return acc_l, acc_b

    def occ_side(k, c):
        for g in range(occ_group):
            j = k * occ_group + g
            acc_l = jnp.zeros((n_lab, LANES), F32)
            acc_b = jnp.zeros((8, LANES), F32)
            for u in range(64):
                acc_l, acc_b = occ_frame(j * 64 + u, u, acc_l, acc_b)
            o_t[j, 0:n_lab] = acc_l
            o_t[j, n_lab:n_lab + 8] = acc_b
            o_t[j, 8 + n_lab:LANES] = jnp.zeros((LANES - 8 - n_lab, LANES), F32)
        return c

    for _ in run:
        pass
    emit_stats(m_ref, s_ref, stats_ref, 0)
    row128 = lax.broadcasted_iota(jnp.int32, (LANES, LANES), 0)
    inner = (row128 < n_lab) & (lane128 < n_lab)
    same = []
    for s in range(n_seq):
        down = jnp.full((n_lab, LANES), -1, jnp.int32)
        for k in range(n_lab):
            down = jnp.where(row32 == k, meta_ref[s, k], down)
        down = jnp.concatenate([down, jnp.full((LANES - n_lab, LANES), -1, jnp.int32)], axis=0)
        across = jnp.broadcast_to(lab_row[s:s + 1], (LANES, LANES))
        same.append(jnp.where((inner & (down == across)) | (row128 == lane128), 1.0, 0.0))
    for j in range(n_blk):
        y = o_t[j].T
        for s in range(2):
            occ_ref[pl.ds(s * frames + 64 * j, 64), :] = jnp.dot(y[64 * s:64 * (s + 1), :], same[s], precision=lax.Precision.HIGHEST, preferred_element_type=F32)


def spread_lse(refs, base, meta_ref, lse_ref, r0, frames):
    m = functools.reduce(jnp.maximum, [r[base:base + 8, :] for r in refs])
    tot = functools.reduce(jnp.add, [r[base + 8:base + 16, :] * jnp.exp(r[base:base + 8, :] - m) for r in refs])
    lse = m + jnp.log(tot)
    t = lax.broadcasted_iota(jnp.int32, (LANES, LANES), 0)
    n_part = frames // LANES
    sums = []
    for q in range(meta_ref.shape[0]):
        live_sum = jnp.zeros((1, LANES), F32)
        for p in range(n_part):
            at = q * n_part + p
            part = jnp.broadcast_to(lse[at:at + 1, :], (LANES, LANES)).T
            live = t + p * LANES < meta_ref[q, meta_ref.shape[1] - 2]
            lse_ref[r0 + at * LANES:r0 + (at + 1) * LANES, :] = jnp.where(live, part, 1.0e30)
            live_sum = live_sum + jnp.sum(jnp.where(live, part, 0.0), axis=0, keepdims=True)
        sums.append(live_sum)
    return sums


def patch_tile(n_slots, frames, meta_refs, col_start, j, i, z_block, lse_ref, occ_ref, g_ref, g_col, lane):
    seq, item = i // n_slots, lax.rem(i, n_slots)
    off = label_col(meta_refs, i) - col_start - j * TILE
    blk = off // LANES
    r0 = pl.multiple_of(seq * frames, frames)
    c0 = pl.multiple_of(blk * LANES, LANES)
    zb = z_block(seq, c0)
    slot_lane = jnp.where(item == 0, n_slots - 1, item - 1)
    occ = jnp.sum(jnp.where(lane == slot_lane, occ_ref[pl.ds(r0, frames), :], 0.0), axis=1, keepdims=True)
    fresh = jnp.exp(zb - lse_ref[pl.ds(r0, frames), :]) - occ
    gc = pl.multiple_of(g_col + c0, LANES)
    old = g_ref[pl.ds(r0, frames), pl.ds(gc, LANES)].astype(F32)
    g_ref[pl.ds(r0, frames), pl.ds(gc, LANES)] = jnp.where(lane == off - blk * LANES, fresh, old).astype(BF16)


def softmax_unit(z, z_row, lse_ref, out, r0, n, c0):
    total = None
    for b in range(n // 32):
        lse = lse_ref[r0 + 32 * b:r0 + 32 * (b + 1), :]
        for k in range(TILE // LANES):
            e = jnp.exp(z[z_row + 32 * b:z_row + 32 * (b + 1), k * LANES:(k + 1) * LANES] - lse)
            out[r0 + 32 * b:r0 + 32 * (b + 1), c0 + k * LANES:c0 + (k + 1) * LANES] = e.astype(BF16)
            total = e if total is None else total + e
    return exact_zero(total)


def grad_h_kernel(n_slots, z_hbm, w_hbm, st0, st1, st2, st3, occ_ref, part_loss, meta_ref, keep_ref, send_ref, loss_ref, g_hbm,
                  wbuf, wsem, zbuf, zsem, acc, lse_ref, g0, g1, gsem, head, nxt):
    n_tiles, rows = z_hbm.shape[0], z_hbm.shape[1]
    frames = rows // meta_ref.shape[0]
    meta_refs = [meta_ref]
    group = zbuf.shape[1]
    n_groups = n_tiles // group
    stream = TileStream(w_hbm, wbuf, wsem, wbuf.shape[0], n_groups, lambda src, j: w_view(src, j, group))
    zs = TileStream(z_hbm, zbuf, zsem, zbuf.shape[0], n_groups, lambda src, j: z_view(src, j, group))
    zs.prime()
    stream.prime()
    col_start = build_lists(meta_refs, n_tiles * TILE, head, nxt)
    sums = spread_lse([st0, st1, st2, st3], frames, meta_ref, lse_ref, 0, frames)
    lane1 = lax.broadcasted_iota(jnp.int32, (8, LANES), 1)
    loss_ref[...] = part_loss[...] + jnp.where(lane1 == 0, sums[0], sums[1])
    lane = lax.broadcasted_iota(jnp.int32, (frames, LANES), 1)

    def patch(j, slot, g):
        for t in range(group):
            def z_block(seq, c0, t=t):
                return zbuf[slot, t, pl.ds(pl.multiple_of(seq * frames, frames), frames), pl.ds(c0, LANES)]

            walk_list(head, nxt, j * group + t,
                      lambda i, t=t, z_block=z_block: patch_tile(n_slots, frames, meta_refs, col_start, j * group + t, i, z_block, lse_ref, occ_ref, g, t * TILE, lane))

    def make_g(slot, u, g):
        t, r = u // 2, u % 2
        return softmax_unit(zbuf.at[slot, t], r * rows // 2, lse_ref, g, r * rows // 2, rows // 2, t * TILE)

    acc[...] = jnp.zeros(acc.shape, F32)
    slot0 = zs.get(0)
    for u in range(2 * group):
        make_g(slot0, u, g0)
    patch(0, slot0, g0)
    n_units = acc.shape[0] // 256

    def g_copy(j, g, k):
        return pltpu.make_async_copy(g, g_hbm.at[j], gsem.at[k])

    def half(j, g_now, g_next, k):
        slot = stream.get(j)
        nj = lax.min(j + 1, n_groups - 1)

        @pl.when(j + 1 < n_groups)
        def _():
            zs.get(nj)

        @pl.when(j >= 1)
        def _():
            g_copy(j - 1, g_next, 1 - k).wait()

        g_copy(j, g_now, k).start()

        zslot = lax.rem(nj, zbuf.shape[0])
        zero = None
        for u in range(n_units):
            d_rows = slice(u * 256, (u + 1) * 256)
            lhs = after(wbuf[slot, d_rows, :], zero)
            acc[d_rows, :] += lax.dot_general(lhs, g_now[...], (((1,), (1,)), ((), ())), preferred_element_type=F32)
            if u < 2 * group:
                zero = make_g(zslot, u, g_next)
        patch(nj, zslot, g_next)

    def step(i, c):
        half(2 * i, g0, g1, 0)
        half(2 * i + 1, g1, g0, 1)
        return c

    lax.fori_loop(0, n_groups // 2, step, 0)
    g_copy(n_groups - 1, g1, 1).wait()
    core = lax.rem(lax.axis_index("tp"), 2)
    n = rows // 2
    keep_ref[...] = acc[:, pl.ds(pl.multiple_of(core * n, n), n)].T
    send_ref[...] = acc[:, pl.ds(pl.multiple_of((1 - core) * n, n), n)].T


def grad_w_kernel(n_slots, g_hbm, z_hbm, h_own_ref, h_oth_ref, st0, st1, st2, st3, occ_ref, meta_ref, gw_hbm,
                  zbuf, zsem, gsem, obuf, osem, ht, lse_ref, g0, g1, head, nxt):
    n_tiles, rows = z_hbm.shape[0], z_hbm.shape[1]
    frames = rows // meta_ref.shape[0]
    d_loc = ht.shape[0]
    group = zbuf.shape[1]
    n_groups = n_tiles // group
    zs = TileStream(z_hbm, zbuf, zsem, zbuf.shape[0], n_groups, lambda src, j: z_view(src, j, group))

    def g_copy(j, g, k):
        return pltpu.make_async_copy(g_hbm.at[j], g.at[0:rows, :], gsem.at[k])

    g_copy(0, g0, 0).start()
    zs.prime()
    col_start = build_lists([meta_ref], n_tiles * TILE, head, nxt)
    d0 = pl.multiple_of(lax.axis_index("dp") * d_loc, LANES)
    ht[:, 0:rows] = h_own_ref[:, pl.ds(d0, d_loc)].T
    ht[:, rows:2 * rows] = h_oth_ref[:, pl.ds(d0, d_loc)].T
    spread_lse([st0, st1, st2, st3], 0, meta_ref, lse_ref, 0, frames)
    lane = lax.broadcasted_iota(jnp.int32, (frames, LANES), 1)
    n_units = 2 * group

    def make_g(slot, u, g):
        t, r = u // 2, u % 2
        return softmax_unit(zbuf.at[slot, t], r * rows // 2, lse_ref, g.at[rows:2 * rows, :], r * rows // 2, rows // 2, t * TILE)

    def patch(j, slot, g):
        for t in range(group):
            def z_block(seq, c0, t=t):
                return zbuf[slot, t, pl.ds(pl.multiple_of(seq * frames, frames), frames), pl.ds(c0, LANES)]

            walk_list(head, nxt, j * group + t,
                      lambda i, t=t, z_block=z_block: patch_tile(n_slots, frames, [meta_ref], col_start, j * group + t, i, z_block, lse_ref, occ_ref, g.at[rows:2 * rows, :], t * TILE, lane))

    def out_copy(j):
        slot = lax.rem(j, obuf.shape[0])
        return pltpu.make_async_copy(obuf.at[slot], w_view(gw_hbm, j, group), osem.at[slot])

    slot0 = zs.get(0)
    for u in range(n_units):
        make_g(slot0, u, g0)
    patch(0, slot0, g0)
    d_half = d_loc // 2

    def half(j, g_now, g_next, k):
        @pl.when(j >= 3)
        def _():
            out_copy(j - 3).wait()

        nj = lax.min(j + 1, n_groups - 1)

        @pl.when(j + 1 < n_groups)
        def _():
            zs.get(nj)
            g_copy(nj, g_next, 1 - k).start()

        g_copy(j, g_now, k).wait()
        slot = lax.rem(nj, zbuf.shape[0])
        oslot = lax.rem(j, obuf.shape[0])
        zero = None
        for u in range(n_units):
            t, r = u // 2, u % 2
            d_rows = slice(r * d_half, (r + 1) * d_half)
            lhs = after(ht[d_rows, :], zero)
            obuf[oslot, d_rows, t * TILE:(t + 1) * TILE] = jnp.dot(lhs, g_now[:, t * TILE:(t + 1) * TILE], preferred_element_type=F32)
            zero = make_g(slot, u, g_next)
        out_copy(j).start()
        patch(nj, slot, g_next)

    def step(i, c):
        half(2 * i, g0, g1, 0)
        half(2 * i + 1, g1, g0, 1)
        return c

    lax.fori_loop(0, n_groups // 2, step, 0)
    for j in range(n_groups - 3, n_groups):
        out_copy(j).wait()


def cost(flops, nbytes):
    return pl.CostEstimate(flops=flops, bytes_accessed=nbytes, transcendentals=0)


def solution(mesh):
    batch_axes = ("part", "dp")
    n_tp = mesh.shape["tp"]
    n_dp = mesh.shape["dp"]
    dp_swap = [(i, n_dp - 1 - i) for i in range(n_dp)]

    others = range(1, n_tp)

    def tp_xor(x, mask):
        return lax.ppermute(x, "tp", [(i, i ^ mask) for i in range(n_tp)])

    def swap_dp(x):
        return lax.ppermute(x, "dp", dp_swap)

    def local_body(hidden, w_loc, labels, in_len, lab_len):
        batch_loc, frames, model_dim = hidden.shape
        vocab_loc = w_loc.shape[1]
        n_lab = labels.shape[1]
        n_slots = n_lab + 1
        rows = batch_loc * frames
        n_tiles = vocab_loc // TILE
        d_loc = model_dim // n_dp
        dma = pltpu.SemaphoreType.DMA
        i32 = jnp.int32
        cut_a, n_lat = 8, 16
        h_own = hidden.reshape(rows, model_dim)
        core = lax.rem(lax.axis_index("tp"), 2)
        h_half = lax.dynamic_index_in_dim(h_own.reshape(2, rows // 2, model_dim), core, 0, keepdims=False)
        h_got = swap_dp(h_half)
        flops = 2 * rows * model_dim * TILE
        wbytes = model_dim * TILE * 2
        zbytes = rows * TILE * 4
        z_type = jax.ShapeDtypeStruct((n_tiles, rows, TILE), F32)
        run_type = jax.ShapeDtypeStruct((rows, LANES), F32)
        pick_type = jax.ShapeDtypeStruct((frames + 16, LANES), F32)
        meta_type = jax.ShapeDtypeStruct((batch_loc, n_slots + 1), i32)
        g_type = jax.ShapeDtypeStruct((n_tiles // 2, rows, 2 * TILE), BF16)
        stat_type = jax.ShapeDtypeStruct((16, LANES), F32)

        def w_scratch(n):
            return [pltpu.VMEM((3, model_dim, n * TILE), BF16), dma((3,))]

        def z_scratch(n):
            return [pltpu.VMEM((3, n, rows, TILE), F32), dma((3,))]

        run_scratch = [pltpu.VMEM((rows, LANES), F32), pltpu.VMEM((rows, LANES), F32)]

        def lists(n_sets):
            return [pltpu.SMEM((n_tiles,), i32), pltpu.SMEM((n_sets * batch_loc * n_slots,), i32)]

        z_own, pick, meta = kernel_call(
            functools.partial(z_own_kernel, n_slots),
            out_shape=(z_type, pick_type, meta_type),
            in_specs=[vmem_spec(), any_spec(), smem_spec(), smem_spec(), smem_spec()],
            out_specs=(any_spec(), vmem_spec(), smem_spec()),
            scratch_shapes=w_scratch(2) + z_scratch(2) + run_scratch + lists(1),
            compiler_params=params(),
            cost_estimate=cost(n_tiles * flops, n_tiles * (wbytes + zbytes)),
        )(h_own, w_loc, labels, in_len, lab_len)

        h_got, pick = lax.optimization_barrier((h_got, pick))
        h_core = tp_xor(h_got, 1)
        picks = [pick] + [tp_xor(pick, k) for k in others]

        z_part, run_m, run_s, h_oth = kernel_call(
            functools.partial(z_first_kernel, 0, cut_a),
            out_shape=(z_type, run_type, run_type, jax.ShapeDtypeStruct((rows, model_dim), BF16)),
            in_specs=[vmem_spec(), vmem_spec(), any_spec()],
            out_specs=(any_spec(), vmem_spec(), vmem_spec(), vmem_spec()),
            scratch_shapes=w_scratch(2) + z_scratch(2),
            compiler_params=params(),
            cost_estimate=cost(cut_a * flops, cut_a * (wbytes + zbytes)),
        )(h_got, h_core, w_loc)

        n_blk = frames // 64
        z_oth, stats_oth, occ, part_loss = kernel_call(
            functools.partial(z_lattice_kernel, cut_a, n_tiles, n_lat, n_lab),
            out_shape=(z_type, stat_type, run_type, jax.ShapeDtypeStruct((8, LANES), F32)),
            in_specs=[vmem_spec(), any_spec()] + [vmem_spec()] * 6 + [smem_spec(), any_spec()],
            out_specs=(any_spec(),) + (vmem_spec(),) * 3,
            input_output_aliases={9: 0},
            scratch_shapes=run_scratch + w_scratch(2) + z_scratch(2) + [
                pltpu.VMEM((n_blk, n_lab, LANES), F32), pltpu.VMEM((n_blk, 8, LANES), F32),
                pltpu.VMEM((frames, n_lab, LANES), F32), pltpu.VMEM((frames, n_lab + 8, LANES), F32),
                pltpu.VMEM((frames, n_lab, LANES), F32), pltpu.VMEM((frames, n_lab + 8, LANES), F32),
                pltpu.VMEM((n_blk, LANES, LANES), F32)],
            compiler_params=params(),
            cost_estimate=cost((n_tiles - cut_a) * flops, (n_tiles - cut_a) * (wbytes + zbytes)),
        )(h_oth, w_loc, run_m, run_s, *picks, meta, z_part)

        st_oth = [stats_oth] + [tp_xor(stats_oth, k) for k in others]
        occ_oth = swap_dp(occ)
        meta_oth = swap_dp(meta)
        keep, send, loss, g_own = kernel_call(
            functools.partial(grad_h_kernel, n_slots),
            out_shape=(jax.ShapeDtypeStruct((rows // 2, model_dim), F32), jax.ShapeDtypeStruct((rows // 2, model_dim), F32), jax.ShapeDtypeStruct((8, LANES), F32), g_type),
            in_specs=[any_spec(), any_spec()] + [vmem_spec()] * 6 + [smem_spec()],
            out_specs=(vmem_spec(),) * 3 + (any_spec(),),
            scratch_shapes=w_scratch(2) + z_scratch(2) + [pltpu.VMEM((model_dim, rows), F32), pltpu.VMEM((rows, LANES), F32),
                                                     pltpu.VMEM((rows, 2 * TILE), BF16), pltpu.VMEM((rows, 2 * TILE), BF16), dma((2,))] + lists(1),
            compiler_params=params(),
            cost_estimate=cost(n_tiles * flops, n_tiles * (wbytes + zbytes)),
        )(z_own, w_loc, *picks, occ, part_loss, meta)

        recv = tp_xor(send, 1)
        chip_sum = keep + recv
        across = tp_xor(chip_sum, 2)

        grad_weight = kernel_call(
            functools.partial(grad_w_kernel, n_slots),
            out_shape=jax.ShapeDtypeStruct((d_loc, vocab_loc), F32),
            in_specs=[any_spec(), any_spec()] + [vmem_spec()] * 7 + [smem_spec()],
            out_specs=any_spec(),
            scratch_shapes=z_scratch(2) + [
                dma((2,)), pltpu.VMEM((3, d_loc, 2 * TILE), F32), dma((3,)),
                pltpu.VMEM((d_loc, 2 * rows), BF16), pltpu.VMEM((rows, LANES), F32),
                pltpu.VMEM((2 * rows, 2 * TILE), BF16), pltpu.VMEM((2 * rows, 2 * TILE), BF16)] + lists(1),
            compiler_params=params(),
            cost_estimate=cost(n_tiles * flops, n_tiles * (2 * zbytes + d_loc * TILE * 4)),
        )(g_own, z_oth, h_own, h_oth, *st_oth, occ_oth, meta_oth)

        chip_sum, grad_weight = lax.optimization_barrier((chip_sum, grad_weight))
        full_half = chip_sum + across
        other_half = tp_xor(full_half, 1)
        grad_hidden = jnp.where(core == 0, jnp.stack([full_half, other_half]), jnp.stack([other_half, full_half])).reshape(batch_loc, frames, model_dim)
        return loss[0, :batch_loc], grad_weight, grad_hidden


    return jax.shard_map(
        local_body,
        mesh=mesh,
        in_specs=(P(batch_axes, None, None), P(None, "tp"), P(batch_axes, None), P(batch_axes), P(batch_axes)),
        out_specs=(P(batch_axes), P(batch_axes, "tp"), P(batch_axes, None, None)),
        check_vma=False,
    )
```

profile of v0, /device:TPU:0, one launch (start us, length us, event | category | flops | bytes accessed | tf_op | source)
XLA Modules:
  0.0 178.9 jit_solution(7296699010499206808)
XLA Ops:
  0.6 1.1 dynamic-slice_bitcast_fusion
  1.8 3.4 %collective-permute-start = (bf16[256,1280]{1,0:T(8,128)(2,1)S(1)}, bf16[256,1280]{1,0:T(8,128)(2,1)S(1)}, u32[]{:S(2)}, u32[]{:S(2)}) collective-permute-start(bf16[256,1280]{1,0:T(8,128)(2,1)S(1)} %dynamic-slice_bitcast_fusion), channel_id=1, source_target_pairs={{0,4},{4,0},{1,5},{5,1},{2,6},{6,2},{3,7},{7,3}} | collective-permute-start | bytes 1966088 | tf_op jit(solution)/shard_map/ppermute | solution.py:663
  5.1 35.9 %shard_map.76 = (f32[32,512,512]{2,1,0:T(8,128)}, f32[272,128]{1,0:T(8,128)}, s32[2,34]{1,0:T(2,128)}) custom-call(bf16[512,1280]{1,0:T(8,128)(2,1)} %bitcast.8, bf16[1280,16384]{1,0:T(8,128)(2,1)} %w_hbm.7, s32[2,32]{1,0:T(2,128)} %labels_ref.1, s32[2]{0:T(128)} %in_len_ref.1, s32[2]{0:T(128)} %lab_len_ref.1), custom_call_target="tpu_custom_call" | custom-call | flops 21474836480 | bytes 75497472 | tf_op jit(solution)/shard_map/pallas_call | solution.py:701
  41.1 0.5 collective-permute-start.1
  41.6 0.8 collective-permute-start.2
  42.4 0.6 collective-permute-start.3
  43.2 0.9 copy-done.1
  44.1 12.5 %shard_map.77 = (f32[32,512,512]{2,1,0:T(8,128)}, f32[512,128]{1,0:T(8,128)}, f32[512,128]{1,0:T(8,128)}, bf16[512,1280]{1,0:T(8,128)(2,1)}) custom-call(bf16[256,1280]{1,0:T(8,128)(2,1)} %copy-done, bf16[256,1280]{1,0:T(8,128)(2,1)} %copy-done.1, bf16[1280,16384]{1,0:T(8,128)(2,1)} %w_hbm.7), custom_call_target="tpu_custom_call" | custom-call | flops 5368709120 | bytes 18874368 | tf_op jit(solution)/shard_map/pallas_call | solution.py:715
  56.7 0.6 copy-done.3
  57.4 34.5 %shard_map.78 = (f32[32,512,512]{2,1,0:T(8,128)}, f32[16,128]{1,0:T(8,128)}, f32[512,128]{1,0:T(8,128)}, f32[8,128]{1,0:T(8,128)}) custom-call(bf16[512,1280]{1,0:T(8,128)(2,1)} %get-tuple-element.26.h_ref.h_oth_ref, bf16[1280,16384]{1,0:T(8,128)(2,1)} %w_hbm.7, f32[512,128]{1,0:T(8,128)} %get-tuple-element.27.m_in, ...), custom_call_target="tpu_custom_call", output_to_operand_aliasing={{0}: (9, {})} | custom-call | flops 16106127360 | bytes 56623104 | tf_op jit(solution)/shard_map/pallas_call | solution.py:726
  91.9 34.2 %shard_map.79 = (f32[256,1280]{1,0:T(8,128)}, f32[256,1280]{1,0:T(8,128)}, f32[8,128]{1,0:T(8,128)}, bf16[16,512,1024]{2,1,0:T(8,128)(2,1)}) custom-call(f32[32,512,512]{2,1,0:T(8,128)} %get-tuple-element.22.z_hbm, bf16[1280,16384]{1,0:T(8,128)(2,1)} %w_hbm.7, f32[272,128]{1,0:T(8,128)} %get-tuple-element.24.p0.st0, f32[272,128]{1,0:T(8,128)} %copy-done.3, ...), custom_call_target="tpu_custom_call" | custom-call | flops 21474836480 | bytes 75497472 | tf_op jit(solution)/shard_map/pallas_call | solution.py:744
  126.1 1.2 collective-permute-start.5
  127.3 0.3 collective-permute-start.9
  127.6 0.4 collective-permute-start.7
  128.0 1.5 collective-permute-start.8
  129.5 0.7 collective-permute-done.5
  130.2 1.0 collective-permute-start.10
  131.2 1.5 add.11
  132.7 2.9 %collective-permute-done.10.meta_ref = s32[2,34]{1,0:T(2,128)S(1)} collective-permute-done((s32[2,34]{1,0:T(2,128)S(1)}, s32[2,34]{1,0:T(2,128)S(1)}, u32[]{:S(2)}, u32[]{:S(2)}) %collective-permute-start.10) | collective-permute-done | bytes 304 | tf_op jit(solution)/shard_map/ppermute | solution.py:663
  135.7 0.5 copy-done.11
  136.4 37.6 %shard_map.80 = f32[640,16384]{1,0:T(8,128)} custom-call(bf16[16,512,1024]{2,1,0:T(8,128)(2,1)} %get-tuple-element.36.g_hbm, f32[32,512,512]{2,1,0:T(8,128)} %get-tuple-element.37.z_hbm, bf16[512,1280]{1,0:T(8,128)(2,1)} %bitcast.9, bf16[512,1280]{1,0:T(8,128)(2,1)} %get-tuple-element.26.h_ref.h_oth_ref, f32[16,128]{1,0:T(8,128)} %get-tuple-element.38.st0, ...), custom_call_target="tpu_custom_call" | custom-call | flops 21474836480 | bytes 109051904 | tf_op jit(solution)/shard_map/pallas_call | solution.py:759
  174.2 1.2 slice_bitcast_fusion
  175.4 1.8 %collective-permute-done.12 = f32[256,1280]{1,0:T(8,128)S(1)} collective-permute-done((f32[256,1280]{1,0:T(8,128)S(1)}, f32[256,1280]{1,0:T(8,128)S(1)}, u32[]{:S(2)}, u32[]{:S(2)}) %collective-permute-start.12) | collective-permute-done | bytes 1310752 | tf_op jit(solution)/shard_map/ppermute | solution.py:660
  177.2 1.7 maximum_select_fusion
  (38 shorter events, 0.8 us)
Async XLA Ops:
  1.8 39.3 %collective-permute-start = (bf16[256,1280]{1,0:T(8,128)(2,1)S(1)}, bf16[256,1280]{1,0:T(8,128)(2,1)S(1)}, u32[]{:S(2)}, u32[]{:S(2)}) collective-permute-start(bf16[256,1280]{1,0:T(8,128)(2,1)S(1)} %dynamic-slice_bitcast_fusion), channel_id=1, source_target_pairs={{0,4},{4,0},{1,5},{5,1},{2,6},{6,2},{3,7},{7,3}} | collective-permute-start | bytes 1966088 | tf_op jit(solution)/shard_map/ppermute | solution.py:663
  41.1 2.1 %copy-start = (bf16[256,1280]{1,0:T(8,128)(2,1)}, bf16[256,1280]{1,0:T(8,128)(2,1)S(1)}, u32[]{:S(2)}) copy-start(bf16[256,1280]{1,0:T(8,128)(2,1)S(1)} %collective-permute-done.h_got) | copy-start | bytes 1966084
  41.1 2.1 %collective-permute-start.4 = (bf16[256,1280]{1,0:T(8,128)(2,1)S(1)}, bf16[256,1280]{1,0:T(8,128)(2,1)S(1)}, u32[]{:S(2)}, u32[]{:S(2)}) collective-permute-start(bf16[256,1280]{1,0:T(8,128)(2,1)S(1)} %collective-permute-done.h_got), channel_id=1, source_target_pairs={{0,1},{1,0},{2,3},{3,2},{4,5},{5,4},{6,7},{7,6}} | collective-permute-start | bytes 1966088 | tf_op jit(solution)/shard_map/ppermute | solution.py:660
  41.1 15.5 %collective-permute-start.1 = (f32[272,128]{1,0:T(8,128)}, f32[272,128]{1,0:T(8,128)S(1)}, u32[]{:S(2)}, u32[]{:S(2)}) collective-permute-start(f32[272,128]{1,0:T(8,128)} %get-tuple-element.24.p0.st0), channel_id=1, source_target_pairs={{0,1},{1,0},{2,3},{3,2},{4,5},{5,4},{6,7},{7,6}} | collective-permute-start | bytes 417800 | tf_op jit(solution)/shard_map/ppermute | solution.py:660
  41.6 15.0 %collective-permute-start.2 = (f32[272,128]{1,0:T(8,128)}, f32[272,128]{1,0:T(8,128)S(1)}, u32[]{:S(2)}, u32[]{:S(2)}) collective-permute-start(f32[272,128]{1,0:T(8,128)} %get-tuple-element.24.p0.st0), channel_id=1, source_target_pairs={{0,2},{1,3},{2,0},{3,1},{4,6},{5,7},{6,4},{7,5}} | collective-permute-start | bytes 417800 | tf_op jit(solution)/shard_map/ppermute | solution.py:660
  42.4 14.2 %collective-permute-start.3 = (f32[272,128]{1,0:T(8,128)}, f32[272,128]{1,0:T(8,128)S(1)}, u32[]{:S(2)}, u32[]{:S(2)}) collective-permute-start(f32[272,128]{1,0:T(8,128)} %get-tuple-element.24.p0.st0), channel_id=1, source_target_pairs={{0,3},{1,2},{2,1},{3,0},{4,7},{5,6},{6,5},{7,4}} | collective-permute-start | bytes 417800 | tf_op jit(solution)/shard_map/ppermute | solution.py:660
  43.2 0.9 copy-start.1
  56.6 0.7 copy-start.3
  56.6 0.7 copy-start.4
  56.6 0.7 copy-start.5
  91.9 35.4 %copy-start.12 = (f32[512,128]{1,0:T(8,128)S(1)}, f32[512,128]{1,0:T(8,128)}, u32[]{:S(2)}) copy-start(f32[512,128]{1,0:T(8,128)} %get-tuple-element.31.occ_ref) | copy-start | bytes 786436
  91.9 35.7 %copy-start.6 = (f32[16,128]{1,0:T(8,128)S(1)}, f32[16,128]{1,0:T(8,128)}, u32[]{:S(2)}) copy-start(f32[16,128]{1,0:T(8,128)} %get-tuple-element.38.st0) | copy-start | bytes 24580
  91.9 38.2 %copy-start.10 = (s32[2,34]{1,0:T(2,128)S(1)}, s32[2,34]{1,0:T(2,128)}, u32[]{:S(2)}) copy-start(s32[2,34]{1,0:T(2,128)} %get-tuple-element.29.meta_ref) | copy-start | bytes 820
  126.1 4.0 %collective-permute-start.5 = (f32[256,1280]{1,0:T(8,128)}, f32[256,1280]{1,0:T(8,128)S(1)}, u32[]{:S(2)}, u32[]{:S(2)}) collective-permute-start(f32[256,1280]{1,0:T(8,128)} %get-tuple-element.35), channel_id=1, source_target_pairs={{0,1},{1,0},{2,3},{3,2},{4,5},{5,4},{6,7},{7,6}} | collective-permute-start | bytes 3932168 | tf_op jit(solution)/shard_map/ppermute | solution.py:660
  127.3 8.4 %collective-permute-start.9 = (f32[512,128]{1,0:T(8,128)S(1)}, f32[512,128]{1,0:T(8,128)S(1)}, u32[]{:S(2)}, u32[]{:S(2)}) collective-permute-start(f32[512,128]{1,0:T(8,128)S(1)} %copy-done.12), channel_id=1, source_target_pairs={{0,4},{4,0},{1,5},{5,1},{2,6},{6,2},{3,7},{7,3}} | collective-permute-start | bytes 786440 | tf_op jit(solution)/shard_map/ppermute | solution.py:663
  127.6 8.0 %collective-permute-start.6 = (f32[16,128]{1,0:T(8,128)S(1)}, f32[16,128]{1,0:T(8,128)S(1)}, u32[]{:S(2)}, u32[]{:S(2)}) collective-permute-start(f32[16,128]{1,0:T(8,128)S(1)} %copy-done.6), channel_id=1, source_target_pairs={{0,1},{1,0},{2,3},{3,2},{4,5},{5,4},{6,7},{7,6}} | collective-permute-start | bytes 24584 | tf_op jit(solution)/shard_map/ppermute | solution.py:660
  127.6 8.0 %collective-permute-start.7 = (f32[16,128]{1,0:T(8,128)S(1)}, f32[16,128]{1,0:T(8,128)S(1)}, u32[]{:S(2)}, u32[]{:S(2)}) collective-permute-start(f32[16,128]{1,0:T(8,128)S(1)} %copy-done.6), channel_id=1, source_target_pairs={{0,2},{1,3},{2,0},{3,1},{4,6},{5,7},{6,4},{7,5}} | collective-permute-start | bytes 24584 | tf_op jit(solution)/shard_map/ppermute | solution.py:660
  128.0 7.6 %collective-permute-start.8 = (f32[16,128]{1,0:T(8,128)S(1)}, f32[16,128]{1,0:T(8,128)S(1)}, u32[]{:S(2)}, u32[]{:S(2)}) collective-permute-start(f32[16,128]{1,0:T(8,128)S(1)} %copy-done.6), channel_id=1, source_target_pairs={{0,3},{1,2},{2,1},{3,0},{4,7},{5,6},{6,5},{7,4}} | collective-permute-start | bytes 24584 | tf_op jit(solution)/shard_map/ppermute | solution.py:660
  130.2 5.4 %collective-permute-start.10 = (s32[2,34]{1,0:T(2,128)S(1)}, s32[2,34]{1,0:T(2,128)S(1)}, u32[]{:S(2)}, u32[]{:S(2)}) collective-permute-start(s32[2,34]{1,0:T(2,128)S(1)} %copy-done.10), channel_id=1, source_target_pairs={{0,4},{4,0},{1,5},{5,1},{2,6},{6,2},{3,7},{7,3}} | collective-permute-start | bytes 824 | tf_op jit(solution)/shard_map/ppermute | solution.py:663
  135.6 38.4 %collective-permute-start.11 = (f32[256,1280]{1,0:T(8,128)S(1)}, f32[256,1280]{1,0:T(8,128)S(1)}, u32[]{:S(2)}, u32[]{:S(2)}) collective-permute-start(f32[256,1280]{1,0:T(8,128)S(1)} %add.11), channel_id=1, source_target_pairs={{0,2},{1,3},{2,0},{3,1},{4,6},{5,7},{6,4},{7,5}} | collective-permute-start | bytes 3932168 | tf_op jit(solution)/shard_map/ppermute | solution.py:660
  135.6 0.6 copy-start.8
  135.7 0.6 copy-start.9
  135.7 0.7 copy-start.2
  174.2 3.1 %collective-permute-start.12 = (f32[256,1280]{1,0:T(8,128)S(1)}, f32[256,1280]{1,0:T(8,128)S(1)}, u32[]{:S(2)}, u32[]{:S(2)}) collective-permute-start(f32[256,1280]{1,0:T(8,128)S(1)} %add.12), channel_id=1, source_target_pairs={{0,1},{1,0},{2,3},{3,2},{4,5},{5,4},{6,7},{7,6}} | collective-permute-start | bytes 3932168 | tf_op jit(solution)/shard_map/ppermute | solution.py:660
  (2 other events, 1.2 us)
where the time goes:
time: 179 us
  Pallas kernels  155 us (87%)
  starting transfers between devices  9.69 us (5%)
  waiting for transfers between devices  5.64 us (3%)
  local copies, waits for them, and re-layouts  4.65 us (3%)
  other arithmetic  3.28 us (2%)
    pallas_call x1, Pallas kernels, local_body(): kernel_call(functools.partial(grad_w_kernel, n_slots), out_shape=jax.Shap...  37.6 us
    pallas_call x1, Pallas kernels, local_body(): kernel_call(functools.partial(z_own_kernel, n_slots), out_shape=(z_type,...  35.9 us
    pallas_call x1, Pallas kernels, local_body(): kernel_call(functools.partial(z_lattice_kernel, cut_a, n_tiles, n_lat, n_...  34.5 us
    pallas_call x1, Pallas kernels, local_body(): kernel_call(functools.partial(grad_h_kernel, n_slots), out_shape=(jax.Sha...  34.2 us
    pallas_call x1, Pallas kernels, local_body(): kernel_call(functools.partial(z_first_kernel, 0, cut_a), out_shape=(z_typ...  12.5 us
    ppermute x10, starting transfers between devices, tp_xor(): return lax.ppermute(x, 'tp', [(i, i ^ mask) for i in range(n_tp)])  4.97 us
    ppermute x3, starting transfers between devices, swap_dp(): return lax.ppermute(x, 'dp', dp_swap)  4.72 us
  transfers between devices with their start and end apart: 13, of which 4 were waited for; matrix products, arithmetic and copies ran while one was open for 1% of the time, Pallas kernels for 48%

commit v1 on v0

--- a/solution.py
+++ b/solution.py
@@ -163,11 +163,13 @@
             out_ref[at:at + 1, :] = flat[0:1, p * LANES:(p + 1) * LANES]
 
 
-def z_own_kernel(n_slots, h_ref, w_hbm, labels_ref, in_len_ref, lab_len_ref, z_hbm, pick_ref, meta_ref, wbuf, wsem, zbuf, zsem, m_ref, s_ref, head, nxt):
+def z_own_kernel(n_slots, h_hbm, w_hbm, labels_ref, in_len_ref, lab_len_ref, z_hbm, pick_ref, meta_ref, h_ref, hsem, wbuf, wsem, zbuf, zsem, m_ref, s_ref, head, nxt):
     n_tiles = z_hbm.shape[0]
     rows = h_ref.shape[0]
     n_seq = meta_ref.shape[0]
     frames = rows // n_seq
+    h_copy = pltpu.make_async_copy(h_hbm, h_ref, hsem.at[0])
+    h_copy.start()
     n_lab = n_slots - 1
     for q in range(n_seq):
         def put(k, c, q=q):
@@ -184,6 +186,7 @@
     m_ref[...] = jnp.full(m_ref.shape, NEG_BIG, F32)
     s_ref[...] = jnp.zeros(s_ref.shape, F32)
     pick_ref[...] = jnp.zeros(pick_ref.shape, F32)
+    h_copy.wait()
     lane = lax.broadcasted_iota(jnp.int32, (frames, LANES), 1)
 
     def out_copy(j):
@@ -222,7 +225,7 @@
         out_copy(j).wait()
 
 
-def z_oth_loop(lo, hi, h_ref, w_hbm, z_hbm, wbuf, wsem, zbuf, zsem, m_ref, s_ref, sections):
+def z_oth_loop(lo, hi, join, h_ref, w_hbm, z_hbm, wbuf, wsem, zbuf, zsem, m_ref, s_ref, sections):
     group = zbuf.shape[1]
     lo, n_groups = lo // group, (hi - lo) // group
     stream = TileStream(w_hbm, wbuf, wsem, wbuf.shape[0], n_groups, lambda src, j: w_view(src, lo + j, group))
@@ -233,6 +236,7 @@
         return pltpu.make_async_copy(zbuf.at[slot], z_view(z_hbm, lo + j, group), zsem.at[slot])
 
     base = 0
+    join.wait()
     for n, side, make_carry in sections:
         carry = make_carry()
 
@@ -256,24 +260,36 @@
         out_copy(j).wait()
 
 
-def join_rows(h_got, h_core, h_ref):
-    n = h_got.shape[0]
-    core = lax.rem(lax.axis_index("tp"), 2)
-    h_ref[pl.ds(pl.multiple_of(core * n, n), n), :] = h_got[...]
-    h_ref[pl.ds(pl.multiple_of((1 - core) * n, n), n), :] = h_core[...]
-
-
-def z_first_kernel(lo, hi, h_got, h_core, w_hbm, z_hbm, m_ref, s_ref, h_ref, wbuf, wsem, zbuf, zsem):
-    join_rows(h_got, h_core, h_ref)
+class JoinRows:
+    def __init__(self, h_got, h_core, h_ref, hsem):
+        n = h_got.shape[0]
+        core = lax.rem(lax.axis_index("tp"), 2)
+        self.copies = [pltpu.make_async_copy(src, h_ref.at[pl.ds(pl.multiple_of(at * n, n), n), :], hsem.at[k])
+                       for k, (src, at) in enumerate(((h_got, core), (h_core, 1 - core)))]
+
+    def start(self):
+        for c in self.copies:
+            c.start()
+
+    def wait(self):
+        for c in self.copies:
+            c.wait()
+
+
+def z_first_kernel(lo, hi, h_got, h_core, w_hbm, z_hbm, m_ref, s_ref, h_ref, hsem, wbuf, wsem, zbuf, zsem):
+    join = JoinRows(h_got, h_core, h_ref, hsem)
+    join.start()
     m_ref[...] = jnp.full(m_ref.shape, NEG_BIG, F32)
     s_ref[...] = jnp.zeros(s_ref.shape, F32)
-    for _ in z_oth_loop(lo, hi, h_ref, w_hbm, z_hbm, wbuf, wsem, zbuf, zsem, m_ref, s_ref, [((hi - lo) // zbuf.shape[1], lambda k, c: c, lambda: 0)]):
+    for _ in z_oth_loop(lo, hi, join, h_ref, w_hbm, z_hbm, wbuf, wsem, zbuf, zsem, m_ref, s_ref, [((hi - lo) // zbuf.shape[1], lambda k, c: c, lambda: 0)]):
         pass
 
 
-def z_lattice_kernel(lo, hi, n_lat, n_lab, h_ref, w_hbm, m_in, s_in, p0, p1, p2, p3, meta_ref, z_in,
+def z_lattice_part(lo, hi, n_lat, n_lab, before_tail, h_got, h_core, w_hbm, m_in, s_in, p0, p1, p2, p3, meta_ref,
                      z_hbm, stats_ref, occ_ref, loss_ref, m_ref, s_ref,
-                     wbuf, wsem, zbuf, zsem, e_lab, e_blk, a_lab, a_blk, b_lab, b_blk, o_t):
+                     h_ref, hsem, wbuf, wsem, zbuf, zsem, e_lab, e_blk, a_lab, a_blk, b_lab, b_blk, o_t):
+    join = JoinRows(h_got, h_core, h_ref, hsem)
+    join.start()
     n_blk = e_lab.shape[0]
     frames = n_blk * 64
     m_ref[...] = m_in[...]
@@ -327,13 +343,14 @@
         mid = jnp.minimum(hi_v, c)
         return top + jnp.log2(1.0 + (jnp.exp2(lo_v - top) + jnp.exp2(mid - top)))
 
-    def emission(t):
-        j, u = t // 64, lax.rem(t, 64)
-        idx32 = jnp.where(lane32 == 1, 64 + u, u)
-        idx8 = jnp.where(lane8 == 1, 64 + u, u)
-        el = jnp.take_along_axis(e_lab[j], idx32, axis=1)
-        eb = jnp.take_along_axis(e_blk[j], idx8, axis=1)
-        return el, eb
+    pick32 = jnp.where(lane32 == 1, 64, 0)
+    pick8 = jnp.where(lane8 == 1, 64, 0)
+
+    def lanes_of(x, idx):
+        return jnp.take_along_axis(x, idx, axis=1, mode="promise_in_bounds")
+
+    def emission(j, u):
+        return lanes_of(e_lab[j], pick32 + u), lanes_of(e_blk[j], pick8 + u)
 
     neg32 = jnp.full((n_lab, LANES), NEG_BIG, F32)
     neg8 = jnp.full((8, LANES), NEG_BIG, F32)
@@ -343,9 +360,9 @@
     skip_dn = skip_dn & (row32 > 0)
     skip_up = skip_up & (row32 < n_lab - 1)
 
-    def lat_step(i, carry):
+    def lat_step(i, j, u, carry):
         al, ab, at, bl, bb, bt = carry
-        el, eb = emission(i)
+        el, eb = emission(j, u)
         eb32 = jnp.broadcast_to(eb[0:1], (n_lab, LANES))
         rolled = pltpu.roll(al, 1, 0)
         prev = jnp.where(row32 == 0, NEG_BIG, rolled)
@@ -360,7 +377,7 @@
         ab = jnp.where(i < live32, eb32 + nb, ab)
         at = jnp.where(i < live8, eb + nt, at)
         t = frames - 1 - i
-        fl, fb = emission(t)
+        fl, fb = emission(n_blk - 1 - j, 63 - u)
         fb32 = jnp.broadcast_to(fb[0:1], (n_lab, LANES))
         last = row32 == n_lab - 1
         up_l = jnp.where(skip_up, pltpu.roll(bl, n_lab - 1, 0), NEG_BIG)
@@ -381,15 +398,17 @@
     per_tile = frames // n_lat_groups
 
     def lattice_side(k, carry):
+        i = k * per_tile
+        j = lax.div(i, 64)
         for u in range(per_tile):
-            carry = lat_step(k * per_tile + u, carry)
+            carry = lat_step(i + u, j, i - 64 * j + u, carry)
         return carry
 
     n_occ = (hi - lo - n_lat) // group
     occ_group = frames // n_occ // 64
     back32 = jnp.where(lane32 >= 64, 1, 0)
     back8 = jnp.where(lane8 >= 64, 1, 0)
-    run = z_oth_loop(lo, hi, h_ref, w_hbm, z_hbm, wbuf, wsem, zbuf, zsem, m_ref, s_ref,
+    run = z_oth_loop(lo, hi, join, h_ref, w_hbm, z_hbm, wbuf, wsem, zbuf, zsem, m_ref, s_ref,
                      [(n_lat_groups, lattice_side, lambda: (neg32, start32, neg8, neg32, fin_b, fin_t)),
                       (n_occ, lambda k, c: occ_side(k, c), lambda: 0)])
     al, ab, at, _, _, _ = next(run)
@@ -409,8 +428,8 @@
         occ_u = jnp.exp2(a_blk[i, n_lab:n_lab + 8] + b_blk[i, n_lab:n_lab + 8] + loss8)
         blank = jnp.sum(occ_b, axis=0, keepdims=True) + occ_u[0:1]
         blank = jnp.where(i < live8, jnp.broadcast_to(blank, (8, LANES)), 0.0)
-        acc_l = jnp.where(lax.rem(lane32, 64) == u, jnp.take_along_axis(occ_l, back32, axis=1), acc_l)
-        acc_b = jnp.where(lax.rem(lane8, 64) == u, jnp.take_along_axis(blank, back8, axis=1), acc_b)
+        acc_l = jnp.where(lax.rem(lane32, 64) == u, lanes_of(occ_l, back32), acc_l)
+        acc_b = jnp.where(lax.rem(lane8, 64) == u, lanes_of(blank, back8), acc_b)
         return acc_l, acc_b
 
     def occ_side(k, c):
@@ -425,6 +444,8 @@
             o_t[j, 8 + n_lab:LANES] = jnp.zeros((LANES - 8 - n_lab, LANES), F32)
         return c
 
+    next(run)
+    before_tail()
     for _ in run:
         pass
     emit_stats(m_ref, s_ref, stats_ref, 0)
@@ -489,7 +510,7 @@
     return exact_zero(total)
 
 
-def grad_h_kernel(n_slots, z_hbm, w_hbm, st0, st1, st2, st3, occ_ref, part_loss, meta_ref, keep_ref, send_ref, loss_ref, g_hbm,
+def grad_h_part(n_slots, z_hbm, w_hbm, st0, st1, st2, st3, occ_ref, part_loss, meta_ref, keep_ref, send_ref, loss_ref, g_hbm,
                   wbuf, wsem, zbuf, zsem, acc, lse_ref, g0, g1, gsem, head, nxt):
     n_tiles, rows = z_hbm.shape[0], z_hbm.shape[1]
     frames = rows // meta_ref.shape[0]
@@ -499,7 +520,7 @@
     stream = TileStream(w_hbm, wbuf, wsem, wbuf.shape[0], n_groups, lambda src, j: w_view(src, j, group))
     zs = TileStream(z_hbm, zbuf, zsem, zbuf.shape[0], n_groups, lambda src, j: z_view(src, j, group))
     zs.prime()
-    stream.prime()
+    yield stream.prime
     col_start = build_lists(meta_refs, n_tiles * TILE, head, nxt)
     sums = spread_lse([st0, st1, st2, st3], frames, meta_ref, lse_ref, 0, frames)
     lane1 = lax.broadcasted_iota(jnp.int32, (8, LANES), 1)
@@ -565,8 +586,22 @@
     send_ref[...] = acc[:, pl.ds(pl.multiple_of((1 - core) * n, n), n)].T
 
 
-def grad_w_kernel(n_slots, g_hbm, z_hbm, h_own_ref, h_oth_ref, st0, st1, st2, st3, occ_ref, meta_ref, gw_hbm,
-                  zbuf, zsem, gsem, obuf, osem, ht, lse_ref, g0, g1, head, nxt):
+def mid_kernel(lo, hi, n_lat, n_lab, h_got, h_core, w_hbm, m_in, s_in, p0, p1, p2, p3, z_own, meta_ref, z_in,
+               z_hbm, stats_ref, occ_ref, keep_ref, send_ref, loss_ref, g_hbm,
+               part_loss, m_ref, s_ref, h_ref, hsem, wbuf, wsem, zbuf, zsem, e_lab, e_blk, a_lab, a_blk, b_lab, b_blk, o_t,
+               zin_buf, zin_sem, acc, lse_ref, g0, g1, gsem, head, nxt):
+    second = grad_h_part(n_lab + 1, z_own, w_hbm, p0, p1, p2, p3, occ_ref, part_loss, meta_ref, keep_ref, send_ref, loss_ref, g_hbm,
+                         wbuf, wsem, zin_buf, zin_sem, acc, lse_ref, g0, g1, gsem, head, nxt)
+    prime_w = next(second)
+    z_lattice_part(lo, hi, n_lat, n_lab, prime_w, h_got, h_core, w_hbm, m_in, s_in, p0, p1, p2, p3, meta_ref,
+                   z_hbm, stats_ref, occ_ref, part_loss, m_ref, s_ref,
+                   h_ref, hsem, wbuf, wsem, zbuf, zsem, e_lab, e_blk, a_lab, a_blk, b_lab, b_blk, o_t)
+    for _ in second:
+        pass
+
+
+def grad_w_kernel(n_slots, g_hbm, z_hbm, h_own_ref, h_got, h_core, st0, st1, st2, st3, occ_ref, meta_ref, gw_hbm,
+                  h_ref, hsem, zbuf, zsem, gsem, obuf, osem, ht, lse_ref, g0, g1, head, nxt):
     n_tiles, rows = z_hbm.shape[0], z_hbm.shape[1]
     frames = rows // meta_ref.shape[0]
     d_loc = ht.shape[0]
@@ -577,13 +612,16 @@
     def g_copy(j, g, k):
         return pltpu.make_async_copy(g_hbm.at[j], g.at[0:rows, :], gsem.at[k])
 
+    join = JoinRows(h_got, h_core, h_ref, hsem)
+    join.start()
+    zs.prime()
     g_copy(0, g0, 0).start()
-    zs.prime()
     col_start = build_lists([meta_ref], n_tiles * TILE, head, nxt)
     d0 = pl.multiple_of(lax.axis_index("dp") * d_loc, LANES)
     ht[:, 0:rows] = h_own_ref[:, pl.ds(d0, d_loc)].T
-    ht[:, rows:2 * rows] = h_oth_ref[:, pl.ds(d0, d_loc)].T
     spread_lse([st0, st1, st2, st3], 0, meta_ref, lse_ref, 0, frames)
+    join.wait()
+    ht[:, rows:2 * rows] = h_ref[:, pl.ds(d0, d_loc)].T
     lane = lax.broadcasted_iota(jnp.int32, (frames, LANES), 1)
     n_units = 2 * group
 
@@ -658,6 +696,9 @@
 
     def tp_xor(x, mask):
         return lax.ppermute(x, "tp", [(i, i ^ mask) for i in range(n_tp)])
+
+    def in_hbm(x):
+        return pltpu.with_memory_space_constraint(x, pltpu.HBM)
 
     def swap_dp(x):
         return lax.ppermute(x, "dp", dp_swap)
@@ -686,6 +727,7 @@
         meta_type = jax.ShapeDtypeStruct((batch_loc, n_slots + 1), i32)
         g_type = jax.ShapeDtypeStruct((n_tiles // 2, rows, 2 * TILE), BF16)
         stat_type = jax.ShapeDtypeStruct((16, LANES), F32)
+        g_scratch = [pltpu.VMEM((rows, 2 * TILE), BF16)] * 2
 
         def w_scratch(n):
             return [pltpu.VMEM((3, model_dim, n * TILE), BF16), dma((3,))]
@@ -693,6 +735,7 @@
         def z_scratch(n):
             return [pltpu.VMEM((3, n, rows, TILE), F32), dma((3,))]
 
+        h_scratch = [pltpu.VMEM((rows, model_dim), BF16), dma((2,))]
         run_scratch = [pltpu.VMEM((rows, LANES), F32), pltpu.VMEM((rows, LANES), F32)]
 
         def lists(n_sets):
@@ -701,57 +744,49 @@
         z_own, pick, meta = kernel_call(
             functools.partial(z_own_kernel, n_slots),
             out_shape=(z_type, pick_type, meta_type),
-            in_specs=[vmem_spec(), any_spec(), smem_spec(), smem_spec(), smem_spec()],
+            in_specs=[any_spec(), any_spec(), smem_spec(), smem_spec(), smem_spec()],
             out_specs=(any_spec(), vmem_spec(), smem_spec()),
-            scratch_shapes=w_scratch(2) + z_scratch(2) + run_scratch + lists(1),
+            scratch_shapes=h_scratch + w_scratch(4) + z_scratch(4) + run_scratch + lists(1),
             compiler_params=params(),
             cost_estimate=cost(n_tiles * flops, n_tiles * (wbytes + zbytes)),
-        )(h_own, w_loc, labels, in_len, lab_len)
+        )(in_hbm(h_own), w_loc, labels, in_len, lab_len)
 
         h_got, pick = lax.optimization_barrier((h_got, pick))
-        h_core = tp_xor(h_got, 1)
+        h_core = in_hbm(tp_xor(h_got, 1))
+        h_got = in_hbm(h_got)
         picks = [pick] + [tp_xor(pick, k) for k in others]
 
-        z_part, run_m, run_s, h_oth = kernel_call(
+        z_part, run_m, run_s = kernel_call(
             functools.partial(z_first_kernel, 0, cut_a),
-            out_shape=(z_type, run_type, run_type, jax.ShapeDtypeStruct((rows, model_dim), BF16)),
-            in_specs=[vmem_spec(), vmem_spec(), any_spec()],
-            out_specs=(any_spec(), vmem_spec(), vmem_spec(), vmem_spec()),
-            scratch_shapes=w_scratch(2) + z_scratch(2),
+            out_shape=(z_type, run_type, run_type),
+            in_specs=[any_spec()] * 3,
+            out_specs=(any_spec(), vmem_spec(), vmem_spec()),
+            scratch_shapes=h_scratch + w_scratch(4) + z_scratch(4),
             compiler_params=params(),
             cost_estimate=cost(cut_a * flops, cut_a * (wbytes + zbytes)),
         )(h_got, h_core, w_loc)
 
         n_blk = frames // 64
-        z_oth, stats_oth, occ, part_loss = kernel_call(
-            functools.partial(z_lattice_kernel, cut_a, n_tiles, n_lat, n_lab),
-            out_shape=(z_type, stat_type, run_type, jax.ShapeDtypeStruct((8, LANES), F32)),
-            in_specs=[vmem_spec(), any_spec()] + [vmem_spec()] * 6 + [smem_spec(), any_spec()],
-            out_specs=(any_spec(),) + (vmem_spec(),) * 3,
-            input_output_aliases={9: 0},
-            scratch_shapes=run_scratch + w_scratch(2) + z_scratch(2) + [
+        half_type = jax.ShapeDtypeStruct((rows // 2, model_dim), F32)
+        loss_type = jax.ShapeDtypeStruct((8, LANES), F32)
+        z_oth, stats_oth, occ, keep, send, loss, g_own = kernel_call(
+            functools.partial(mid_kernel, cut_a, n_tiles, n_lat, n_lab),
+            out_shape=(z_type, stat_type, run_type, half_type, half_type, loss_type, g_type),
+            in_specs=[any_spec()] * 3 + [vmem_spec()] * 6 + [any_spec(), smem_spec(), any_spec()],
+            out_specs=(any_spec(),) + (vmem_spec(),) * 5 + (any_spec(),),
+            input_output_aliases={11: 0},
+            scratch_shapes=[pltpu.VMEM((8, LANES), F32)] + run_scratch + h_scratch + w_scratch(2) + z_scratch(2) + [
                 pltpu.VMEM((n_blk, n_lab, LANES), F32), pltpu.VMEM((n_blk, 8, LANES), F32),
                 pltpu.VMEM((frames, n_lab, LANES), F32), pltpu.VMEM((frames, n_lab + 8, LANES), F32),
                 pltpu.VMEM((frames, n_lab, LANES), F32), pltpu.VMEM((frames, n_lab + 8, LANES), F32),
-                pltpu.VMEM((n_blk, LANES, LANES), F32)],
+                pltpu.VMEM((n_blk, LANES, LANES), F32)] + z_scratch(2) + [
+                pltpu.VMEM((model_dim, rows), F32), pltpu.VMEM((rows, LANES), F32)] + g_scratch + [dma((2,))] + lists(1),
             compiler_params=params(),
-            cost_estimate=cost((n_tiles - cut_a) * flops, (n_tiles - cut_a) * (wbytes + zbytes)),
-        )(h_oth, w_loc, run_m, run_s, *picks, meta, z_part)
-
+            cost_estimate=cost((2 * n_tiles - cut_a) * flops, (2 * n_tiles - cut_a) * (wbytes + zbytes)),
+        )(h_got, h_core, w_loc, run_m, run_s, *picks, z_own, meta, z_part)
         st_oth = [stats_oth] + [tp_xor(stats_oth, k) for k in others]
         occ_oth = swap_dp(occ)
         meta_oth = swap_dp(meta)
-        keep, send, loss, g_own = kernel_call(
-            functools.partial(grad_h_kernel, n_slots),
-            out_shape=(jax.ShapeDtypeStruct((rows // 2, model_dim), F32), jax.ShapeDtypeStruct((rows // 2, model_dim), F32), jax.ShapeDtypeStruct((8, LANES), F32), g_type),
-            in_specs=[any_spec(), any_spec()] + [vmem_spec()] * 6 + [smem_spec()],
-            out_specs=(vmem_spec(),) * 3 + (any_spec(),),
-            scratch_shapes=w_scratch(2) + z_scratch(2) + [pltpu.VMEM((model_dim, rows), F32), pltpu.VMEM((rows, LANES), F32),
-                                                     pltpu.VMEM((rows, 2 * TILE), BF16), pltpu.VMEM((rows, 2 * TILE), BF16), dma((2,))] + lists(1),
-            compiler_params=params(),
-            cost_estimate=cost(n_tiles * flops, n_tiles * (wbytes + zbytes)),
-        )(z_own, w_loc, *picks, occ, part_loss, meta)
-
         recv = tp_xor(send, 1)
         chip_sum = keep + recv
         across = tp_xor(chip_sum, 2)
@@ -759,15 +794,15 @@
         grad_weight = kernel_call(
             functools.partial(grad_w_kernel, n_slots),
             out_shape=jax.ShapeDtypeStruct((d_loc, vocab_loc), F32),
-            in_specs=[any_spec(), any_spec()] + [vmem_spec()] * 7 + [smem_spec()],
+            in_specs=[any_spec(), any_spec(), vmem_spec(), any_spec(), any_spec()] + [vmem_spec()] * 5 + [smem_spec()],
             out_specs=any_spec(),
-            scratch_shapes=z_scratch(2) + [
+            scratch_shapes=h_scratch + z_scratch(2) + [
                 dma((2,)), pltpu.VMEM((3, d_loc, 2 * TILE), F32), dma((3,)),
                 pltpu.VMEM((d_loc, 2 * rows), BF16), pltpu.VMEM((rows, LANES), F32),
                 pltpu.VMEM((2 * rows, 2 * TILE), BF16), pltpu.VMEM((2 * rows, 2 * TILE), BF16)] + lists(1),
             compiler_params=params(),
             cost_estimate=cost(n_tiles * flops, n_tiles * (2 * zbytes + d_loc * TILE * 4)),
-        )(g_own, z_oth, h_own, h_oth, *st_oth, occ_oth, meta_oth)
+        )(g_own, z_oth, h_own, h_got, h_core, *st_oth, occ_oth, meta_oth)
 
         chip_sum, grad_weight = lax.optimization_barrier((chip_sum, grad_weight))
         full_half = chip_sum + across

time: 179 us -> 180 us (level)
    pallas_call x2 -> x1, Pallas kernels: 68.7 us -> 71.1 us  [local_body(): kernel_call(functools.partial(mid_kernel, cut_a, n_tiles, n_lat, n_lab),...]
    pallas_call x1, Pallas kernels: 35.9 us -> 33.6 us  [local_body(): kernel_call(functools.partial(z_own_kernel, n_slots), out_shape=(z_type,...]
  transfers between devices with their start and end apart: 13 -> 13, of which waited for: 4 -> 4; matrix products, arithmetic and copies ran while one was open for 1% -> 1% of each run, Pallas kernels for 48% -> 47%
where the time goes in v1:
time: 180 us
  Pallas kernels  156 us (87%)
  starting transfers between devices  9.56 us (5%)
  waiting for transfers between devices  5.68 us (3%)
  local copies, waits for them, and re-layouts  4.6 us (3%)
  other arithmetic  3.28 us (2%)
    pallas_call x1, Pallas kernels, local_body(): kernel_call(functools.partial(mid_kernel, cut_a, n_tiles, n_lat, n_lab),...  71.1 us
    pallas_call x1, Pallas kernels, local_body(): kernel_call(functools.partial(grad_w_kernel, n_slots), out_shape=jax.Shap...  37.6 us
    pallas_call x1, Pallas kernels, local_body(): kernel_call(functools.partial(z_own_kernel, n_slots), out_shape=(z_type,...  33.6 us
    pallas_call x1, Pallas kernels, local_body(): kernel_call(functools.partial(z_first_kernel, 0, cut_a), out_shape=(z_typ...  13.4 us
    ppermute x3, starting transfers between devices, swap_dp(): return lax.ppermute(x, 'dp', dp_swap)  4.89 us
    ppermute x10, starting transfers between devices, tp_xor(): return lax.ppermute(x, 'tp', [(i, i ^ mask) for i in range(n_tp)])  4.68 us
  transfers between devices with their start and end apart: 13, of which 4 were waited for; matrix products, arithmetic and copies ran while one was open for 1% of the time, Pallas kernels for 47%

profile of v1, /device:TPU:0, one launch (start us, length us, event | category | flops | bytes accessed | tf_op | source)
XLA Modules:
  0.0 179.7 jit_solution(3499950764981865832)
XLA Ops:
  0.6 1.1 dynamic-slice_bitcast_fusion
  1.8 3.4 %collective-permute-start = (bf16[256,1280]{1,0:T(8,128)(2,1)S(1)}, bf16[256,1280]{1,0:T(8,128)(2,1)S(1)}, u32[]{:S(2)}, u32[]{:S(2)}) collective-permute-start(bf16[256,1280]{1,0:T(8,128)(2,1)S(1)} %dynamic-slice_bitcast_fusion), channel_id=1, source_target_pairs={{0,4},{4,0},{1,5},{5,1},{2,6},{6,2},{3,7},{7,3}} | collective-permute-start | bytes 1966088 | tf_op jit(solution)/shard_map/ppermute | solution.py:704
  5.1 33.6 %shard_map.76 = (f32[32,512,512]{2,1,0:T(8,128)}, f32[272,128]{1,0:T(8,128)}, s32[2,34]{1,0:T(2,128)}) custom-call(bf16[512,1280]{1,0:T(8,128)(2,1)} %bitcast.8, bf16[1280,16384]{1,0:T(8,128)(2,1)} %w_hbm.5, s32[2,32]{1,0:T(2,128)} %labels_ref.1, s32[2]{0:T(128)} %in_len_ref.1, s32[2]{0:T(128)} %lab_len_ref.1), custom_call_target="tpu_custom_call" | custom-call | flops 21474836480 | bytes 75497472 | tf_op jit(solution)/shard_map/pallas_call | solution.py:744
  38.8 0.5 collective-permute-start.2
  39.3 0.9 collective-permute-start.3
  40.2 0.5 collective-permute-start.4
  40.7 0.2 collective-permute-done.1.h_core
  40.9 0.8 copy-done.1
  41.7 13.4 %shard_map.77 = (f32[32,512,512]{2,1,0:T(8,128)}, f32[512,128]{1,0:T(8,128)}, f32[512,128]{1,0:T(8,128)}) custom-call(bf16[256,1280]{1,0:T(8,128)(2,1)} %copy-done, bf16[256,1280]{1,0:T(8,128)(2,1)} %copy-done.1, bf16[1280,16384]{1,0:T(8,128)(2,1)} %w_hbm.5), custom_call_target="tpu_custom_call" | custom-call | flops 5368709120 | bytes 18874368 | tf_op jit(solution)/shard_map/pallas_call | solution.py:759
  55.2 0.6 copy-done.7
  55.9 71.1 %shard_map.78 = (f32[32,512,512]{2,1,0:T(8,128)}, f32[16,128]{1,0:T(8,128)}, f32[512,128]{1,0:T(8,128)}, f32[256,1280]{1,0:T(8,128)}, f32[256,1280]{1,0:T(8,128)...) custom-call(bf16[256,1280]{1,0:T(8,128)(2,1)} %copy-done, ...), custom_call_target="tpu_custom_call", output_to_operand_aliasing={{0}: (11, {})} | custom-call | flops 37580963840 | bytes 132120576 | tf_op jit(solution)/shard_map/pallas_call | solution.py:772
  127.1 0.7 collective-permute-start.5
  127.8 0.5 collective-permute-start.9
  128.3 1.9 %collective-permute-start.8 = (f32[16,128]{1,0:T(8,128)}, f32[16,128]{1,0:T(8,128)S(1)}, u32[]{:S(2)}, u32[]{:S(2)}) collective-permute-start(f32[16,128]{1,0:T(8,128)} %get-tuple-element.33.st0), channel_id=1, source_target_pairs={{0,3},{1,2},{2,1},{3,0},{4,7},{5,6},{6,5},{7,4}} | collective-permute-start | bytes 24584 | tf_op jit(solution)/shard_map/ppermute | solution.py:698
  130.2 0.5 collective-permute-done.5
  130.7 1.0 collective-permute-start.10
  131.7 1.5 add.11
  133.2 3.1 %collective-permute-done.10.meta_ref = s32[2,34]{1,0:T(2,128)S(1)} collective-permute-done((s32[2,34]{1,0:T(2,128)S(1)}, s32[2,34]{1,0:T(2,128)S(1)}, u32[]{:S(2)}, u32[]{:S(2)}) %collective-permute-start.10) | collective-permute-done | bytes 304 | tf_op jit(solution)/shard_map/ppermute | solution.py:704
  136.5 0.3 copy-done.6
  136.8 0.3 copy-done.3
  137.2 37.6 %shard_map.79 = f32[640,16384]{1,0:T(8,128)} custom-call(bf16[16,512,1024]{2,1,0:T(8,128)(2,1)} %get-tuple-element.31.g_hbm, f32[32,512,512]{2,1,0:T(8,128)} %get-tuple-element.32.z_hbm, bf16[512,1280]{1,0:T(8,128)(2,1)} %bitcast.9, bf16[256,1280]{1,0:T(8,128)(2,1)} %copy-done, bf16[256,1280]{1,0:T(8,128)(2,1)} %copy-done.1, ...), custom_call_target="tpu_custom_call" | custom-call | flops 21474836480 | bytes 109051904 | tf_op jit(solution)/shard_map/pallas_call | solution.py:794
  175.0 1.2 slice_bitcast_fusion
  176.2 1.8 %collective-permute-done.12 = f32[256,1280]{1,0:T(8,128)S(1)} collective-permute-done((f32[256,1280]{1,0:T(8,128)S(1)}, f32[256,1280]{1,0:T(8,128)S(1)}, u32[]{:S(2)}, u32[]{:S(2)}) %collective-permute-start.12) | collective-permute-done | bytes 1310752 | tf_op jit(solution)/shard_map/ppermute | solution.py:698
  178.0 1.7 maximum_select_fusion
  (33 shorter events, 0.7 us)
Async XLA Ops:
  1.8 37.0 %collective-permute-start = (bf16[256,1280]{1,0:T(8,128)(2,1)S(1)}, bf16[256,1280]{1,0:T(8,128)(2,1)S(1)}, u32[]{:S(2)}, u32[]{:S(2)}) collective-permute-start(bf16[256,1280]{1,0:T(8,128)(2,1)S(1)} %dynamic-slice_bitcast_fusion), channel_id=1, source_target_pairs={{0,4},{4,0},{1,5},{5,1},{2,6},{6,2},{3,7},{7,3}} | collective-permute-start | bytes 1966088 | tf_op jit(solution)/shard_map/ppermute | solution.py:704
  38.7 2.1 %copy-start = (bf16[256,1280]{1,0:T(8,128)(2,1)}, bf16[256,1280]{1,0:T(8,128)(2,1)S(1)}, u32[]{:S(2)}) copy-start(bf16[256,1280]{1,0:T(8,128)(2,1)S(1)} %collective-permute-done.h_got) | copy-start | bytes 1966084
  38.8 2.1 %collective-permute-start.1 = (bf16[256,1280]{1,0:T(8,128)(2,1)S(1)}, bf16[256,1280]{1,0:T(8,128)(2,1)S(1)}, u32[]{:S(2)}, u32[]{:S(2)}) collective-permute-start(bf16[256,1280]{1,0:T(8,128)(2,1)S(1)} %collective-permute-done.h_got), channel_id=1, source_target_pairs={{0,1},{1,0},{2,3},{3,2},{4,5},{5,4},{6,7},{7,6}} | collective-permute-start | bytes 1966088 | tf_op jit(solution)/shard_map/ppermute | solution.py:698
  38.8 16.4 %collective-permute-start.2 = (f32[272,128]{1,0:T(8,128)}, f32[272,128]{1,0:T(8,128)S(1)}, u32[]{:S(2)}, u32[]{:S(2)}) collective-permute-start(f32[272,128]{1,0:T(8,128)} %get-tuple-element.24.p0), channel_id=1, source_target_pairs={{0,1},{1,0},{2,3},{3,2},{4,5},{5,4},{6,7},{7,6}} | collective-permute-start | bytes 417800 | tf_op jit(solution)/shard_map/ppermute | solution.py:698
  39.3 15.9 %collective-permute-start.3 = (f32[272,128]{1,0:T(8,128)}, f32[272,128]{1,0:T(8,128)S(1)}, u32[]{:S(2)}, u32[]{:S(2)}) collective-permute-start(f32[272,128]{1,0:T(8,128)} %get-tuple-element.24.p0), channel_id=1, source_target_pairs={{0,2},{1,3},{2,0},{3,1},{4,6},{5,7},{6,4},{7,5}} | collective-permute-start | bytes 417800 | tf_op jit(solution)/shard_map/ppermute | solution.py:698
  40.2 15.0 %collective-permute-start.4 = (f32[272,128]{1,0:T(8,128)}, f32[272,128]{1,0:T(8,128)S(1)}, u32[]{:S(2)}, u32[]{:S(2)}) collective-permute-start(f32[272,128]{1,0:T(8,128)} %get-tuple-element.24.p0), channel_id=1, source_target_pairs={{0,3},{1,2},{2,1},{3,0},{4,7},{5,6},{6,5},{7,4}} | collective-permute-start | bytes 417800 | tf_op jit(solution)/shard_map/ppermute | solution.py:698
  40.9 0.8 copy-start.1
  55.2 0.7 copy-start.7
  55.2 0.7 copy-start.8
  55.2 0.7 copy-start.9
  55.9 74.7 %copy-start.10 = (s32[2,34]{1,0:T(2,128)S(1)}, s32[2,34]{1,0:T(2,128)}, u32[]{:S(2)}) copy-start(s32[2,34]{1,0:T(2,128)} %get-tuple-element.26.meta_ref) | copy-start | bytes 820
  127.1 3.6 %collective-permute-start.5 = (f32[256,1280]{1,0:T(8,128)}, f32[256,1280]{1,0:T(8,128)S(1)}, u32[]{:S(2)}, u32[]{:S(2)}) collective-permute-start(f32[256,1280]{1,0:T(8,128)} %get-tuple-element.30), channel_id=1, source_target_pairs={{0,1},{1,0},{2,3},{3,2},{4,5},{5,4},{6,7},{7,6}} | collective-permute-start | bytes 3932168 | tf_op jit(solution)/shard_map/ppermute | solution.py:698
  127.8 8.7 %collective-permute-start.9 = (f32[512,128]{1,0:T(8,128)}, f32[512,128]{1,0:T(8,128)S(1)}, u32[]{:S(2)}, u32[]{:S(2)}) collective-permute-start(f32[512,128]{1,0:T(8,128)} %get-tuple-element.34), channel_id=1, source_target_pairs={{0,4},{4,0},{1,5},{5,1},{2,6},{6,2},{3,7},{7,3}} | collective-permute-start | bytes 786440 | tf_op jit(solution)/shard_map/ppermute | solution.py:704
  128.3 8.2 %collective-permute-start.6 = (f32[16,128]{1,0:T(8,128)}, f32[16,128]{1,0:T(8,128)S(1)}, u32[]{:S(2)}, u32[]{:S(2)}) collective-permute-start(f32[16,128]{1,0:T(8,128)} %get-tuple-element.33.st0), channel_id=1, source_target_pairs={{0,1},{1,0},{2,3},{3,2},{4,5},{5,4},{6,7},{7,6}} | collective-permute-start | bytes 24584 | tf_op jit(solution)/shard_map/ppermute | solution.py:698
  128.3 8.2 %collective-permute-start.7 = (f32[16,128]{1,0:T(8,128)}, f32[16,128]{1,0:T(8,128)S(1)}, u32[]{:S(2)}, u32[]{:S(2)}) collective-permute-start(f32[16,128]{1,0:T(8,128)} %get-tuple-element.33.st0), channel_id=1, source_target_pairs={{0,2},{1,3},{2,0},{3,1},{4,6},{5,7},{6,4},{7,5}} | collective-permute-start | bytes 24584 | tf_op jit(solution)/shard_map/ppermute | solution.py:698
  128.3 8.2 %collective-permute-start.8 = (f32[16,128]{1,0:T(8,128)}, f32[16,128]{1,0:T(8,128)S(1)}, u32[]{:S(2)}, u32[]{:S(2)}) collective-permute-start(f32[16,128]{1,0:T(8,128)} %get-tuple-element.33.st0), channel_id=1, source_target_pairs={{0,3},{1,2},{2,1},{3,0},{4,7},{5,6},{6,5},{7,4}} | collective-permute-start | bytes 24584 | tf_op jit(solution)/shard_map/ppermute | solution.py:698
  130.7 5.6 %collective-permute-start.10 = (s32[2,34]{1,0:T(2,128)S(1)}, s32[2,34]{1,0:T(2,128)S(1)}, u32[]{:S(2)}, u32[]{:S(2)}) collective-permute-start(s32[2,34]{1,0:T(2,128)S(1)} %copy-done.10), channel_id=1, source_target_pairs={{0,4},{4,0},{1,5},{5,1},{2,6},{6,2},{3,7},{7,3}} | collective-permute-start | bytes 824 | tf_op jit(solution)/shard_map/ppermute | solution.py:704
  136.3 0.5 copy-start.6
  136.3 38.5 %collective-permute-start.11 = (f32[256,1280]{1,0:T(8,128)S(1)}, f32[256,1280]{1,0:T(8,128)S(1)}, u32[]{:S(2)}, u32[]{:S(2)}) collective-permute-start(f32[256,1280]{1,0:T(8,128)S(1)} %add.11), channel_id=1, source_target_pairs={{0,2},{1,3},{2,0},{3,1},{4,6},{5,7},{6,4},{7,5}} | collective-permute-start | bytes 3932168 | tf_op jit(solution)/shard_map/ppermute | solution.py:698
  136.5 0.6 copy-start.3
  136.5 0.6 copy-start.4
  136.5 0.6 copy-start.5
  136.5 0.7 copy-start.2
  175.0 3.1 %collective-permute-start.12 = (f32[256,1280]{1,0:T(8,128)S(1)}, f32[256,1280]{1,0:T(8,128)S(1)}, u32[]{:S(2)}, u32[]{:S(2)}) collective-permute-start(f32[256,1280]{1,0:T(8,128)S(1)} %add.12), channel_id=1, source_target_pairs={{0,1},{1,0},{2,3},{3,2},{4,5},{5,4},{6,7},{7,6}} | collective-permute-start | bytes 3932168 | tf_op jit(solution)/shard_map/ppermute | solution.py:698

commit v2 on v1

--- a/solution.py
+++ b/solution.py
@@ -10,9 +10,12 @@
 NEG_BIG = -1.0e30
 LOG2E = 1.4426950408889634
 F32 = jnp.float32
+DOWN = dict(axis=0, keepdims=True)
+ALONG = dict(axis=1, keepdims=True)
 BF16 = jnp.bfloat16
 TILE = 512
 LANES = 128
+HALF = LANES // 2
 MIB = 1 << 20
 
 
@@ -153,8 +156,8 @@
 
 
 def emit_stats(m_ref, s_ref, out_ref, base):
-    row_m = jnp.max(m_ref[...], axis=1, keepdims=True)
-    row_s = jnp.sum(s_ref[...] * jnp.exp(m_ref[...] - row_m), axis=1, keepdims=True)
+    row_m = jnp.max(m_ref[...], **ALONG)
+    row_s = jnp.sum(s_ref[...] * jnp.exp(m_ref[...] - row_m), **ALONG)
     rows = m_ref.shape[0]
     for k, v in enumerate((row_m, row_s)):
         flat = jnp.broadcast_to(v, (rows, LANES)).T
@@ -163,7 +166,7 @@
             out_ref[at:at + 1, :] = flat[0:1, p * LANES:(p + 1) * LANES]
 
 
-def z_own_kernel(n_slots, h_hbm, w_hbm, labels_ref, in_len_ref, lab_len_ref, z_hbm, pick_ref, meta_ref, h_ref, hsem, wbuf, wsem, zbuf, zsem, m_ref, s_ref, head, nxt):
+def z_own_kernel(n_slots, h_hbm, w_hbm, labels_ref, in_len_ref, lab_len_ref, z_hbm, pick_ref, meta_ref, h_ref, hsem, wbuf, wsem, zbuf, zsem, m_ref, s_ref, blank, head, nxt):
     n_tiles = z_hbm.shape[0]
     rows = h_ref.shape[0]
     n_seq = meta_ref.shape[0]
@@ -186,8 +189,10 @@
     m_ref[...] = jnp.full(m_ref.shape, NEG_BIG, F32)
     s_ref[...] = jnp.zeros(s_ref.shape, F32)
     pick_ref[...] = jnp.zeros(pick_ref.shape, F32)
+    blank[...] = jnp.zeros(blank.shape, F32)
+    half = frames // 2
     h_copy.wait()
-    lane = lax.broadcasted_iota(jnp.int32, (frames, LANES), 1)
+    lane = lax.broadcasted_iota(jnp.int32, (half, LANES), 1)
 
     def out_copy(j):
         slot = lax.rem(j, zbuf.shape[0])
@@ -210,17 +215,32 @@
                 off = label_col([meta_ref], i) - col_start - (j * group + t) * TILE
                 blk = off // LANES
                 r0 = pl.multiple_of(seq * frames, frames)
-                zb = zbuf[zslot, t, pl.ds(r0, frames), pl.ds(pl.multiple_of(blk * LANES, LANES), LANES)]
-                at = item + 64 * seq
-                moved = pltpu.roll(zb, lax.rem(at - (off - blk * LANES) + 2 * LANES, LANES), 1)
-                pick_ref[0:frames, :] = jnp.where(lane == at, moved, pick_ref[0:frames, :])
+                src = off - blk * LANES
+                c0 = pl.multiple_of(blk * LANES, LANES)
+
+                def moved(p, at):
+                    zb = zbuf[zslot, t, pl.ds(r0 + p * half, half), pl.ds(c0, LANES)]
+                    return pltpu.roll(zb, lax.rem(at - src + LANES, LANES), 1)
+
+                @pl.when(item > 0)
+                def _():
+                    for p in range(2):
+                        at = item - 1 + n_lab * seq + HALF * p
+                        pick_ref[0:half, :] = jnp.where(lane == at, moved(p, at), pick_ref[0:half, :])
+
+                @pl.when(item == 0)
+                def _():
+                    for p in range(2):
+                        at = 2 * seq + p
+                        blank[...] = jnp.where(lane == at, moved(p, at), blank[...])
 
             walk_list(head, nxt, j * group + t, visit)
         return c
 
     n_groups = n_tiles // group
     lax.fori_loop(0, n_groups, step, 0)
-    emit_stats(m_ref, s_ref, pick_ref, frames)
+    emit_stats(m_ref, s_ref, pick_ref, half)
+    pick_ref[half + 16:half + 24, :] = blank[...].T[0:8]
     for j in range(n_groups - 3, n_groups):
         out_copy(j).wait()
 
@@ -276,24 +296,15 @@
             c.wait()
 
 
-def z_first_kernel(lo, hi, h_got, h_core, w_hbm, z_hbm, m_ref, s_ref, h_ref, hsem, wbuf, wsem, zbuf, zsem):
-    join = JoinRows(h_got, h_core, h_ref, hsem)
-    join.start()
-    m_ref[...] = jnp.full(m_ref.shape, NEG_BIG, F32)
-    s_ref[...] = jnp.zeros(s_ref.shape, F32)
-    for _ in z_oth_loop(lo, hi, join, h_ref, w_hbm, z_hbm, wbuf, wsem, zbuf, zsem, m_ref, s_ref, [((hi - lo) // zbuf.shape[1], lambda k, c: c, lambda: 0)]):
-        pass
-
-
-def z_lattice_part(lo, hi, n_lat, n_lab, before_tail, h_got, h_core, w_hbm, m_in, s_in, p0, p1, p2, p3, meta_ref,
+def z_lattice_part(lo, hi, n_lat, per_group, n_lab, before_tail, h_got, h_core, w_hbm, p0, p1, p2, p3, meta_ref,
                      z_hbm, stats_ref, occ_ref, loss_ref, m_ref, s_ref,
                      h_ref, hsem, wbuf, wsem, zbuf, zsem, e_lab, e_blk, a_lab, a_blk, b_lab, b_blk, o_t):
     join = JoinRows(h_got, h_core, h_ref, hsem)
     join.start()
     n_blk = e_lab.shape[0]
-    frames = n_blk * 64
-    m_ref[...] = m_in[...]
-    s_ref[...] = s_in[...]
+    frames = n_blk * HALF
+    m_ref[...] = jnp.full(m_ref.shape, NEG_BIG, F32)
+    s_ref[...] = jnp.zeros(s_ref.shape, F32)
     lane128 = lax.broadcasted_iota(jnp.int32, (LANES, LANES), 1)
     row32 = lax.broadcasted_iota(jnp.int32, (n_lab, LANES), 0)
     row8 = lax.broadcasted_iota(jnp.int32, (8, LANES), 0)
@@ -318,19 +329,23 @@
     end_blk = row32 == used32
     end_top = (row8 == 0) & (used8 == n_lab)
     shift0 = jnp.zeros((1, LANES), F32)
-    seq1 = lane8[0:1] >= 64
+    seq1 = lane8[0:1] >= HALF
     half_len = jnp.where(seq1, meta_ref[1, n_lab], meta_ref[0, n_lab])
+    half = frames // 2
+    packed = functools.reduce(jnp.add, [p[0:half, :] for p in (p0, p1, p2, p3)])
+    blanks = functools.reduce(jnp.add, [p[half + 16:half + 24, :] for p in (p0, p1, p2, p3)])
     for j in range(n_blk):
-        part = functools.reduce(jnp.add, [p[pl.ds(64 * j, 64), :] for p in (p0, p1, p2, p3)])
-        blk = jnp.concatenate([part, pltpu.roll(part, 64, 1)], axis=0)
-        blk = jnp.where(lane128 <= n_lab, blk, NEG_BIG)
-        x = blk.T
-        top = jnp.max(x[0:n_lab + 8], axis=0, keepdims=True)
-        e_blk[j] = jnp.broadcast_to((x[0:1] - top) * LOG2E, (8, LANES))
-        e_lab[j] = (pltpu.roll(x, LANES - 1, 0)[0:n_lab] - top) * LOG2E
-        shift0 = shift0 + jnp.where(lax.rem(lane8[0:1], 64) + 64 * j < half_len, top, 0.0)
-    shift_seq0 = jnp.sum(jnp.where(seq1, 0.0, shift0), axis=1, keepdims=True)
-    shift_seq1 = jnp.sum(jnp.where(seq1, shift0, 0.0), axis=1, keepdims=True)
+        far, near = j // 2, HALF * (j % 2)
+        part = packed[near:near + HALF]
+        x = jnp.concatenate([pltpu.roll(part, (LANES - HALF * far - n_lab * q) % LANES, 1) for q in range(2)], axis=0).T[0:n_lab]
+        rows_b = [pltpu.roll(blanks, (HALF * q - near) % LANES, 1)[2 * q + far:2 * q + far + 1] for q in range(2)]
+        x_blank = jnp.where(seq1, rows_b[1], rows_b[0])
+        top = jnp.maximum(jnp.max(x, **DOWN), x_blank)
+        e_blk[j] = jnp.broadcast_to((x_blank - top) * LOG2E, (8, LANES))
+        e_lab[j] = (x - top) * LOG2E
+        shift0 = shift0 + jnp.where(lax.rem(lane8[0:1], HALF) + HALF * j < half_len, top, 0.0)
+    shift_seq0 = jnp.sum(jnp.where(seq1, 0.0, shift0), **ALONG)
+    shift_seq1 = jnp.sum(jnp.where(seq1, shift0, 0.0), **ALONG)
 
     def lse2(a, b):
         hi_v = jnp.maximum(a, b)
@@ -343,8 +358,8 @@
         mid = jnp.minimum(hi_v, c)
         return top + jnp.log2(1.0 + (jnp.exp2(lo_v - top) + jnp.exp2(mid - top)))
 
-    pick32 = jnp.where(lane32 == 1, 64, 0)
-    pick8 = jnp.where(lane8 == 1, 64, 0)
+    pick32 = jnp.where(lane32 == 1, HALF, 0)
+    pick8 = jnp.where(lane8 == 1, HALF, 0)
 
     def lanes_of(x, idx):
         return jnp.take_along_axis(x, idx, axis=1, mode="promise_in_bounds")
@@ -388,34 +403,34 @@
         bl = jnp.where(t < live32, ml, bl)
         bb = jnp.where(t < live32, mb, bb)
         bt = jnp.where(t < live8, mt, bt)
-        b_lab[t] = bl
-        b_blk[t, 0:n_lab] = bb
-        b_blk[t, n_lab:n_lab + 8] = bt
+        b_lab[t + pad] = bl
+        b_blk[t + pad, 0:n_lab] = bb
+        b_blk[t + pad, n_lab:n_lab + 8] = bt
         return al, ab, at, bl, bb, bt
 
     group = zbuf.shape[1]
     n_lat_groups = n_lat // group
-    per_tile = frames // n_lat_groups
+    pad = b_lab.shape[0] - frames
 
     def lattice_side(k, carry):
-        i = k * per_tile
-        j = lax.div(i, 64)
-        for u in range(per_tile):
-            carry = lat_step(i + u, j, i - 64 * j + u, carry)
+        for u in range(per_group):
+            i = k * per_group + u
+            j = lax.min(lax.div(i, HALF), n_blk - 1)
+            carry = lat_step(i, j, lax.rem(i, HALF), carry)
         return carry
 
     n_occ = (hi - lo - n_lat) // group
-    occ_group = frames // n_occ // 64
-    back32 = jnp.where(lane32 >= 64, 1, 0)
-    back8 = jnp.where(lane8 >= 64, 1, 0)
+    occ_group = frames // n_occ // HALF
+    back32 = jnp.where(lane32 >= HALF, 1, 0)
+    back8 = jnp.where(lane8 >= HALF, 1, 0)
     run = z_oth_loop(lo, hi, join, h_ref, w_hbm, z_hbm, wbuf, wsem, zbuf, zsem, m_ref, s_ref,
                      [(n_lat_groups, lattice_side, lambda: (neg32, start32, neg8, neg32, fin_b, fin_t)),
                       (n_occ, lambda k, c: occ_side(k, c), lambda: 0)])
     al, ab, at, _, _, _ = next(run)
 
     lasts = [jnp.where(end, v, NEG_BIG) for end, v in ((end_lab, al), (end_blk, ab), (end_top, at))]
-    top = functools.reduce(jnp.maximum, [jnp.max(v, axis=0, keepdims=True) for v in lasts])
-    total = functools.reduce(jnp.add, [jnp.sum(jnp.exp2(v - top), axis=0, keepdims=True) for v in lasts])
+    top = functools.reduce(jnp.maximum, [jnp.max(v, **DOWN) for v in lasts])
+    total = functools.reduce(jnp.add, [jnp.sum(jnp.exp2(v - top), **DOWN) for v in lasts])
     loss = -(top + jnp.log2(total))
     loss32 = jnp.broadcast_to(loss, (n_lab, LANES))
     loss8 = jnp.broadcast_to(loss, (8, LANES))
@@ -423,13 +438,13 @@
     loss_ref[...] = jnp.broadcast_to(loss * (1.0 / LOG2E) - jnp.where(lane1 == 0, shift_seq0, jnp.where(lane1 == 1, shift_seq1, 0.0)), (8, LANES))
 
     def occ_frame(i, u, acc_l, acc_b):
-        occ_l = jnp.where(i < live32, jnp.exp2(a_lab[i] + b_lab[i] + loss32), 0.0)
-        occ_b = jnp.exp2(a_blk[i, 0:n_lab] + b_blk[i, 0:n_lab] + loss32)
-        occ_u = jnp.exp2(a_blk[i, n_lab:n_lab + 8] + b_blk[i, n_lab:n_lab + 8] + loss8)
-        blank = jnp.sum(occ_b, axis=0, keepdims=True) + occ_u[0:1]
+        occ_l = jnp.where(i < live32, jnp.exp2(a_lab[i] + b_lab[i + pad] + loss32), 0.0)
+        occ_b = jnp.exp2(a_blk[i, 0:n_lab] + b_blk[i + pad, 0:n_lab] + loss32)
+        occ_u = jnp.exp2(a_blk[i, n_lab:n_lab + 8] + b_blk[i + pad, n_lab:n_lab + 8] + loss8)
+        blank = jnp.sum(occ_b, **DOWN) + occ_u[0:1]
         blank = jnp.where(i < live8, jnp.broadcast_to(blank, (8, LANES)), 0.0)
-        acc_l = jnp.where(lax.rem(lane32, 64) == u, lanes_of(occ_l, back32), acc_l)
-        acc_b = jnp.where(lax.rem(lane8, 64) == u, lanes_of(blank, back8), acc_b)
+        acc_l = jnp.where(lax.rem(lane32, HALF) == u, lanes_of(occ_l, back32), acc_l)
+        acc_b = jnp.where(lax.rem(lane8, HALF) == u, lanes_of(blank, back8), acc_b)
         return acc_l, acc_b
 
     def occ_side(k, c):
@@ -437,8 +452,8 @@
             j = k * occ_group + g
             acc_l = jnp.zeros((n_lab, LANES), F32)
             acc_b = jnp.zeros((8, LANES), F32)
-            for u in range(64):
-                acc_l, acc_b = occ_frame(j * 64 + u, u, acc_l, acc_b)
+            for u in range(HALF):
+                acc_l, acc_b = occ_frame(j * HALF + u, u, acc_l, acc_b)
             o_t[j, 0:n_lab] = acc_l
             o_t[j, n_lab:n_lab + 8] = acc_b
             o_t[j, 8 + n_lab:LANES] = jnp.zeros((LANES - 8 - n_lab, LANES), F32)
@@ -450,19 +465,20 @@
         pass
     emit_stats(m_ref, s_ref, stats_ref, 0)
     row128 = lax.broadcasted_iota(jnp.int32, (LANES, LANES), 0)
-    inner = (row128 < n_lab) & (lane128 < n_lab)
     same = []
     for s in range(n_seq):
         down = jnp.full((n_lab, LANES), -1, jnp.int32)
         for k in range(n_lab):
             down = jnp.where(row32 == k, meta_ref[s, k], down)
         down = jnp.concatenate([down, jnp.full((LANES - n_lab, LANES), -1, jnp.int32)], axis=0)
-        across = jnp.broadcast_to(lab_row[s:s + 1], (LANES, LANES))
-        same.append(jnp.where((inner & (down == across)) | (row128 == lane128), 1.0, 0.0))
+        across = pltpu.roll(jnp.broadcast_to(lab_row[s:s + 1], (LANES, LANES)), HALF * s, 1)
+        own = lane128 - HALF * s
+        inner = (row128 < n_lab) & (own >= 0) & (own < n_lab)
+        same.append(jnp.where((inner & (down == across)) | ((row128 == own) & (own < HALF)), 1.0, 0.0))
     for j in range(n_blk):
         y = o_t[j].T
-        for s in range(2):
-            occ_ref[pl.ds(s * frames + 64 * j, 64), :] = jnp.dot(y[64 * s:64 * (s + 1), :], same[s], precision=lax.Precision.HIGHEST, preferred_element_type=F32)
+        occ_ref[HALF * j:HALF * (j + 1), :] = functools.reduce(jnp.add, [
+            jnp.dot(y[HALF * q:HALF * (q + 1), :], same[q], precision=lax.Precision.HIGHEST, preferred_element_type=F32) for q in range(n_seq)])
 
 
 def spread_lse(refs, base, meta_ref, lse_ref, r0, frames):
@@ -479,7 +495,7 @@
             part = jnp.broadcast_to(lse[at:at + 1, :], (LANES, LANES)).T
             live = t + p * LANES < meta_ref[q, meta_ref.shape[1] - 2]
             lse_ref[r0 + at * LANES:r0 + (at + 1) * LANES, :] = jnp.where(live, part, 1.0e30)
-            live_sum = live_sum + jnp.sum(jnp.where(live, part, 0.0), axis=0, keepdims=True)
+            live_sum = live_sum + jnp.sum(jnp.where(live, part, 0.0), **DOWN)
         sums.append(live_sum)
     return sums
 
@@ -491,8 +507,8 @@
     r0 = pl.multiple_of(seq * frames, frames)
     c0 = pl.multiple_of(blk * LANES, LANES)
     zb = z_block(seq, c0)
-    slot_lane = jnp.where(item == 0, n_slots - 1, item - 1)
-    occ = jnp.sum(jnp.where(lane == slot_lane, occ_ref[pl.ds(r0, frames), :], 0.0), axis=1, keepdims=True)
+    slot_lane = jnp.where(item == 0, n_slots - 1, item - 1) + HALF * seq
+    occ = jnp.sum(jnp.where(lane == slot_lane, occ_ref[...], 0.0), **ALONG)
     fresh = jnp.exp(zb - lse_ref[pl.ds(r0, frames), :]) - occ
     gc = pl.multiple_of(g_col + c0, LANES)
     old = g_ref[pl.ds(r0, frames), pl.ds(gc, LANES)].astype(F32)
@@ -522,7 +538,7 @@
     zs.prime()
     yield stream.prime
     col_start = build_lists(meta_refs, n_tiles * TILE, head, nxt)
-    sums = spread_lse([st0, st1, st2, st3], frames, meta_ref, lse_ref, 0, frames)
+    sums = spread_lse([st0, st1, st2, st3], frames // 2, meta_ref, lse_ref, 0, frames)
     lane1 = lax.broadcasted_iota(jnp.int32, (8, LANES), 1)
     loss_ref[...] = part_loss[...] + jnp.where(lane1 == 0, sums[0], sums[1])
     lane = lax.broadcasted_iota(jnp.int32, (frames, LANES), 1)
@@ -586,14 +602,14 @@
     send_ref[...] = acc[:, pl.ds(pl.multiple_of((1 - core) * n, n), n)].T
 
 
-def mid_kernel(lo, hi, n_lat, n_lab, h_got, h_core, w_hbm, m_in, s_in, p0, p1, p2, p3, z_own, meta_ref, z_in,
+def mid_kernel(lo, hi, n_lat, per_group, n_lab, h_got, h_core, w_hbm, p0, p1, p2, p3, z_own, meta_ref,
                z_hbm, stats_ref, occ_ref, keep_ref, send_ref, loss_ref, g_hbm,
                part_loss, m_ref, s_ref, h_ref, hsem, wbuf, wsem, zbuf, zsem, e_lab, e_blk, a_lab, a_blk, b_lab, b_blk, o_t,
                zin_buf, zin_sem, acc, lse_ref, g0, g1, gsem, head, nxt):
     second = grad_h_part(n_lab + 1, z_own, w_hbm, p0, p1, p2, p3, occ_ref, part_loss, meta_ref, keep_ref, send_ref, loss_ref, g_hbm,
                          wbuf, wsem, zin_buf, zin_sem, acc, lse_ref, g0, g1, gsem, head, nxt)
     prime_w = next(second)
-    z_lattice_part(lo, hi, n_lat, n_lab, prime_w, h_got, h_core, w_hbm, m_in, s_in, p0, p1, p2, p3, meta_ref,
+    z_lattice_part(lo, hi, n_lat, per_group, n_lab, prime_w, h_got, h_core, w_hbm, p0, p1, p2, p3, meta_ref,
                    z_hbm, stats_ref, occ_ref, part_loss, m_ref, s_ref,
                    h_ref, hsem, wbuf, wsem, zbuf, zsem, e_lab, e_blk, a_lab, a_blk, b_lab, b_blk, o_t)
     for _ in second:
@@ -713,7 +729,7 @@
         d_loc = model_dim // n_dp
         dma = pltpu.SemaphoreType.DMA
         i32 = jnp.int32
-        cut_a, n_lat = 8, 16
+        n_lat, lat_steps, lat_pad = 24, 22, 8
         h_own = hidden.reshape(rows, model_dim)
         core = lax.rem(lax.axis_index("tp"), 2)
         h_half = lax.dynamic_index_in_dim(h_own.reshape(2, rows // 2, model_dim), core, 0, keepdims=False)
@@ -722,8 +738,7 @@
         wbytes = model_dim * TILE * 2
         zbytes = rows * TILE * 4
         z_type = jax.ShapeDtypeStruct((n_tiles, rows, TILE), F32)
-        run_type = jax.ShapeDtypeStruct((rows, LANES), F32)
-        pick_type = jax.ShapeDtypeStruct((frames + 16, LANES), F32)
+        pick_type = jax.ShapeDtypeStruct((frames // 2 + 24, LANES), F32)
         meta_type = jax.ShapeDtypeStruct((batch_loc, n_slots + 1), i32)
         g_type = jax.ShapeDtypeStruct((n_tiles // 2, rows, 2 * TILE), BF16)
         stat_type = jax.ShapeDtypeStruct((16, LANES), F32)
@@ -746,7 +761,7 @@
             out_shape=(z_type, pick_type, meta_type),
             in_specs=[any_spec(), any_spec(), smem_spec(), smem_spec(), smem_spec()],
             out_specs=(any_spec(), vmem_spec(), smem_spec()),
-            scratch_shapes=h_scratch + w_scratch(4) + z_scratch(4) + run_scratch + lists(1),
+            scratch_shapes=h_scratch + w_scratch(4) + z_scratch(4) + run_scratch + [pltpu.VMEM((frames // 2, LANES), F32)] + lists(1),
             compiler_params=params(),
             cost_estimate=cost(n_tiles * flops, n_tiles * (wbytes + zbytes)),
         )(in_hbm(h_own), w_loc, labels, in_len, lab_len)
@@ -756,34 +771,24 @@
         h_got = in_hbm(h_got)
         picks = [pick] + [tp_xor(pick, k) for k in others]
 
-        z_part, run_m, run_s = kernel_call(
-            functools.partial(z_first_kernel, 0, cut_a),
-            out_shape=(z_type, run_type, run_type),
-            in_specs=[any_spec()] * 3,
-            out_specs=(any_spec(), vmem_spec(), vmem_spec()),
-            scratch_shapes=h_scratch + w_scratch(4) + z_scratch(4),
-            compiler_params=params(),
-            cost_estimate=cost(cut_a * flops, cut_a * (wbytes + zbytes)),
-        )(h_got, h_core, w_loc)
-
-        n_blk = frames // 64
+        n_blk = frames // HALF
         half_type = jax.ShapeDtypeStruct((rows // 2, model_dim), F32)
+        occ_type = jax.ShapeDtypeStruct((frames, LANES), F32)
         loss_type = jax.ShapeDtypeStruct((8, LANES), F32)
         z_oth, stats_oth, occ, keep, send, loss, g_own = kernel_call(
-            functools.partial(mid_kernel, cut_a, n_tiles, n_lat, n_lab),
-            out_shape=(z_type, stat_type, run_type, half_type, half_type, loss_type, g_type),
-            in_specs=[any_spec()] * 3 + [vmem_spec()] * 6 + [any_spec(), smem_spec(), any_spec()],
+            functools.partial(mid_kernel, 0, n_tiles, n_lat, lat_steps, n_lab),
+            out_shape=(z_type, stat_type, occ_type, half_type, half_type, loss_type, g_type),
+            in_specs=[any_spec()] * 3 + [vmem_spec()] * 4 + [any_spec(), smem_spec()],
             out_specs=(any_spec(),) + (vmem_spec(),) * 5 + (any_spec(),),
-            input_output_aliases={11: 0},
             scratch_shapes=[pltpu.VMEM((8, LANES), F32)] + run_scratch + h_scratch + w_scratch(2) + z_scratch(2) + [
                 pltpu.VMEM((n_blk, n_lab, LANES), F32), pltpu.VMEM((n_blk, 8, LANES), F32),
-                pltpu.VMEM((frames, n_lab, LANES), F32), pltpu.VMEM((frames, n_lab + 8, LANES), F32),
-                pltpu.VMEM((frames, n_lab, LANES), F32), pltpu.VMEM((frames, n_lab + 8, LANES), F32),
+                pltpu.VMEM((frames + lat_pad, n_lab, LANES), F32), pltpu.VMEM((frames + lat_pad, n_lab + 8, LANES), F32),
+                pltpu.VMEM((frames + lat_pad, n_lab, LANES), F32), pltpu.VMEM((frames + lat_pad, n_lab + 8, LANES), F32),
                 pltpu.VMEM((n_blk, LANES, LANES), F32)] + z_scratch(2) + [
                 pltpu.VMEM((model_dim, rows), F32), pltpu.VMEM((rows, LANES), F32)] + g_scratch + [dma((2,))] + lists(1),
             compiler_params=params(),
-            cost_estimate=cost((2 * n_tiles - cut_a) * flops, (2 * n_tiles - cut_a) * (wbytes + zbytes)),
-        )(h_got, h_core, w_loc, run_m, run_s, *picks, z_own, meta, z_part)
+            cost_estimate=cost((2 * n_tiles) * flops, (2 * n_tiles) * (wbytes + zbytes)),
+        )(h_got, h_core, w_loc, *picks, z_own, meta)
         st_oth = [stats_oth] + [tp_xor(stats_oth, k) for k in others]
         occ_oth = swap_dp(occ)
         meta_oth = swap_dp(meta)

time: 180 us -> 174 us (0.967)
  Pallas kernels: 156 us -> 149 us
  waiting for transfers between devices: 5.68 us -> 7.69 us
    pallas_call x2 -> x1, Pallas kernels: 84.6 us -> 77.4 us  [local_body(): kernel_call(functools.partial(mid_kernel, 0, n_tiles, n_lat, lat_steps, n...]
    ppermute x10, waiting for transfers between devices: 2.54 us -> 6.62 us  [tp_xor(): return lax.ppermute(x, 'tp', [(i, i ^ mask) for i in range(n_tp)])]
    ppermute x3, waiting for transfers between devices: 3.14 us -> 1.07 us  [swap_dp(): return lax.ppermute(x, 'dp', dp_swap)]
  transfers between devices with their start and end apart: 13 -> 13, of which waited for: 4 -> 6; matrix products, arithmetic and copies ran while one was open for 1% -> 2% of each run, Pallas kernels for 47% -> 41%
where the time goes in v2:
time: 174 us
  Pallas kernels  149 us (86%)
  starting transfers between devices  9.41 us (5%)
  waiting for transfers between devices  7.69 us (4%)
  local copies, waits for them, and re-layouts  3.85 us (2%)
  other arithmetic  3.28 us (2%)
    pallas_call x1, Pallas kernels, local_body(): kernel_call(functools.partial(mid_kernel, 0, n_tiles, n_lat, lat_steps, n...  77.4 us
    pallas_call x1, Pallas kernels, local_body(): kernel_call(functools.partial(grad_w_kernel, n_slots), out_shape=jax.Shap...  37.5 us
    pallas_call x1, Pallas kernels, local_body(): kernel_call(functools.partial(z_own_kernel, n_slots), out_shape=(z_type,...  33.7 us
    ppermute x10, waiting for transfers between devices, tp_xor(): return lax.ppermute(x, 'tp', [(i, i ^ mask) for i in range(n_tp)])  6.62 us
    ppermute x3, starting transfers between devices, swap_dp(): return lax.ppermute(x, 'dp', dp_swap)  4.92 us
    ppermute x10, starting transfers between devices, tp_xor(): return lax.ppermute(x, 'tp', [(i, i ^ mask) for i in range(n_tp)])  4.49 us
  transfers between devices with their start and end apart: 13, of which 6 were waited for; matrix products, arithmetic and copies ran while one was open for 2% of the time, Pallas kernels for 41%

profile of v2, /device:TPU:0, one launch (start us, length us, event | category | flops | bytes accessed | tf_op | source)
XLA Modules:
  0.0 173.7 jit_solution(14013932028293105087)
XLA Ops:
  0.6 1.1 dynamic-slice_bitcast_fusion
  1.8 3.4 %collective-permute-start = (bf16[256,1280]{1,0:T(8,128)(2,1)S(1)}, bf16[256,1280]{1,0:T(8,128)(2,1)S(1)}, u32[]{:S(2)}, u32[]{:S(2)}) collective-permute-start(bf16[256,1280]{1,0:T(8,128)(2,1)S(1)} %dynamic-slice_bitcast_fusion), channel_id=1, source_target_pairs={{0,4},{4,0},{1,5},{5,1},{2,6},{6,2},{3,7},{7,3}} | collective-permute-start | bytes 1966088 | tf_op jit(solution)/shard_map/ppermute | solution.py:720
  5.1 33.7 %shard_map.76 = (f32[32,512,512]{2,1,0:T(8,128)}, f32[152,128]{1,0:T(8,128)}, s32[2,34]{1,0:T(2,128)}) custom-call(bf16[512,1280]{1,0:T(8,128)(2,1)} %bitcast.8, bf16[1280,16384]{1,0:T(8,128)(2,1)} %w_hbm.3, s32[2,32]{1,0:T(2,128)} %labels_ref.1, s32[2]{0:T(128)} %in_len_ref.1, s32[2]{0:T(128)} %lab_len_ref.1), custom_call_target="tpu_custom_call" | custom-call | flops 21474836480 | bytes 75497472 | tf_op jit(solution)/shard_map/pallas_call | solution.py:759
  38.9 0.5 collective-permute-start.2
  39.4 0.8 collective-permute-start.3
  40.3 0.5 collective-permute-start.4
  40.8 0.3 collective-permute-done.2.p1
  41.1 3.5 %collective-permute-done.3.p2 = f32[152,128]{1,0:T(8,128)S(1)} collective-permute-done((f32[152,128]{1,0:T(8,128)}, f32[152,128]{1,0:T(8,128)S(1)}, u32[]{:S(2)}, u32[]{:S(2)}) %collective-permute-start.3) | collective-permute-done | bytes 77856 | tf_op jit(solution)/shard_map/ppermute | solution.py:714
  44.6 0.5 collective-permute-done.4.p3
  45.2 0.5 copy-done.9
  45.8 0.2 copy-done.1
  46.0 77.4 %shard_map.77 = (f32[32,512,512]{2,1,0:T(8,128)}, f32[16,128]{1,0:T(8,128)}, f32[256,128]{1,0:T(8,128)}, f32[256,1280]{1,0:T(8,128)}, f32[256,1280]{1,0:T(8,128)...) custom-call(bf16[256,1280]{1,0:T(8,128)(2,1)} %copy-done, bf16[256,1280]{1,0:T(8,128)(2,1)} %copy-done.1, ...), custom_call_target="tpu_custom_call" | custom-call | flops 42949672960 | bytes 150994944 | tf_op jit(solution)/shard_map/pallas_call | solution.py:778
  123.5 0.5 collective-permute-start.5
  124.0 0.5 collective-permute-start.9
  124.5 1.9 %collective-permute-start.8 = (f32[16,128]{1,0:T(8,128)}, f32[16,128]{1,0:T(8,128)S(1)}, u32[]{:S(2)}, u32[]{:S(2)}) collective-permute-start(f32[16,128]{1,0:T(8,128)} %get-tuple-element.27.st0), channel_id=1, source_target_pairs={{0,3},{1,2},{2,1},{3,0},{4,7},{5,6},{6,5},{7,4}} | collective-permute-start | bytes 24584 | tf_op jit(solution)/shard_map/ppermute | solution.py:714
  126.4 0.5 collective-permute-done.5
  126.9 1.0 collective-permute-start.10
  127.9 1.5 add.11
  129.4 1.1 collective-permute-done.10.meta_ref
  130.7 0.3 copy-done.6
  131.3 37.5 %shard_map.78 = f32[640,16384]{1,0:T(8,128)} custom-call(bf16[16,512,1024]{2,1,0:T(8,128)(2,1)} %get-tuple-element.25.g_hbm, f32[32,512,512]{2,1,0:T(8,128)} %get-tuple-element.26.z_hbm, bf16[512,1280]{1,0:T(8,128)(2,1)} %bitcast.9, bf16[256,1280]{1,0:T(8,128)(2,1)} %copy-done, bf16[256,1280]{1,0:T(8,128)(2,1)} %copy-done.1, ...), custom_call_target="tpu_custom_call" | custom-call | flops 21474836480 | bytes 109051904 | tf_op jit(solution)/shard_map/pallas_call | solution.py:799
  169.1 1.2 slice_bitcast_fusion
  170.3 1.8 %collective-permute-done.12 = f32[256,1280]{1,0:T(8,128)S(1)} collective-permute-done((f32[256,1280]{1,0:T(8,128)S(1)}, f32[256,1280]{1,0:T(8,128)S(1)}, u32[]{:S(2)}, u32[]{:S(2)}) %collective-permute-start.12) | collective-permute-done | bytes 1310752 | tf_op jit(solution)/shard_map/ppermute | solution.py:714
  172.1 1.7 maximum_select_fusion
  (32 shorter events, 0.8 us)
Async XLA Ops:
  1.8 37.1 %collective-permute-start = (bf16[256,1280]{1,0:T(8,128)(2,1)S(1)}, bf16[256,1280]{1,0:T(8,128)(2,1)S(1)}, u32[]{:S(2)}, u32[]{:S(2)}) collective-permute-start(bf16[256,1280]{1,0:T(8,128)(2,1)S(1)} %dynamic-slice_bitcast_fusion), channel_id=1, source_target_pairs={{0,4},{4,0},{1,5},{5,1},{2,6},{6,2},{3,7},{7,3}} | collective-permute-start | bytes 1966088 | tf_op jit(solution)/shard_map/ppermute | solution.py:720
  38.9 6.3 %copy-start = (bf16[256,1280]{1,0:T(8,128)(2,1)}, bf16[256,1280]{1,0:T(8,128)(2,1)S(1)}, u32[]{:S(2)}) copy-start(bf16[256,1280]{1,0:T(8,128)(2,1)S(1)} %collective-permute-done.h_got) | copy-start | bytes 1966084
  38.9 6.2 %collective-permute-start.1 = (bf16[256,1280]{1,0:T(8,128)(2,1)S(1)}, bf16[256,1280]{1,0:T(8,128)(2,1)S(1)}, u32[]{:S(2)}, u32[]{:S(2)}) collective-permute-start(bf16[256,1280]{1,0:T(8,128)(2,1)S(1)} %collective-permute-done.h_got), channel_id=1, source_target_pairs={{0,1},{1,0},{2,3},{3,2},{4,5},{5,4},{6,7},{7,6}} | collective-permute-start | bytes 1966088 | tf_op jit(solution)/shard_map/ppermute | solution.py:714
  38.9 2.2 %collective-permute-start.2 = (f32[152,128]{1,0:T(8,128)}, f32[152,128]{1,0:T(8,128)S(1)}, u32[]{:S(2)}, u32[]{:S(2)}) collective-permute-start(f32[152,128]{1,0:T(8,128)} %get-tuple-element.19.p0), channel_id=1, source_target_pairs={{0,1},{1,0},{2,3},{3,2},{4,5},{5,4},{6,7},{7,6}} | collective-permute-start | bytes 233480 | tf_op jit(solution)/shard_map/ppermute | solution.py:714
  39.4 5.2 %collective-permute-start.3 = (f32[152,128]{1,0:T(8,128)}, f32[152,128]{1,0:T(8,128)S(1)}, u32[]{:S(2)}, u32[]{:S(2)}) collective-permute-start(f32[152,128]{1,0:T(8,128)} %get-tuple-element.19.p0), channel_id=1, source_target_pairs={{0,2},{1,3},{2,0},{3,1},{4,6},{5,7},{6,4},{7,5}} | collective-permute-start | bytes 233480 | tf_op jit(solution)/shard_map/ppermute | solution.py:714
  40.3 4.9 %collective-permute-start.4 = (f32[152,128]{1,0:T(8,128)}, f32[152,128]{1,0:T(8,128)S(1)}, u32[]{:S(2)}, u32[]{:S(2)}) collective-permute-start(f32[152,128]{1,0:T(8,128)} %get-tuple-element.19.p0), channel_id=1, source_target_pairs={{0,3},{1,2},{2,1},{3,0},{4,7},{5,6},{6,5},{7,4}} | collective-permute-start | bytes 233480 | tf_op jit(solution)/shard_map/ppermute | solution.py:714
  41.1 4.0 %copy-start.7 = (f32[152,128]{1,0:T(8,128)}, f32[152,128]{1,0:T(8,128)S(1)}, u32[]{:S(2)}) copy-start(f32[152,128]{1,0:T(8,128)S(1)} %collective-permute-done.2.p1) | copy-start | bytes 233476
  44.6 0.6 copy-start.8
  45.1 0.6 copy-start.9
  45.1 0.9 copy-start.1
  46.0 80.8 %copy-start.10 = (s32[2,34]{1,0:T(2,128)S(1)}, s32[2,34]{1,0:T(2,128)}, u32[]{:S(2)}) copy-start(s32[2,34]{1,0:T(2,128)} %get-tuple-element.21.meta_ref) | copy-start | bytes 820
  123.5 3.4 %collective-permute-start.5 = (f32[256,1280]{1,0:T(8,128)}, f32[256,1280]{1,0:T(8,128)S(1)}, u32[]{:S(2)}, u32[]{:S(2)}) collective-permute-start(f32[256,1280]{1,0:T(8,128)} %get-tuple-element.24), channel_id=1, source_target_pairs={{0,1},{1,0},{2,3},{3,2},{4,5},{5,4},{6,7},{7,6}} | collective-permute-start | bytes 3932168 | tf_op jit(solution)/shard_map/ppermute | solution.py:714
  124.0 6.7 %collective-permute-start.9 = (f32[256,128]{1,0:T(8,128)}, f32[256,128]{1,0:T(8,128)S(1)}, u32[]{:S(2)}, u32[]{:S(2)}) collective-permute-start(f32[256,128]{1,0:T(8,128)} %get-tuple-element.28), channel_id=1, source_target_pairs={{0,4},{4,0},{1,5},{5,1},{2,6},{6,2},{3,7},{7,3}} | collective-permute-start | bytes 393224 | tf_op jit(solution)/shard_map/ppermute | solution.py:720
  124.5 6.1 %collective-permute-start.6 = (f32[16,128]{1,0:T(8,128)}, f32[16,128]{1,0:T(8,128)S(1)}, u32[]{:S(2)}, u32[]{:S(2)}) collective-permute-start(f32[16,128]{1,0:T(8,128)} %get-tuple-element.27.st0), channel_id=1, source_target_pairs={{0,1},{1,0},{2,3},{3,2},{4,5},{5,4},{6,7},{7,6}} | collective-permute-start | bytes 24584 | tf_op jit(solution)/shard_map/ppermute | solution.py:714
  124.5 6.1 %collective-permute-start.7 = (f32[16,128]{1,0:T(8,128)}, f32[16,128]{1,0:T(8,128)S(1)}, u32[]{:S(2)}, u32[]{:S(2)}) collective-permute-start(f32[16,128]{1,0:T(8,128)} %get-tuple-element.27.st0), channel_id=1, source_target_pairs={{0,2},{1,3},{2,0},{3,1},{4,6},{5,7},{6,4},{7,5}} | collective-permute-start | bytes 24584 | tf_op jit(solution)/shard_map/ppermute | solution.py:714
  124.5 6.1 %collective-permute-start.8 = (f32[16,128]{1,0:T(8,128)}, f32[16,128]{1,0:T(8,128)S(1)}, u32[]{:S(2)}, u32[]{:S(2)}) collective-permute-start(f32[16,128]{1,0:T(8,128)} %get-tuple-element.27.st0), channel_id=1, source_target_pairs={{0,3},{1,2},{2,1},{3,0},{4,7},{5,6},{6,5},{7,4}} | collective-permute-start | bytes 24584 | tf_op jit(solution)/shard_map/ppermute | solution.py:714
  126.9 3.6 %collective-permute-start.10 = (s32[2,34]{1,0:T(2,128)S(1)}, s32[2,34]{1,0:T(2,128)S(1)}, u32[]{:S(2)}, u32[]{:S(2)}) collective-permute-start(s32[2,34]{1,0:T(2,128)S(1)} %copy-done.10), channel_id=1, source_target_pairs={{0,4},{4,0},{1,5},{5,1},{2,6},{6,2},{3,7},{7,3}} | collective-permute-start | bytes 824 | tf_op jit(solution)/shard_map/ppermute | solution.py:720
  130.4 0.6 copy-start.6
  130.4 38.4 %collective-permute-start.11 = (f32[256,1280]{1,0:T(8,128)S(1)}, f32[256,1280]{1,0:T(8,128)S(1)}, u32[]{:S(2)}, u32[]{:S(2)}) collective-permute-start(f32[256,1280]{1,0:T(8,128)S(1)} %add.11), channel_id=1, source_target_pairs={{0,2},{1,3},{2,0},{3,1},{4,6},{5,7},{6,4},{7,5}} | collective-permute-start | bytes 3932168 | tf_op jit(solution)/shard_map/ppermute | solution.py:714
  130.6 0.6 copy-start.3
  130.6 0.6 copy-start.4
  130.6 0.6 copy-start.5
  130.7 0.7 copy-start.2
  169.0 3.1 %collective-permute-start.12 = (f32[256,1280]{1,0:T(8,128)S(1)}, f32[256,1280]{1,0:T(8,128)S(1)}, u32[]{:S(2)}, u32[]{:S(2)}) collective-permute-start(f32[256,1280]{1,0:T(8,128)S(1)} %add.12), channel_id=1, source_target_pairs={{0,1},{1,0},{2,3},{3,2},{4,5},{5,4},{6,7},{7,6}} | collective-permute-start | bytes 3932168 | tf_op jit(solution)/shard_map/ppermute | solution.py:714

commit v3 on v2

--- a/solution.py
+++ b/solution.py
@@ -298,7 +298,7 @@
 
 def z_lattice_part(lo, hi, n_lat, per_group, n_lab, before_tail, h_got, h_core, w_hbm, p0, p1, p2, p3, meta_ref,
                      z_hbm, stats_ref, occ_ref, loss_ref, m_ref, s_ref,
-                     h_ref, hsem, wbuf, wsem, zbuf, zsem, e_lab, e_blk, a_lab, a_blk, b_lab, b_blk, o_t):
+                     h_ref, hsem, wbuf, wsem, zbuf, zsem, e_lab, e_blk, s_lab, s_blk, r_lab, r_blk, o_t):
     join = JoinRows(h_got, h_core, h_ref, hsem)
     join.start()
     n_blk = e_lab.shape[0]
@@ -317,10 +317,11 @@
     used8 = jnp.zeros((8, LANES), jnp.int32)
     for s in range(n_seq):
         for k in range(n_lab):
-            labs = jnp.where((row32 == k) & (lane32 == s), meta_ref[s, k], labs)
+            labs = jnp.where((row32 == k) & ((lane32 == s) | (lane32 == s + n_seq)), meta_ref[s, k], labs)
             lab_row = jnp.where((row8 == s) & (lane8 == k), meta_ref[s, k], lab_row)
-        live8 = jnp.where(lane8 == s, meta_ref[s, n_lab], live8)
-        used8 = jnp.where(lane8 == s, meta_ref[s, n_lab + 1], used8)
+        here = (lane8 == s) | (lane8 == s + n_seq)
+        live8 = jnp.where(here, meta_ref[s, n_lab], live8)
+        used8 = jnp.where(here, meta_ref[s, n_lab + 1], used8)
     live32 = jnp.broadcast_to(live8[0:1], (n_lab, LANES))
     used32 = jnp.broadcast_to(used8[0:1], (n_lab, LANES))
     skip_dn = labs != pltpu.roll(labs, 1, 0)
@@ -358,59 +359,56 @@
         mid = jnp.minimum(hi_v, c)
         return top + jnp.log2(1.0 + (jnp.exp2(lo_v - top) + jnp.exp2(mid - top)))
 
-    pick32 = jnp.where(lane32 == 1, HALF, 0)
-    pick8 = jnp.where(lane8 == 1, HALF, 0)
+    fwd8, fwd32 = lane8 < n_seq, lane32 < n_seq
+    ahead8 = fwd8 & (row8 == 0)
+    behind8 = (lane8 >= n_seq) & (row8 == 7)
+    base8 = jnp.where(fwd8, HALF * lane8, HALF * (lane8 - n_seq) + HALF - 1)
+    base8 = jnp.where(lane8 < 2 * n_seq, base8, HALF)
+    skip = jnp.where(fwd32, jnp.where(skip_dn & (row32 > 0), 1, 0), jnp.where(skip_up & (row32 < n_lab - 1), 1, 0)) > 0
 
     def lanes_of(x, idx):
         return jnp.take_along_axis(x, idx, axis=1, mode="promise_in_bounds")
 
-    def emission(j, u):
-        return lanes_of(e_lab[j], pick32 + u), lanes_of(e_blk[j], pick8 + u)
+    def tall(x):
+        return jnp.concatenate([x] * (n_lab // 8), axis=0)
 
     neg32 = jnp.full((n_lab, LANES), NEG_BIG, F32)
-    neg8 = jnp.full((8, LANES), NEG_BIG, F32)
-    start32 = jnp.where(row32 == 0, 0.0, NEG_BIG)
-    fin_b = jnp.where(end_blk, 0.0, NEG_BIG)
-    fin_t = jnp.where(end_top, 0.0, NEG_BIG)
-    skip_dn = skip_dn & (row32 > 0)
-    skip_up = skip_up & (row32 < n_lab - 1)
+    first_b = jnp.where(fwd32, jnp.where(row32 == 0, 0.0, NEG_BIG), jnp.where(end_blk, 0.0, NEG_BIG))
+    first_t = jnp.where(fwd8, NEG_BIG, jnp.where(end_top, 0.0, NEG_BIG))
 
     def lat_step(i, j, u, carry):
-        al, ab, at, bl, bb, bt = carry
-        el, eb = emission(j, u)
-        eb32 = jnp.broadcast_to(eb[0:1], (n_lab, LANES))
-        rolled = pltpu.roll(al, 1, 0)
-        prev = jnp.where(row32 == 0, NEG_BIG, rolled)
-        prev_t = jnp.where(row8 == 0, rolled[0:8], NEG_BIG)
-        nl = lse3(al, ab, jnp.where(skip_dn, rolled, NEG_BIG))
-        nb = lse2(ab, prev)
-        nt = lse2(at, prev_t)
-        a_lab[i] = nl
-        a_blk[i, 0:n_lab] = nb
-        a_blk[i, n_lab:n_lab + 8] = nt
-        al = jnp.where(i < live32, el + nl, al)
-        ab = jnp.where(i < live32, eb32 + nb, ab)
-        at = jnp.where(i < live8, eb + nt, at)
-        t = frames - 1 - i
-        fl, fb = emission(n_blk - 1 - j, 63 - u)
-        fb32 = jnp.broadcast_to(fb[0:1], (n_lab, LANES))
-        last = row32 == n_lab - 1
-        up_l = jnp.where(skip_up, pltpu.roll(bl, n_lab - 1, 0), NEG_BIG)
-        up_b = jnp.where(last, jnp.broadcast_to(bt[0:1], (n_lab, LANES)), pltpu.roll(bb, n_lab - 1, 0))
-        ml = fl + lse3(bl, up_b, up_l)
-        mb = fb32 + lse2(bb, bl)
-        mt = fb + bt
-        bl = jnp.where(t < live32, ml, bl)
-        bb = jnp.where(t < live32, mb, bb)
-        bt = jnp.where(t < live8, mt, bt)
-        b_lab[t + pad] = bl
-        b_blk[t + pad, 0:n_lab] = bb
-        b_blk[t + pad, n_lab:n_lab + 8] = bt
-        return al, ab, at, bl, bb, bt
+        lab, blk, top_b = carry
+        idx8 = base8 + jnp.where(fwd8, u, -u)
+        idx32 = tall(idx8)
+        back = n_blk - 1 - j
+        e_l = jnp.where(fwd32, lanes_of(e_lab[j], idx32), lanes_of(e_lab[back], idx32))
+        e_b = jnp.where(fwd8, lanes_of(e_blk[j], idx8), lanes_of(e_blk[back], idx8))
+        lab_dn = pltpu.roll(lab, 1, 0)
+        lab_up = pltpu.roll(lab, n_lab - 1, 0)
+        blk_side = jnp.where(fwd32, blk, pltpu.roll(blk, n_lab - 1, 0))
+        blk_side = jnp.concatenate([blk_side[:n_lab - 8], jnp.where(behind8, jnp.broadcast_to(top_b[0:1], (8, LANES)), blk_side[n_lab - 8:])], axis=0)
+        lab_side = jnp.where(fwd32, lab_dn, lab)
+        lab_side = jnp.concatenate([jnp.where(ahead8, NEG_BIG, lab_side[:8]), lab_side[8:]], axis=0)
+        new_l = lse3(lab, blk_side, jnp.where(skip, jnp.where(fwd32, lab_dn, lab_up), NEG_BIG))
+        new_b = lse2(blk, lab_side)
+        new_t = lse2(top_b, jnp.where(ahead8, lab_dn[:8], NEG_BIG))
+        s_lab[i] = new_l
+        s_blk[i, 0:n_lab] = new_b
+        s_blk[i, n_lab:n_lab + 8] = new_t
+        behind = frames - 1 - i + pad
+        r_lab[behind] = pltpu.roll(new_l, LANES - n_seq, 1)
+        r_blk[behind, 0:n_lab] = pltpu.roll(new_b, LANES - n_seq, 1)
+        r_blk[behind, n_lab:n_lab + 8] = pltpu.roll(new_t, LANES - n_seq, 1)
+        at8 = jnp.where(fwd8, i, frames - 1 - i)
+        live = tall(at8) < live32
+        lab = jnp.where(live, e_l + new_l, lab)
+        blk = jnp.where(live, tall(e_b) + new_b, blk)
+        top_b = jnp.where(at8 < live8, e_b + new_t, top_b)
+        return lab, blk, top_b
 
     group = zbuf.shape[1]
     n_lat_groups = n_lat // group
-    pad = b_lab.shape[0] - frames
+    pad = s_lab.shape[0] - frames
 
     def lattice_side(k, carry):
         for u in range(per_group):
@@ -421,41 +419,40 @@
 
     n_occ = (hi - lo - n_lat) // group
     occ_group = frames // n_occ // HALF
-    back32 = jnp.where(lane32 >= HALF, 1, 0)
-    back8 = jnp.where(lane8 >= HALF, 1, 0)
+    seq_of8 = jnp.where(lane8 >= HALF, 1, 0)
     run = z_oth_loop(lo, hi, join, h_ref, w_hbm, z_hbm, wbuf, wsem, zbuf, zsem, m_ref, s_ref,
-                     [(n_lat_groups, lattice_side, lambda: (neg32, start32, neg8, neg32, fin_b, fin_t)),
+                     [(n_lat_groups, lattice_side, lambda: (neg32, first_b, first_t)),
                       (n_occ, lambda k, c: occ_side(k, c), lambda: 0)])
-    al, ab, at, _, _, _ = next(run)
+    al, ab, at = next(run)
 
     lasts = [jnp.where(end, v, NEG_BIG) for end, v in ((end_lab, al), (end_blk, ab), (end_top, at))]
     top = functools.reduce(jnp.maximum, [jnp.max(v, **DOWN) for v in lasts])
     total = functools.reduce(jnp.add, [jnp.sum(jnp.exp2(v - top), **DOWN) for v in lasts])
     loss = -(top + jnp.log2(total))
-    loss32 = jnp.broadcast_to(loss, (n_lab, LANES))
-    loss8 = jnp.broadcast_to(loss, (8, LANES))
+    loss_at = lanes_of(jnp.broadcast_to(loss, (8, LANES)), seq_of8)
     lane1 = lane8[0:1]
     loss_ref[...] = jnp.broadcast_to(loss * (1.0 / LOG2E) - jnp.where(lane1 == 0, shift_seq0, jnp.where(lane1 == 1, shift_seq1, 0.0)), (8, LANES))
-
-    def occ_frame(i, u, acc_l, acc_b):
-        occ_l = jnp.where(i < live32, jnp.exp2(a_lab[i] + b_lab[i + pad] + loss32), 0.0)
-        occ_b = jnp.exp2(a_blk[i, 0:n_lab] + b_blk[i + pad, 0:n_lab] + loss32)
-        occ_u = jnp.exp2(a_blk[i, n_lab:n_lab + 8] + b_blk[i + pad, n_lab:n_lab + 8] + loss8)
-        blank = jnp.sum(occ_b, **DOWN) + occ_u[0:1]
-        blank = jnp.where(i < live8, jnp.broadcast_to(blank, (8, LANES)), 0.0)
-        acc_l = jnp.where(lax.rem(lane32, HALF) == u, lanes_of(occ_l, back32), acc_l)
-        acc_b = jnp.where(lax.rem(lane8, HALF) == u, lanes_of(blank, back8), acc_b)
-        return acc_l, acc_b
 
     def occ_side(k, c):
         for g in range(occ_group):
             j = k * occ_group + g
-            acc_l = jnp.zeros((n_lab, LANES), F32)
-            acc_b = jnp.zeros((8, LANES), F32)
+            seq_of32 = tall(seq_of8)
+            logs = [neg32, neg32, neg32[0:8]]
             for u in range(HALF):
-                acc_l, acc_b = occ_frame(j * HALF + u, u, acc_l, acc_b)
-            o_t[j, 0:n_lab] = acc_l
-            o_t[j, n_lab:n_lab + 8] = acc_b
+                i = j * HALF + u
+                here8 = lax.rem(lane8, HALF) == u
+                here32 = lax.rem(lane32, HALF) == u
+                sum_l = s_lab[i] + r_lab[i + pad]
+                sum_b = s_blk[i] + r_blk[i + pad]
+                logs[0] = jnp.where(here32, lanes_of(sum_l, seq_of32), logs[0])
+                logs[1] = jnp.where(here32, lanes_of(sum_b[:n_lab], seq_of32), logs[1])
+                logs[2] = jnp.where(here8, lanes_of(sum_b[n_lab:], seq_of8), logs[2])
+            rest = e_blk[j] + loss_at
+            live = lax.rem(lane8, HALF) + HALF * j < jnp.broadcast_to(half_len, (8, LANES))
+            occ_l = jnp.exp2(logs[0] + e_lab[j] + tall(loss_at))
+            occ_b = jnp.sum(jnp.exp2(logs[1] + tall(rest)), **DOWN) + jnp.exp2(logs[2] + rest)[0:1]
+            o_t[j, 0:n_lab] = jnp.where(tall(jnp.where(live, 1, 0)) > 0, occ_l, 0.0)
+            o_t[j, n_lab:n_lab + 8] = jnp.where(live, jnp.broadcast_to(occ_b, (8, LANES)), 0.0)
             o_t[j, 8 + n_lab:LANES] = jnp.zeros((LANES - 8 - n_lab, LANES), F32)
         return c
 
@@ -604,14 +601,14 @@
 
 def mid_kernel(lo, hi, n_lat, per_group, n_lab, h_got, h_core, w_hbm, p0, p1, p2, p3, z_own, meta_ref,
                z_hbm, stats_ref, occ_ref, keep_ref, send_ref, loss_ref, g_hbm,
-               part_loss, m_ref, s_ref, h_ref, hsem, wbuf, wsem, zbuf, zsem, e_lab, e_blk, a_lab, a_blk, b_lab, b_blk, o_t,
+               part_loss, m_ref, s_ref, h_ref, hsem, wbuf, wsem, zbuf, zsem, e_lab, e_blk, s_lab, s_blk, r_lab, r_blk, o_t,
                zin_buf, zin_sem, acc, lse_ref, g0, g1, gsem, head, nxt):
     second = grad_h_part(n_lab + 1, z_own, w_hbm, p0, p1, p2, p3, occ_ref, part_loss, meta_ref, keep_ref, send_ref, loss_ref, g_hbm,
                          wbuf, wsem, zin_buf, zin_sem, acc, lse_ref, g0, g1, gsem, head, nxt)
     prime_w = next(second)
     z_lattice_part(lo, hi, n_lat, per_group, n_lab, prime_w, h_got, h_core, w_hbm, p0, p1, p2, p3, meta_ref,
                    z_hbm, stats_ref, occ_ref, part_loss, m_ref, s_ref,
-                   h_ref, hsem, wbuf, wsem, zbuf, zsem, e_lab, e_blk, a_lab, a_blk, b_lab, b_blk, o_t)
+                   h_ref, hsem, wbuf, wsem, zbuf, zsem, e_lab, e_blk, s_lab, s_blk, r_lab, r_blk, o_t)
     for _ in second:
         pass
 
@@ -782,8 +779,7 @@
             out_specs=(any_spec(),) + (vmem_spec(),) * 5 + (any_spec(),),
             scratch_shapes=[pltpu.VMEM((8, LANES), F32)] + run_scratch + h_scratch + w_scratch(2) + z_scratch(2) + [
                 pltpu.VMEM((n_blk, n_lab, LANES), F32), pltpu.VMEM((n_blk, 8, LANES), F32),
-                pltpu.VMEM((frames + lat_pad, n_lab, LANES), F32), pltpu.VMEM((frames + lat_pad, n_lab + 8, LANES), F32),
-                pltpu.VMEM((frames + lat_pad, n_lab, LANES), F32), pltpu.VMEM((frames + lat_pad, n_lab + 8, LANES), F32),
+                *[pltpu.VMEM((frames + lat_pad, n, LANES), F32) for n in (n_lab, n_lab + 8) * 2],
                 pltpu.VMEM((n_blk, LANES, LANES), F32)] + z_scratch(2) + [
                 pltpu.VMEM((model_dim, rows), F32), pltpu.VMEM((rows, LANES), F32)] + g_scratch + [dma((2,))] + lists(1),
             compiler_params=params(),

time: 174 us -> 171 us (0.983)
  Pallas kernels: 149 us -> 145 us
    pallas_call x1, Pallas kernels: 77.4 us -> 74.1 us  [local_body(): kernel_call(functools.partial(mid_kernel, 0, n_tiles, n_lat, lat_steps, n...]
  transfers between devices with their start and end apart: 13 -> 13, of which waited for: 6 -> 6; matrix products, arithmetic and copies ran while one was open for 2% -> 2% of each run, Pallas kernels for 41% -> 42%
where the time goes in v3:
time: 171 us; the launch traced here: 170 us
  Pallas kernels  145 us (85%)
  starting transfers between devices  9.43 us (6%)
  waiting for transfers between devices  7.7 us (5%)
  local copies, waits for them, and re-layouts  3.85 us (2%)
  other arithmetic  3.28 us (2%)
    pallas_call x1, Pallas kernels, local_body(): kernel_call(functools.partial(mid_kernel, 0, n_tiles, n_lat, lat_steps, n...  74.1 us
    pallas_call x1, Pallas kernels, local_body(): kernel_call(functools.partial(grad_w_kernel, n_slots), out_shape=jax.Shap...  37.5 us
    pallas_call x1, Pallas kernels, local_body(): kernel_call(functools.partial(z_own_kernel, n_slots), out_shape=(z_type,...  33.7 us
    ppermute x10, waiting for transfers between devices, tp_xor(): return lax.ppermute(x, 'tp', [(i, i ^ mask) for i in range(n_tp)])  6.63 us
    ppermute x3, starting transfers between devices, swap_dp(): return lax.ppermute(x, 'dp', dp_swap)  4.91 us
    ppermute x10, starting transfers between devices, tp_xor(): return lax.ppermute(x, 'tp', [(i, i ^ mask) for i in range(n_tp)])  4.53 us
  transfers between devices with their start and end apart: 13, of which 6 were waited for; matrix products, arithmetic and copies ran while one was open for 2% of the time, Pallas kernels for 42%

profile of v3, /device:TPU:0, one launch (start us, length us, event | category | flops | bytes accessed | tf_op | source)
XLA Modules:
  0.0 170.5 jit_solution(595599372562123323)
XLA Ops:
  0.6 1.1 dynamic-slice_bitcast_fusion
  1.8 3.4 %collective-permute-start = (bf16[256,1280]{1,0:T(8,128)(2,1)S(1)}, bf16[256,1280]{1,0:T(8,128)(2,1)S(1)}, u32[]{:S(2)}, u32[]{:S(2)}) collective-permute-start(bf16[256,1280]{1,0:T(8,128)(2,1)S(1)} %dynamic-slice_bitcast_fusion), channel_id=1, source_target_pairs={{0,4},{4,0},{1,5},{5,1},{2,6},{6,2},{3,7},{7,3}} | collective-permute-start | bytes 1966088 | tf_op jit(solution)/shard_map/ppermute | solution.py:717
  5.1 33.7 %shard_map.76 = (f32[32,512,512]{2,1,0:T(8,128)}, f32[152,128]{1,0:T(8,128)}, s32[2,34]{1,0:T(2,128)}) custom-call(bf16[512,1280]{1,0:T(8,128)(2,1)} %bitcast.8, bf16[1280,16384]{1,0:T(8,128)(2,1)} %w_hbm.3, s32[2,32]{1,0:T(2,128)} %labels_ref.1, s32[2]{0:T(128)} %in_len_ref.1, s32[2]{0:T(128)} %lab_len_ref.1), custom_call_target="tpu_custom_call" | custom-call | flops 21474836480 | bytes 75497472 | tf_op jit(solution)/shard_map/pallas_call | solution.py:756
  38.9 0.5 collective-permute-start.2
  39.4 0.8 collective-permute-start.3
  40.3 0.5 collective-permute-start.4
  40.8 0.3 collective-permute-done.2.p1
  41.1 3.5 %collective-permute-done.3.p2 = f32[152,128]{1,0:T(8,128)S(1)} collective-permute-done((f32[152,128]{1,0:T(8,128)}, f32[152,128]{1,0:T(8,128)S(1)}, u32[]{:S(2)}, u32[]{:S(2)}) %collective-permute-start.3) | collective-permute-done | bytes 77856 | tf_op jit(solution)/shard_map/ppermute | solution.py:711
  44.6 0.5 collective-permute-done.4.p3
  45.2 0.5 copy-done.9
  45.8 0.2 copy-done.1
  46.0 74.1 %shard_map.77 = (f32[32,512,512]{2,1,0:T(8,128)}, f32[16,128]{1,0:T(8,128)}, f32[256,128]{1,0:T(8,128)}, f32[256,1280]{1,0:T(8,128)}, f32[256,1280]{1,0:T(8,128)...) custom-call(bf16[256,1280]{1,0:T(8,128)(2,1)} %copy-done, bf16[256,1280]{1,0:T(8,128)(2,1)} %copy-done.1, ...), custom_call_target="tpu_custom_call" | custom-call | flops 42949672960 | bytes 150994944 | tf_op jit(solution)/shard_map/pallas_call | solution.py:775
  120.2 0.5 collective-permute-start.5
  120.7 0.5 collective-permute-start.9
  121.2 1.9 %collective-permute-start.8 = (f32[16,128]{1,0:T(8,128)}, f32[16,128]{1,0:T(8,128)S(1)}, u32[]{:S(2)}, u32[]{:S(2)}) collective-permute-start(f32[16,128]{1,0:T(8,128)} %get-tuple-element.27.st0), channel_id=1, source_target_pairs={{0,3},{1,2},{2,1},{3,0},{4,7},{5,6},{6,5},{7,4}} | collective-permute-start | bytes 24584 | tf_op jit(solution)/shard_map/ppermute | solution.py:711
  123.1 0.5 collective-permute-done.5
  123.5 1.0 collective-permute-start.10
  124.6 1.5 add.11
  126.1 1.1 collective-permute-done.10.meta_ref
  127.4 0.3 copy-done.6
  128.0 37.5 %shard_map.78 = f32[640,16384]{1,0:T(8,128)} custom-call(bf16[16,512,1024]{2,1,0:T(8,128)(2,1)} %get-tuple-element.25.g_hbm, f32[32,512,512]{2,1,0:T(8,128)} %get-tuple-element.26.z_hbm, bf16[512,1280]{1,0:T(8,128)(2,1)} %bitcast.9, bf16[256,1280]{1,0:T(8,128)(2,1)} %copy-done, bf16[256,1280]{1,0:T(8,128)(2,1)} %copy-done.1, ...), custom_call_target="tpu_custom_call" | custom-call | flops 21474836480 | bytes 109051904 | tf_op jit(solution)/shard_map/pallas_call | solution.py:795
  165.8 1.2 slice_bitcast_fusion
  167.0 1.8 %collective-permute-done.12 = f32[256,1280]{1,0:T(8,128)S(1)} collective-permute-done((f32[256,1280]{1,0:T(8,128)S(1)}, f32[256,1280]{1,0:T(8,128)S(1)}, u32[]{:S(2)}, u32[]{:S(2)}) %collective-permute-start.12) | collective-permute-done | bytes 1310752 | tf_op jit(solution)/shard_map/ppermute | solution.py:711
  168.8 1.7 maximum_select_fusion
  (32 shorter events, 0.9 us)
Async XLA Ops:
  1.8 37.1 %collective-permute-start = (bf16[256,1280]{1,0:T(8,128)(2,1)S(1)}, bf16[256,1280]{1,0:T(8,128)(2,1)S(1)}, u32[]{:S(2)}, u32[]{:S(2)}) collective-permute-start(bf16[256,1280]{1,0:T(8,128)(2,1)S(1)} %dynamic-slice_bitcast_fusion), channel_id=1, source_target_pairs={{0,4},{4,0},{1,5},{5,1},{2,6},{6,2},{3,7},{7,3}} | collective-permute-start | bytes 1966088 | tf_op jit(solution)/shard_map/ppermute | solution.py:717
  38.9 6.3 %copy-start = (bf16[256,1280]{1,0:T(8,128)(2,1)}, bf16[256,1280]{1,0:T(8,128)(2,1)S(1)}, u32[]{:S(2)}) copy-start(bf16[256,1280]{1,0:T(8,128)(2,1)S(1)} %collective-permute-done.h_got) | copy-start | bytes 1966084
  38.9 6.2 %collective-permute-start.1 = (bf16[256,1280]{1,0:T(8,128)(2,1)S(1)}, bf16[256,1280]{1,0:T(8,128)(2,1)S(1)}, u32[]{:S(2)}, u32[]{:S(2)}) collective-permute-start(bf16[256,1280]{1,0:T(8,128)(2,1)S(1)} %collective-permute-done.h_got), channel_id=1, source_target_pairs={{0,1},{1,0},{2,3},{3,2},{4,5},{5,4},{6,7},{7,6}} | collective-permute-start | bytes 1966088 | tf_op jit(solution)/shard_map/ppermute | solution.py:711
  38.9 2.2 %collective-permute-start.2 = (f32[152,128]{1,0:T(8,128)}, f32[152,128]{1,0:T(8,128)S(1)}, u32[]{:S(2)}, u32[]{:S(2)}) collective-permute-start(f32[152,128]{1,0:T(8,128)} %get-tuple-element.19.p0), channel_id=1, source_target_pairs={{0,1},{1,0},{2,3},{3,2},{4,5},{5,4},{6,7},{7,6}} | collective-permute-start | bytes 233480 | tf_op jit(solution)/shard_map/ppermute | solution.py:711
  39.4 5.2 %collective-permute-start.3 = (f32[152,128]{1,0:T(8,128)}, f32[152,128]{1,0:T(8,128)S(1)}, u32[]{:S(2)}, u32[]{:S(2)}) collective-permute-start(f32[152,128]{1,0:T(8,128)} %get-tuple-element.19.p0), channel_id=1, source_target_pairs={{0,2},{1,3},{2,0},{3,1},{4,6},{5,7},{6,4},{7,5}} | collective-permute-start | bytes 233480 | tf_op jit(solution)/shard_map/ppermute | solution.py:711
  40.3 4.9 %collective-permute-start.4 = (f32[152,128]{1,0:T(8,128)}, f32[152,128]{1,0:T(8,128)S(1)}, u32[]{:S(2)}, u32[]{:S(2)}) collective-permute-start(f32[152,128]{1,0:T(8,128)} %get-tuple-element.19.p0), channel_id=1, source_target_pairs={{0,3},{1,2},{2,1},{3,0},{4,7},{5,6},{6,5},{7,4}} | collective-permute-start | bytes 233480 | tf_op jit(solution)/shard_map/ppermute | solution.py:711
  41.1 4.0 %copy-start.7 = (f32[152,128]{1,0:T(8,128)}, f32[152,128]{1,0:T(8,128)S(1)}, u32[]{:S(2)}) copy-start(f32[152,128]{1,0:T(8,128)S(1)} %collective-permute-done.2.p1) | copy-start | bytes 233476
  44.6 0.6 copy-start.8
  45.1 0.6 copy-start.9
  45.1 0.9 copy-start.1
  46.0 77.5 %copy-start.10 = (s32[2,34]{1,0:T(2,128)S(1)}, s32[2,34]{1,0:T(2,128)}, u32[]{:S(2)}) copy-start(s32[2,34]{1,0:T(2,128)} %get-tuple-element.21.meta_ref) | copy-start | bytes 820
  120.2 3.4 %collective-permute-start.5 = (f32[256,1280]{1,0:T(8,128)}, f32[256,1280]{1,0:T(8,128)S(1)}, u32[]{:S(2)}, u32[]{:S(2)}) collective-permute-start(f32[256,1280]{1,0:T(8,128)} %get-tuple-element.24), channel_id=1, source_target_pairs={{0,1},{1,0},{2,3},{3,2},{4,5},{5,4},{6,7},{7,6}} | collective-permute-start | bytes 3932168 | tf_op jit(solution)/shard_map/ppermute | solution.py:711
  120.7 6.7 %collective-permute-start.9 = (f32[256,128]{1,0:T(8,128)}, f32[256,128]{1,0:T(8,128)S(1)}, u32[]{:S(2)}, u32[]{:S(2)}) collective-permute-start(f32[256,128]{1,0:T(8,128)} %get-tuple-element.28), channel_id=1, source_target_pairs={{0,4},{4,0},{1,5},{5,1},{2,6},{6,2},{3,7},{7,3}} | collective-permute-start | bytes 393224 | tf_op jit(solution)/shard_map/ppermute | solution.py:717
  121.2 6.1 %collective-permute-start.6 = (f32[16,128]{1,0:T(8,128)}, f32[16,128]{1,0:T(8,128)S(1)}, u32[]{:S(2)}, u32[]{:S(2)}) collective-permute-start(f32[16,128]{1,0:T(8,128)} %get-tuple-element.27.st0), channel_id=1, source_target_pairs={{0,1},{1,0},{2,3},{3,2},{4,5},{5,4},{6,7},{7,6}} | collective-permute-start | bytes 24584 | tf_op jit(solution)/shard_map/ppermute | solution.py:711
  121.2 6.1 %collective-permute-start.7 = (f32[16,128]{1,0:T(8,128)}, f32[16,128]{1,0:T(8,128)S(1)}, u32[]{:S(2)}, u32[]{:S(2)}) collective-permute-start(f32[16,128]{1,0:T(8,128)} %get-tuple-element.27.st0), channel_id=1, source_target_pairs={{0,2},{1,3},{2,0},{3,1},{4,6},{5,7},{6,4},{7,5}} | collective-permute-start | bytes 24584 | tf_op jit(solution)/shard_map/ppermute | solution.py:711
  121.2 6.2 %collective-permute-start.8 = (f32[16,128]{1,0:T(8,128)}, f32[16,128]{1,0:T(8,128)S(1)}, u32[]{:S(2)}, u32[]{:S(2)}) collective-permute-start(f32[16,128]{1,0:T(8,128)} %get-tuple-element.27.st0), channel_id=1, source_target_pairs={{0,3},{1,2},{2,1},{3,0},{4,7},{5,6},{6,5},{7,4}} | collective-permute-start | bytes 24584 | tf_op jit(solution)/shard_map/ppermute | solution.py:711
  123.5 3.6 %collective-permute-start.10 = (s32[2,34]{1,0:T(2,128)S(1)}, s32[2,34]{1,0:T(2,128)S(1)}, u32[]{:S(2)}, u32[]{:S(2)}) collective-permute-start(s32[2,34]{1,0:T(2,128)S(1)} %copy-done.10), channel_id=1, source_target_pairs={{0,4},{4,0},{1,5},{5,1},{2,6},{6,2},{3,7},{7,3}} | collective-permute-start | bytes 824 | tf_op jit(solution)/shard_map/ppermute | solution.py:717
  127.1 0.6 copy-start.6
  127.1 38.5 %collective-permute-start.11 = (f32[256,1280]{1,0:T(8,128)S(1)}, f32[256,1280]{1,0:T(8,128)S(1)}, u32[]{:S(2)}, u32[]{:S(2)}) collective-permute-start(f32[256,1280]{1,0:T(8,128)S(1)} %add.11), channel_id=1, source_target_pairs={{0,2},{1,3},{2,0},{3,1},{4,6},{5,7},{6,4},{7,5}} | collective-permute-start | bytes 3932168 | tf_op jit(solution)/shard_map/ppermute | solution.py:711
  127.3 0.6 copy-start.3
  127.3 0.6 copy-start.4
  127.4 0.6 copy-start.5
  127.4 0.7 copy-start.2
  165.7 3.1 %collective-permute-start.12 = (f32[256,1280]{1,0:T(8,128)S(1)}, f32[256,1280]{1,0:T(8,128)S(1)}, u32[]{:S(2)}, u32[]{:S(2)}) collective-permute-start(f32[256,1280]{1,0:T(8,128)S(1)} %add.12), channel_id=1, source_target_pairs={{0,1},{1,0},{2,3},{3,2},{4,5},{5,4},{6,7},{7,6}} | collective-permute-start | bytes 3932168 | tf_op jit(solution)/shard_map/ppermute | solution.py:711

commit v4 on v3

--- a/solution.py
+++ b/solution.py
@@ -36,7 +36,7 @@
 
 
 def params():
-    return pltpu.CompilerParams(vmem_limit_bytes=56 * MIB)
+    return pltpu.CompilerParams(vmem_limit_bytes=59 * MIB)
 
 
 def label_col(meta_refs, i):
@@ -613,8 +613,8 @@
         pass
 
 
-def grad_w_kernel(n_slots, g_hbm, z_hbm, h_own_ref, h_got, h_core, st0, st1, st2, st3, occ_ref, meta_ref, gw_hbm,
-                  h_ref, hsem, zbuf, zsem, gsem, obuf, osem, ht, lse_ref, g0, g1, head, nxt):
+def grad_w_kernel(n_slots, g_hbm, z_hbm, h_own_hbm, h_got, h_core, st0, st1, st2, st3, occ_ref, meta_ref, gw_hbm,
+                  h_ref, hsem, h_own_ref, zbuf, zsem, gsem, obuf, osem, ht, lse_ref, g0, g1, head, nxt):
     n_tiles, rows = z_hbm.shape[0], z_hbm.shape[1]
     frames = rows // meta_ref.shape[0]
     d_loc = ht.shape[0]
@@ -626,11 +626,14 @@
         return pltpu.make_async_copy(g_hbm.at[j], g.at[0:rows, :], gsem.at[k])
 
     join = JoinRows(h_got, h_core, h_ref, hsem)
+    own_copy = pltpu.make_async_copy(h_own_hbm, h_own_ref, hsem.at[2])
+    own_copy.start()
     join.start()
     zs.prime()
     g_copy(0, g0, 0).start()
     col_start = build_lists([meta_ref], n_tiles * TILE, head, nxt)
     d0 = pl.multiple_of(lax.axis_index("dp") * d_loc, LANES)
+    own_copy.wait()
     ht[:, 0:rows] = h_own_ref[:, pl.ds(d0, d_loc)].T
     spread_lse([st0, st1, st2, st3], 0, meta_ref, lse_ref, 0, frames)
     join.wait()
@@ -659,11 +662,12 @@
         make_g(slot0, u, g0)
     patch(0, slot0, g0)
     d_half = d_loc // 2
+    n_out = obuf.shape[0]
 
     def half(j, g_now, g_next, k):
-        @pl.when(j >= 3)
+        @pl.when(j >= n_out)
         def _():
-            out_copy(j - 3).wait()
+            out_copy(j - n_out).wait()
 
         nj = lax.min(j + 1, n_groups - 1)
 
@@ -691,7 +695,7 @@
         return c
 
     lax.fori_loop(0, n_groups // 2, step, 0)
-    for j in range(n_groups - 3, n_groups):
+    for j in range(n_groups - n_out, n_groups):
         out_copy(j).wait()
 
 
@@ -726,6 +730,7 @@
         d_loc = model_dim // n_dp
         dma = pltpu.SemaphoreType.DMA
         i32 = jnp.int32
+        out_slots = 4
         n_lat, lat_steps, lat_pad = 24, 22, 8
         h_own = hidden.reshape(rows, model_dim)
         core = lax.rem(lax.axis_index("tp"), 2)
@@ -741,13 +746,13 @@
         stat_type = jax.ShapeDtypeStruct((16, LANES), F32)
         g_scratch = [pltpu.VMEM((rows, 2 * TILE), BF16)] * 2
 
-        def w_scratch(n):
-            return [pltpu.VMEM((3, model_dim, n * TILE), BF16), dma((3,))]
-
-        def z_scratch(n):
-            return [pltpu.VMEM((3, n, rows, TILE), F32), dma((3,))]
-
-        h_scratch = [pltpu.VMEM((rows, model_dim), BF16), dma((2,))]
+        def w_scratch(n, slots):
+            return [pltpu.VMEM((slots, model_dim, n * TILE), BF16), dma((slots,))]
+
+        def z_scratch(n, slots=3):
+            return [pltpu.VMEM((slots, n, rows, TILE), F32), dma((slots,))]
+
+        h_scratch = [pltpu.VMEM((rows, model_dim), BF16), dma((3,))]
         run_scratch = [pltpu.VMEM((rows, LANES), F32), pltpu.VMEM((rows, LANES), F32)]
 
         def lists(n_sets):
@@ -758,7 +763,7 @@
             out_shape=(z_type, pick_type, meta_type),
             in_specs=[any_spec(), any_spec(), smem_spec(), smem_spec(), smem_spec()],
             out_specs=(any_spec(), vmem_spec(), smem_spec()),
-            scratch_shapes=h_scratch + w_scratch(4) + z_scratch(4) + run_scratch + [pltpu.VMEM((frames // 2, LANES), F32)] + lists(1),
+            scratch_shapes=h_scratch + w_scratch(4, 4) + z_scratch(4) + run_scratch + [pltpu.VMEM((frames // 2, LANES), F32)] + lists(1),
             compiler_params=params(),
             cost_estimate=cost(n_tiles * flops, n_tiles * (wbytes + zbytes)),
         )(in_hbm(h_own), w_loc, labels, in_len, lab_len)
@@ -777,10 +782,10 @@
             out_shape=(z_type, stat_type, occ_type, half_type, half_type, loss_type, g_type),
             in_specs=[any_spec()] * 3 + [vmem_spec()] * 4 + [any_spec(), smem_spec()],
             out_specs=(any_spec(),) + (vmem_spec(),) * 5 + (any_spec(),),
-            scratch_shapes=[pltpu.VMEM((8, LANES), F32)] + run_scratch + h_scratch + w_scratch(2) + z_scratch(2) + [
+            scratch_shapes=[pltpu.VMEM((8, LANES), F32)] + run_scratch + h_scratch + w_scratch(2, 5) + z_scratch(2) + [
                 pltpu.VMEM((n_blk, n_lab, LANES), F32), pltpu.VMEM((n_blk, 8, LANES), F32),
                 *[pltpu.VMEM((frames + lat_pad, n, LANES), F32) for n in (n_lab, n_lab + 8) * 2],
-                pltpu.VMEM((n_blk, LANES, LANES), F32)] + z_scratch(2) + [
+                pltpu.VMEM((n_blk, LANES, LANES), F32)] + z_scratch(2, 4) + [
                 pltpu.VMEM((model_dim, rows), F32), pltpu.VMEM((rows, LANES), F32)] + g_scratch + [dma((2,))] + lists(1),
             compiler_params=params(),
             cost_estimate=cost((2 * n_tiles) * flops, (2 * n_tiles) * (wbytes + zbytes)),
@@ -795,15 +800,15 @@
         grad_weight = kernel_call(
             functools.partial(grad_w_kernel, n_slots),
             out_shape=jax.ShapeDtypeStruct((d_loc, vocab_loc), F32),
-            in_specs=[any_spec(), any_spec(), vmem_spec(), any_spec(), any_spec()] + [vmem_spec()] * 5 + [smem_spec()],
+            in_specs=[any_spec()] * 5 + [vmem_spec()] * 5 + [smem_spec()],
             out_specs=any_spec(),
-            scratch_shapes=h_scratch + z_scratch(2) + [
-                dma((2,)), pltpu.VMEM((3, d_loc, 2 * TILE), F32), dma((3,)),
+            scratch_shapes=h_scratch + [h_scratch[0]] + z_scratch(2, 5) + [
+                dma((2,)), pltpu.VMEM((out_slots, d_loc, 2 * TILE), F32), dma((out_slots,)),
                 pltpu.VMEM((d_loc, 2 * rows), BF16), pltpu.VMEM((rows, LANES), F32),
                 pltpu.VMEM((2 * rows, 2 * TILE), BF16), pltpu.VMEM((2 * rows, 2 * TILE), BF16)] + lists(1),
             compiler_params=params(),
             cost_estimate=cost(n_tiles * flops, n_tiles * (2 * zbytes + d_loc * TILE * 4)),
-        )(g_own, z_oth, h_own, h_got, h_core, *st_oth, occ_oth, meta_oth)
+        )(g_own, z_oth, in_hbm(h_own), h_got, h_core, *st_oth, occ_oth, meta_oth)
 
         chip_sum, grad_weight = lax.optimization_barrier((chip_sum, grad_weight))
         full_half = chip_sum + across

time: 171 us -> 174 us (1.018)
  Pallas kernels: 145 us -> 149 us
    pallas_call x1, Pallas kernels: 74.1 us -> 76.2 us  [local_body(): kernel_call(functools.partial(mid_kernel, 0, n_tiles, n_lat, lat_steps, n...]
where the time goes in v4:
time: 174 us
  Pallas kernels  149 us (86%)
  starting transfers between devices  9.39 us (5%)
  waiting for transfers between devices  7.7 us (4%)
  local copies, waits for them, and re-layouts  3.85 us (2%)
  other arithmetic  3.28 us (2%)
    pallas_call x1, Pallas kernels, local_body(): kernel_call(functools.partial(mid_kernel, 0, n_tiles, n_lat, lat_steps, n...  76.2 us
    pallas_call x1, Pallas kernels, local_body(): kernel_call(functools.partial(grad_w_kernel, n_slots), out_shape=jax.Shap...  38.6 us
    pallas_call x1, Pallas kernels, local_body(): kernel_call(functools.partial(z_own_kernel, n_slots), out_shape=(z_type,...  33.7 us
    ppermute x10, waiting for transfers between devices, tp_xor(): return lax.ppermute(x, 'tp', [(i, i ^ mask) for i in range(n_tp)])  6.63 us
    ppermute x3, starting transfers between devices, swap_dp(): return lax.ppermute(x, 'dp', dp_swap)  4.91 us
    ppermute x10, starting transfers between devices, tp_xor(): return lax.ppermute(x, 'tp', [(i, i ^ mask) for i in range(n_tp)])  4.48 us
  transfers between devices with their start and end apart: 13, of which 6 were waited for; matrix products, arithmetic and copies ran while one was open for 2% of the time, Pallas kernels for 42%

profile of v4, /device:TPU:0, one launch (start us, length us, event | category | flops | bytes accessed | tf_op | source)
XLA Modules:
  0.0 173.5 jit_solution(17610868649693642942)
XLA Ops:
  0.6 1.1 dynamic-slice_bitcast_fusion
  1.8 3.4 %collective-permute-start = (bf16[256,1280]{1,0:T(8,128)(2,1)S(1)}, bf16[256,1280]{1,0:T(8,128)(2,1)S(1)}, u32[]{:S(2)}, u32[]{:S(2)}) collective-permute-start(bf16[256,1280]{1,0:T(8,128)(2,1)S(1)} %dynamic-slice_bitcast_fusion), channel_id=1, source_target_pairs={{0,4},{4,0},{1,5},{5,1},{2,6},{6,2},{3,7},{7,3}} | collective-permute-start | bytes 1966088 | tf_op jit(solution)/shard_map/ppermute | solution.py:721
  5.1 33.7 %shard_map.76 = (f32[32,512,512]{2,1,0:T(8,128)}, f32[152,128]{1,0:T(8,128)}, s32[2,34]{1,0:T(2,128)}) custom-call(bf16[512,1280]{1,0:T(8,128)(2,1)} %bitcast.8, bf16[1280,16384]{1,0:T(8,128)(2,1)} %w_hbm.3, s32[2,32]{1,0:T(2,128)} %labels_ref.1, s32[2]{0:T(128)} %in_len_ref.1, s32[2]{0:T(128)} %lab_len_ref.1), custom_call_target="tpu_custom_call" | custom-call | flops 21474836480 | bytes 75497472 | tf_op jit(solution)/shard_map/pallas_call | solution.py:761
  38.9 0.5 collective-permute-start.2
  39.4 0.8 collective-permute-start.3
  40.3 0.5 collective-permute-start.4
  40.8 0.3 collective-permute-done.2.p1
  41.1 3.5 %collective-permute-done.3.p2 = f32[152,128]{1,0:T(8,128)S(1)} collective-permute-done((f32[152,128]{1,0:T(8,128)}, f32[152,128]{1,0:T(8,128)S(1)}, u32[]{:S(2)}, u32[]{:S(2)}) %collective-permute-start.3) | collective-permute-done | bytes 77856 | tf_op jit(solution)/shard_map/ppermute | solution.py:715
  44.6 0.5 collective-permute-done.4.p3
  45.2 0.6 copy-done.9
  45.8 0.2 copy-done.1
  46.0 76.2 %shard_map.77 = (f32[32,512,512]{2,1,0:T(8,128)}, f32[16,128]{1,0:T(8,128)}, f32[256,128]{1,0:T(8,128)}, f32[256,1280]{1,0:T(8,128)}, f32[256,1280]{1,0:T(8,128)...) custom-call(bf16[256,1280]{1,0:T(8,128)(2,1)} %copy-done, bf16[256,1280]{1,0:T(8,128)(2,1)} %copy-done.1, ...), custom_call_target="tpu_custom_call" | custom-call | flops 42949672960 | bytes 150994944 | tf_op jit(solution)/shard_map/pallas_call | solution.py:780
  122.2 0.5 collective-permute-start.5
  122.8 0.5 collective-permute-start.9
  123.3 1.9 %collective-permute-start.8 = (f32[16,128]{1,0:T(8,128)}, f32[16,128]{1,0:T(8,128)S(1)}, u32[]{:S(2)}, u32[]{:S(2)}) collective-permute-start(f32[16,128]{1,0:T(8,128)} %get-tuple-element.27.st0), channel_id=1, source_target_pairs={{0,3},{1,2},{2,1},{3,0},{4,7},{5,6},{6,5},{7,4}} | collective-permute-start | bytes 24584 | tf_op jit(solution)/shard_map/ppermute | solution.py:715
  125.1 0.5 collective-permute-done.5
  125.6 1.0 collective-permute-start.10
  126.6 1.5 add.11
  128.1 1.1 collective-permute-done.10.meta_ref
  129.4 0.3 copy-done.6
  130.1 38.6 %shard_map.78 = f32[640,16384]{1,0:T(8,128)} custom-call(bf16[16,512,1024]{2,1,0:T(8,128)(2,1)} %get-tuple-element.25.g_hbm, f32[32,512,512]{2,1,0:T(8,128)} %get-tuple-element.26.z_hbm, bf16[512,1280]{1,0:T(8,128)(2,1)} %bitcast.9, bf16[256,1280]{1,0:T(8,128)(2,1)} %copy-done, bf16[256,1280]{1,0:T(8,128)(2,1)} %copy-done.1, ...), custom_call_target="tpu_custom_call" | custom-call | flops 21474836480 | bytes 109051904 | tf_op jit(solution)/shard_map/pallas_call | solution.py:800
  168.9 1.2 slice_bitcast_fusion
  170.1 1.8 %collective-permute-done.12 = f32[256,1280]{1,0:T(8,128)S(1)} collective-permute-done((f32[256,1280]{1,0:T(8,128)S(1)}, f32[256,1280]{1,0:T(8,128)S(1)}, u32[]{:S(2)}, u32[]{:S(2)}) %collective-permute-start.12) | collective-permute-done | bytes 1310752 | tf_op jit(solution)/shard_map/ppermute | solution.py:715
  171.9 1.7 maximum_select_fusion
  (32 shorter events, 0.8 us)
Async XLA Ops:
  1.8 37.1 %collective-permute-start = (bf16[256,1280]{1,0:T(8,128)(2,1)S(1)}, bf16[256,1280]{1,0:T(8,128)(2,1)S(1)}, u32[]{:S(2)}, u32[]{:S(2)}) collective-permute-start(bf16[256,1280]{1,0:T(8,128)(2,1)S(1)} %dynamic-slice_bitcast_fusion), channel_id=1, source_target_pairs={{0,4},{4,0},{1,5},{5,1},{2,6},{6,2},{3,7},{7,3}} | collective-permute-start | bytes 1966088 | tf_op jit(solution)/shard_map/ppermute | solution.py:721
  38.9 6.3 %copy-start = (bf16[256,1280]{1,0:T(8,128)(2,1)}, bf16[256,1280]{1,0:T(8,128)(2,1)S(1)}, u32[]{:S(2)}) copy-start(bf16[256,1280]{1,0:T(8,128)(2,1)S(1)} %collective-permute-done.h_got) | copy-start | bytes 1966084
  38.9 6.2 %collective-permute-start.1 = (bf16[256,1280]{1,0:T(8,128)(2,1)S(1)}, bf16[256,1280]{1,0:T(8,128)(2,1)S(1)}, u32[]{:S(2)}, u32[]{:S(2)}) collective-permute-start(bf16[256,1280]{1,0:T(8,128)(2,1)S(1)} %collective-permute-done.h_got), channel_id=1, source_target_pairs={{0,1},{1,0},{2,3},{3,2},{4,5},{5,4},{6,7},{7,6}} | collective-permute-start | bytes 1966088 | tf_op jit(solution)/shard_map/ppermute | solution.py:715
  38.9 2.2 %collective-permute-start.2 = (f32[152,128]{1,0:T(8,128)}, f32[152,128]{1,0:T(8,128)S(1)}, u32[]{:S(2)}, u32[]{:S(2)}) collective-permute-start(f32[152,128]{1,0:T(8,128)} %get-tuple-element.19.p0), channel_id=1, source_target_pairs={{0,1},{1,0},{2,3},{3,2},{4,5},{5,4},{6,7},{7,6}} | collective-permute-start | bytes 233480 | tf_op jit(solution)/shard_map/ppermute | solution.py:715
  39.4 5.2 %collective-permute-start.3 = (f32[152,128]{1,0:T(8,128)}, f32[152,128]{1,0:T(8,128)S(1)}, u32[]{:S(2)}, u32[]{:S(2)}) collective-permute-start(f32[152,128]{1,0:T(8,128)} %get-tuple-element.19.p0), channel_id=1, source_target_pairs={{0,2},{1,3},{2,0},{3,1},{4,6},{5,7},{6,4},{7,5}} | collective-permute-start | bytes 233480 | tf_op jit(solution)/shard_map/ppermute | solution.py:715
  40.3 4.9 %collective-permute-start.4 = (f32[152,128]{1,0:T(8,128)}, f32[152,128]{1,0:T(8,128)S(1)}, u32[]{:S(2)}, u32[]{:S(2)}) collective-permute-start(f32[152,128]{1,0:T(8,128)} %get-tuple-element.19.p0), channel_id=1, source_target_pairs={{0,3},{1,2},{2,1},{3,0},{4,7},{5,6},{6,5},{7,4}} | collective-permute-start | bytes 233480 | tf_op jit(solution)/shard_map/ppermute | solution.py:715
  41.1 4.0 %copy-start.7 = (f32[152,128]{1,0:T(8,128)}, f32[152,128]{1,0:T(8,128)S(1)}, u32[]{:S(2)}) copy-start(f32[152,128]{1,0:T(8,128)S(1)} %collective-permute-done.2.p1) | copy-start | bytes 233476
  44.6 0.6 copy-start.8
  45.1 0.6 copy-start.9
  45.2 0.9 copy-start.1
  46.0 79.6 %copy-start.10 = (s32[2,34]{1,0:T(2,128)S(1)}, s32[2,34]{1,0:T(2,128)}, u32[]{:S(2)}) copy-start(s32[2,34]{1,0:T(2,128)} %get-tuple-element.21.meta_ref) | copy-start | bytes 820
  122.2 3.4 %collective-permute-start.5 = (f32[256,1280]{1,0:T(8,128)}, f32[256,1280]{1,0:T(8,128)S(1)}, u32[]{:S(2)}, u32[]{:S(2)}) collective-permute-start(f32[256,1280]{1,0:T(8,128)} %get-tuple-element.24), channel_id=1, source_target_pairs={{0,1},{1,0},{2,3},{3,2},{4,5},{5,4},{6,7},{7,6}} | collective-permute-start | bytes 3932168 | tf_op jit(solution)/shard_map/ppermute | solution.py:715
  122.8 6.7 %collective-permute-start.9 = (f32[256,128]{1,0:T(8,128)}, f32[256,128]{1,0:T(8,128)S(1)}, u32[]{:S(2)}, u32[]{:S(2)}) collective-permute-start(f32[256,128]{1,0:T(8,128)} %get-tuple-element.28), channel_id=1, source_target_pairs={{0,4},{4,0},{1,5},{5,1},{2,6},{6,2},{3,7},{7,3}} | collective-permute-start | bytes 393224 | tf_op jit(solution)/shard_map/ppermute | solution.py:721
  123.3 6.1 %collective-permute-start.6 = (f32[16,128]{1,0:T(8,128)}, f32[16,128]{1,0:T(8,128)S(1)}, u32[]{:S(2)}, u32[]{:S(2)}) collective-permute-start(f32[16,128]{1,0:T(8,128)} %get-tuple-element.27.st0), channel_id=1, source_target_pairs={{0,1},{1,0},{2,3},{3,2},{4,5},{5,4},{6,7},{7,6}} | collective-permute-start | bytes 24584 | tf_op jit(solution)/shard_map/ppermute | solution.py:715
  123.3 6.1 %collective-permute-start.7 = (f32[16,128]{1,0:T(8,128)}, f32[16,128]{1,0:T(8,128)S(1)}, u32[]{:S(2)}, u32[]{:S(2)}) collective-permute-start(f32[16,128]{1,0:T(8,128)} %get-tuple-element.27.st0), channel_id=1, source_target_pairs={{0,2},{1,3},{2,0},{3,1},{4,6},{5,7},{6,4},{7,5}} | collective-permute-start | bytes 24584 | tf_op jit(solution)/shard_map/ppermute | solution.py:715
  123.3 6.1 %collective-permute-start.8 = (f32[16,128]{1,0:T(8,128)}, f32[16,128]{1,0:T(8,128)S(1)}, u32[]{:S(2)}, u32[]{:S(2)}) collective-permute-start(f32[16,128]{1,0:T(8,128)} %get-tuple-element.27.st0), channel_id=1, source_target_pairs={{0,3},{1,2},{2,1},{3,0},{4,7},{5,6},{6,5},{7,4}} | collective-permute-start | bytes 24584 | tf_op jit(solution)/shard_map/ppermute | solution.py:715
  125.6 3.6 %collective-permute-start.10 = (s32[2,34]{1,0:T(2,128)S(1)}, s32[2,34]{1,0:T(2,128)S(1)}, u32[]{:S(2)}, u32[]{:S(2)}) collective-permute-start(s32[2,34]{1,0:T(2,128)S(1)} %copy-done.10), channel_id=1, source_target_pairs={{0,4},{4,0},{1,5},{5,1},{2,6},{6,2},{3,7},{7,3}} | collective-permute-start | bytes 824 | tf_op jit(solution)/shard_map/ppermute | solution.py:721
  129.2 0.6 copy-start.6
  129.2 39.5 %collective-permute-start.11 = (f32[256,1280]{1,0:T(8,128)S(1)}, f32[256,1280]{1,0:T(8,128)S(1)}, u32[]{:S(2)}, u32[]{:S(2)}) collective-permute-start(f32[256,1280]{1,0:T(8,128)S(1)} %add.11), channel_id=1, source_target_pairs={{0,2},{1,3},{2,0},{3,1},{4,6},{5,7},{6,4},{7,5}} | collective-permute-start | bytes 3932168 | tf_op jit(solution)/shard_map/ppermute | solution.py:715
  129.4 0.6 copy-start.3
  129.4 0.6 copy-start.4
  129.4 0.6 copy-start.5
  129.4 0.7 copy-start.2
  168.8 3.1 %collective-permute-start.12 = (f32[256,1280]{1,0:T(8,128)S(1)}, f32[256,1280]{1,0:T(8,128)S(1)}, u32[]{:S(2)}, u32[]{:S(2)}) collective-permute-start(f32[256,1280]{1,0:T(8,128)S(1)} %add.12), channel_id=1, source_target_pairs={{0,1},{1,0},{2,3},{3,2},{4,5},{5,4},{6,7},{7,6}} | collective-permute-start | bytes 3932168 | tf_op jit(solution)/shard_map/ppermute | solution.py:715

commit v5 on v3

--- a/solution.py
+++ b/solution.py
@@ -280,26 +280,10 @@
         out_copy(j).wait()
 
 
-class JoinRows:
-    def __init__(self, h_got, h_core, h_ref, hsem):
-        n = h_got.shape[0]
-        core = lax.rem(lax.axis_index("tp"), 2)
-        self.copies = [pltpu.make_async_copy(src, h_ref.at[pl.ds(pl.multiple_of(at * n, n), n), :], hsem.at[k])
-                       for k, (src, at) in enumerate(((h_got, core), (h_core, 1 - core)))]
-
-    def start(self):
-        for c in self.copies:
-            c.start()
-
-    def wait(self):
-        for c in self.copies:
-            c.wait()
-
-
-def z_lattice_part(lo, hi, n_lat, per_group, n_lab, before_tail, h_got, h_core, w_hbm, p0, p1, p2, p3, meta_ref,
+def z_lattice_part(lo, hi, n_lat, per_group, n_lab, before_tail, h_oth, w_hbm, p0, p1, p2, p3, meta_ref,
                      z_hbm, stats_ref, occ_ref, loss_ref, m_ref, s_ref,
                      h_ref, hsem, wbuf, wsem, zbuf, zsem, e_lab, e_blk, s_lab, s_blk, r_lab, r_blk, o_t):
-    join = JoinRows(h_got, h_core, h_ref, hsem)
+    join = pltpu.make_async_copy(h_oth, h_ref, hsem.at[0])
     join.start()
     n_blk = e_lab.shape[0]
     frames = n_blk * HALF
@@ -505,11 +489,12 @@
     c0 = pl.multiple_of(blk * LANES, LANES)
     zb = z_block(seq, c0)
     slot_lane = jnp.where(item == 0, n_slots - 1, item - 1) + HALF * seq
-    occ = jnp.sum(jnp.where(lane == slot_lane, occ_ref[...], 0.0), **ALONG)
+    at = off - blk * LANES
+    occ = pltpu.roll(occ_ref[...], lax.rem(at - slot_lane + LANES, LANES), 1)
     fresh = jnp.exp(zb - lse_ref[pl.ds(r0, frames), :]) - occ
     gc = pl.multiple_of(g_col + c0, LANES)
     old = g_ref[pl.ds(r0, frames), pl.ds(gc, LANES)].astype(F32)
-    g_ref[pl.ds(r0, frames), pl.ds(gc, LANES)] = jnp.where(lane == off - blk * LANES, fresh, old).astype(BF16)
+    g_ref[pl.ds(r0, frames), pl.ds(gc, LANES)] = jnp.where(lane == at, fresh, old).astype(BF16)
 
 
 def softmax_unit(z, z_row, lse_ref, out, r0, n, c0):
@@ -599,22 +584,22 @@
     send_ref[...] = acc[:, pl.ds(pl.multiple_of((1 - core) * n, n), n)].T
 
 
-def mid_kernel(lo, hi, n_lat, per_group, n_lab, h_got, h_core, w_hbm, p0, p1, p2, p3, z_own, meta_ref,
+def mid_kernel(lo, hi, n_lat, per_group, n_lab, h_oth, w_hbm, p0, p1, p2, p3, z_own, meta_ref,
                z_hbm, stats_ref, occ_ref, keep_ref, send_ref, loss_ref, g_hbm,
                part_loss, m_ref, s_ref, h_ref, hsem, wbuf, wsem, zbuf, zsem, e_lab, e_blk, s_lab, s_blk, r_lab, r_blk, o_t,
                zin_buf, zin_sem, acc, lse_ref, g0, g1, gsem, head, nxt):
     second = grad_h_part(n_lab + 1, z_own, w_hbm, p0, p1, p2, p3, occ_ref, part_loss, meta_ref, keep_ref, send_ref, loss_ref, g_hbm,
                          wbuf, wsem, zin_buf, zin_sem, acc, lse_ref, g0, g1, gsem, head, nxt)
     prime_w = next(second)
-    z_lattice_part(lo, hi, n_lat, per_group, n_lab, prime_w, h_got, h_core, w_hbm, p0, p1, p2, p3, meta_ref,
+    z_lattice_part(lo, hi, n_lat, per_group, n_lab, prime_w, h_oth, w_hbm, p0, p1, p2, p3, meta_ref,
                    z_hbm, stats_ref, occ_ref, part_loss, m_ref, s_ref,
                    h_ref, hsem, wbuf, wsem, zbuf, zsem, e_lab, e_blk, s_lab, s_blk, r_lab, r_blk, o_t)
     for _ in second:
         pass
 
 
-def grad_w_kernel(n_slots, g_hbm, z_hbm, h_own_ref, h_got, h_core, st0, st1, st2, st3, occ_ref, meta_ref, gw_hbm,
-                  h_ref, hsem, zbuf, zsem, gsem, obuf, osem, ht, lse_ref, g0, g1, head, nxt):
+def grad_w_kernel(n_slots, g_hbm, z_hbm, h_own_hbm, h_oth, st0, st1, st2, st3, occ_ref, meta_ref, gw_hbm,
+                  h_ref, hsem, h_own_ref, zbuf, zsem, gsem, obuf, osem, ht, lse_ref, g0, g1, head, nxt):
     n_tiles, rows = z_hbm.shape[0], z_hbm.shape[1]
     frames = rows // meta_ref.shape[0]
     d_loc = ht.shape[0]
@@ -625,12 +610,15 @@
     def g_copy(j, g, k):
         return pltpu.make_async_copy(g_hbm.at[j], g.at[0:rows, :], gsem.at[k])
 
-    join = JoinRows(h_got, h_core, h_ref, hsem)
+    join = pltpu.make_async_copy(h_oth, h_ref, hsem.at[0])
+    own_copy = pltpu.make_async_copy(h_own_hbm, h_own_ref, hsem.at[1])
+    own_copy.start()
     join.start()
     zs.prime()
     g_copy(0, g0, 0).start()
     col_start = build_lists([meta_ref], n_tiles * TILE, head, nxt)
     d0 = pl.multiple_of(lax.axis_index("dp") * d_loc, LANES)
+    own_copy.wait()
     ht[:, 0:rows] = h_own_ref[:, pl.ds(d0, d_loc)].T
     spread_lse([st0, st1, st2, st3], 0, meta_ref, lse_ref, 0, frames)
     join.wait()
@@ -729,8 +717,7 @@
         n_lat, lat_steps, lat_pad = 24, 22, 8
         h_own = hidden.reshape(rows, model_dim)
         core = lax.rem(lax.axis_index("tp"), 2)
-        h_half = lax.dynamic_index_in_dim(h_own.reshape(2, rows // 2, model_dim), core, 0, keepdims=False)
-        h_got = swap_dp(h_half)
+        h_oth = swap_dp(h_own)
         flops = 2 * rows * model_dim * TILE
         wbytes = model_dim * TILE * 2
         zbytes = rows * TILE * 4
@@ -763,9 +750,7 @@
             cost_estimate=cost(n_tiles * flops, n_tiles * (wbytes + zbytes)),
         )(in_hbm(h_own), w_loc, labels, in_len, lab_len)
 
-        h_got, pick = lax.optimization_barrier((h_got, pick))
-        h_core = in_hbm(tp_xor(h_got, 1))
-        h_got = in_hbm(h_got)
+        h_oth = in_hbm(h_oth)
         picks = [pick] + [tp_xor(pick, k) for k in others]
 
         n_blk = frames // HALF
@@ -775,7 +760,7 @@
         z_oth, stats_oth, occ, keep, send, loss, g_own = kernel_call(
             functools.partial(mid_kernel, 0, n_tiles, n_lat, lat_steps, n_lab),
             out_shape=(z_type, stat_type, occ_type, half_type, half_type, loss_type, g_type),
-            in_specs=[any_spec()] * 3 + [vmem_spec()] * 4 + [any_spec(), smem_spec()],
+            in_specs=[any_spec()] * 2 + [vmem_spec()] * 4 + [any_spec(), smem_spec()],
             out_specs=(any_spec(),) + (vmem_spec(),) * 5 + (any_spec(),),
             scratch_shapes=[pltpu.VMEM((8, LANES), F32)] + run_scratch + h_scratch + w_scratch(2) + z_scratch(2) + [
                 pltpu.VMEM((n_blk, n_lab, LANES), F32), pltpu.VMEM((n_blk, 8, LANES), F32),
@@ -784,7 +769,7 @@
                 pltpu.VMEM((model_dim, rows), F32), pltpu.VMEM((rows, LANES), F32)] + g_scratch + [dma((2,))] + lists(1),
             compiler_params=params(),
             cost_estimate=cost((2 * n_tiles) * flops, (2 * n_tiles) * (wbytes + zbytes)),
-        )(h_got, h_core, w_loc, *picks, z_own, meta)
+        )(h_oth, w_loc, *picks, z_own, meta)
         st_oth = [stats_oth] + [tp_xor(stats_oth, k) for k in others]
         occ_oth = swap_dp(occ)
         meta_oth = swap_dp(meta)
@@ -795,15 +780,15 @@
         grad_weight = kernel_call(
             functools.partial(grad_w_kernel, n_slots),
             out_shape=jax.ShapeDtypeStruct((d_loc, vocab_loc), F32),
-            in_specs=[any_spec(), any_spec(), vmem_spec(), any_spec(), any_spec()] + [vmem_spec()] * 5 + [smem_spec()],
+            in_specs=[any_spec(), any_spec(), any_spec(), any_spec()] + [vmem_spec()] * 5 + [smem_spec()],
             out_specs=any_spec(),
-            scratch_shapes=h_scratch + z_scratch(2) + [
+            scratch_shapes=h_scratch + h_scratch[:1] + z_scratch(2) + [
                 dma((2,)), pltpu.VMEM((3, d_loc, 2 * TILE), F32), dma((3,)),
                 pltpu.VMEM((d_loc, 2 * rows), BF16), pltpu.VMEM((rows, LANES), F32),
                 pltpu.VMEM((2 * rows, 2 * TILE), BF16), pltpu.VMEM((2 * rows, 2 * TILE), BF16)] + lists(1),
             compiler_params=params(),
             cost_estimate=cost(n_tiles * flops, n_tiles * (2 * zbytes + d_loc * TILE * 4)),
-        )(g_own, z_oth, h_own, h_got, h_core, *st_oth, occ_oth, meta_oth)
+        )(g_own, z_oth, in_hbm(h_own), h_oth, *st_oth, occ_oth, meta_oth)
 
         chip_sum, grad_weight = lax.optimization_barrier((chip_sum, grad_weight))
         full_half = chip_sum + across

time: 171 us -> 169 us (0.988)
    ppermute x10 -> x9, starting transfers between devices: 4.53 us -> 4.28 us  [tp_xor(): return lax.ppermute(x, 'tp', [(i, i ^ mask) for i in range(n_tp)])]
    ppermute x10 -> x9, waiting for transfers between devices: 6.63 us -> 6.58 us  [tp_xor(): return lax.ppermute(x, 'tp', [(i, i ^ mask) for i in range(n_tp)])]
  transfers between devices with their start and end apart: 13 -> 12, of which waited for: 6 -> 5; matrix products, arithmetic and copies ran while one was open for 2% -> 2% of each run, Pallas kernels for 42% -> 42%
where the time goes in v5:
time: 169 us
  Pallas kernels  145 us (86%)
  starting transfers between devices  9.22 us (5%)
  waiting for transfers between devices  7.65 us (5%)
  other arithmetic  3.28 us (2%)
  local copies, waits for them, and re-layouts  2.9 us (2%)
    pallas_call x1, Pallas kernels, local_body(): kernel_call(functools.partial(mid_kernel, 0, n_tiles, n_lat, lat_steps, n...  74.4 us
    pallas_call x1, Pallas kernels, local_body(): kernel_call(functools.partial(grad_w_kernel, n_slots), out_shape=jax.Shap...  37 us
    pallas_call x1, Pallas kernels, local_body(): kernel_call(functools.partial(z_own_kernel, n_slots), out_shape=(z_type,...  33.7 us
    ppermute x9, waiting for transfers between devices, tp_xor(): return lax.ppermute(x, 'tp', [(i, i ^ mask) for i in range(n_tp)])  6.58 us
    ppermute x3, starting transfers between devices, swap_dp(): return lax.ppermute(x, 'dp', dp_swap)  4.94 us
    ppermute x9, starting transfers between devices, tp_xor(): return lax.ppermute(x, 'tp', [(i, i ^ mask) for i in range(n_tp)])  4.28 us
  transfers between devices with their start and end apart: 12, of which 5 were waited for; matrix products, arithmetic and copies ran while one was open for 2% of the time, Pallas kernels for 42%

profile of v5, /device:TPU:0, one launch (start us, length us, event | category | flops | bytes accessed | tf_op | source)
XLA Modules:
  0.0 169.0 jit_solution(4631869292991993883)
XLA Ops:
  0.6 3.4 %collective-permute-start = (bf16[512,1280]{1,0:T(8,128)(2,1)}, bf16[512,1280]{1,0:T(8,128)(2,1)S(1)}, u32[]{:S(2)}, u32[]{:S(2)}) collective-permute-start(bf16[512,1280]{1,0:T(8,128)(2,1)} %bitcast.7), channel_id=1, source_target_pairs={{0,4},{4,0},{1,5},{5,1},{2,6},{6,2},{3,7},{7,3}} | collective-permute-start | bytes 3932168 | tf_op jit(solution)/shard_map/ppermute | solution.py:705
  4.0 33.7 %shard_map.76 = (f32[32,512,512]{2,1,0:T(8,128)}, f32[152,128]{1,0:T(8,128)}, s32[2,34]{1,0:T(2,128)}) custom-call(bf16[512,1280]{1,0:T(8,128)(2,1)} %bitcast.8, bf16[1280,16384]{1,0:T(8,128)(2,1)} %w_hbm.3, s32[2,32]{1,0:T(2,128)} %labels_ref.1, s32[2]{0:T(128)} %in_len_ref.1, s32[2]{0:T(128)} %lab_len_ref.1), custom_call_target="tpu_custom_call" | custom-call | flops 21474836480 | bytes 75497472 | tf_op jit(solution)/shard_map/pallas_call | solution.py:743
  37.8 0.9 collective-permute-start.2
  38.6 1.0 collective-permute-start.3
  39.6 3.6 %collective-permute-done.2.p2 = f32[152,128]{1,0:T(8,128)S(1)} collective-permute-done((f32[152,128]{1,0:T(8,128)}, f32[152,128]{1,0:T(8,128)S(1)}, u32[]{:S(2)}, u32[]{:S(2)}) %collective-permute-start.2) | collective-permute-done | bytes 77856 | tf_op jit(solution)/shard_map/ppermute | solution.py:699
  43.2 0.7 collective-permute-done.3.p3
  43.9 0.6 copy-done.8
  44.5 0.5 copy-done
  45.0 74.4 %shard_map.77 = (f32[32,512,512]{2,1,0:T(8,128)}, f32[16,128]{1,0:T(8,128)}, f32[256,128]{1,0:T(8,128)}, f32[256,1280]{1,0:T(8,128)}, f32[256,1280]{1,0:T(8,128)...) custom-call(bf16[512,1280]{1,0:T(8,128)(2,1)} %copy-done, bf16[1280,16384]{1,0:T(8,128)(2,1)} %w_hbm.3, ...), custom_call_target="tpu_custom_call" | custom-call | flops 42949672960 | bytes 150994944 | tf_op jit(solution)/shard_map/pallas_call | solution.py:760
  119.4 0.4 collective-permute-start.4
  119.9 0.6 collective-permute-start.8
  120.4 1.9 %collective-permute-start.7 = (f32[16,128]{1,0:T(8,128)}, f32[16,128]{1,0:T(8,128)S(1)}, u32[]{:S(2)}, u32[]{:S(2)}) collective-permute-start(f32[16,128]{1,0:T(8,128)} %get-tuple-element.23.st0), channel_id=1, source_target_pairs={{0,3},{1,2},{2,1},{3,0},{4,7},{5,6},{6,5},{7,4}} | collective-permute-start | bytes 24584 | tf_op jit(solution)/shard_map/ppermute | solution.py:699
  122.3 0.4 collective-permute-done.4
  122.7 1.0 collective-permute-start.9
  123.8 1.5 add.6
  125.2 1.1 collective-permute-done.9.meta_ref
  126.3 0.1 collective-permute-start.10
  126.5 0.4 copy-done.5
  126.8 0.1 copy-done.2
  127.1 37.0 %shard_map.78 = f32[640,16384]{1,0:T(8,128)} custom-call(bf16[16,512,1024]{2,1,0:T(8,128)(2,1)} %get-tuple-element.21.g_hbm, f32[32,512,512]{2,1,0:T(8,128)} %get-tuple-element.22.z_hbm, bf16[512,1280]{1,0:T(8,128)(2,1)} %bitcast.9, bf16[512,1280]{1,0:T(8,128)(2,1)} %copy-done, f32[16,128]{1,0:T(8,128)} %get-tuple-element.23.st0, f32[16,128]{1,0:T(8,128)} %copy-done.2, ...), custom_call_target="tpu_custom_call" | custom-call | flops 21474836480 | bytes 109051904 | tf_op jit(solution)/shard_map/pallas_call | solution.py:780
  164.1 0.1 add.7
  164.3 1.2 slice_bitcast_fusion
  165.5 1.8 %collective-permute-done.11 = f32[256,1280]{1,0:T(8,128)S(1)} collective-permute-done((f32[256,1280]{1,0:T(8,128)S(1)}, f32[256,1280]{1,0:T(8,128)S(1)}, u32[]{:S(2)}, u32[]{:S(2)}) %collective-permute-start.11) | collective-permute-done | bytes 1310752 | tf_op jit(solution)/shard_map/ppermute | solution.py:699
  167.3 1.7 maximum_select_fusion
  (27 shorter events, 0.2 us)
Async XLA Ops:
  0.6 43.3 %collective-permute-start = (bf16[512,1280]{1,0:T(8,128)(2,1)}, bf16[512,1280]{1,0:T(8,128)(2,1)S(1)}, u32[]{:S(2)}, u32[]{:S(2)}) collective-permute-start(bf16[512,1280]{1,0:T(8,128)(2,1)} %bitcast.7), channel_id=1, source_target_pairs={{0,4},{4,0},{1,5},{5,1},{2,6},{6,2},{3,7},{7,3}} | collective-permute-start | bytes 3932168 | tf_op jit(solution)/shard_map/ppermute | solution.py:705
  37.7 1.9 %collective-permute-start.1 = (f32[152,128]{1,0:T(8,128)}, f32[152,128]{1,0:T(8,128)S(1)}, u32[]{:S(2)}, u32[]{:S(2)}) collective-permute-start(f32[152,128]{1,0:T(8,128)} %get-tuple-element.15.p0), channel_id=1, source_target_pairs={{0,1},{1,0},{2,3},{3,2},{4,5},{5,4},{6,7},{7,6}} | collective-permute-start | bytes 233480 | tf_op jit(solution)/shard_map/ppermute | solution.py:699
  37.8 5.5 %collective-permute-start.2 = (f32[152,128]{1,0:T(8,128)}, f32[152,128]{1,0:T(8,128)S(1)}, u32[]{:S(2)}, u32[]{:S(2)}) collective-permute-start(f32[152,128]{1,0:T(8,128)} %get-tuple-element.15.p0), channel_id=1, source_target_pairs={{0,2},{1,3},{2,0},{3,1},{4,6},{5,7},{6,4},{7,5}} | collective-permute-start | bytes 233480 | tf_op jit(solution)/shard_map/ppermute | solution.py:699
  38.6 5.3 %collective-permute-start.3 = (f32[152,128]{1,0:T(8,128)}, f32[152,128]{1,0:T(8,128)S(1)}, u32[]{:S(2)}, u32[]{:S(2)}) collective-permute-start(f32[152,128]{1,0:T(8,128)} %get-tuple-element.15.p0), channel_id=1, source_target_pairs={{0,3},{1,2},{2,1},{3,0},{4,7},{5,6},{6,5},{7,4}} | collective-permute-start | bytes 233480 | tf_op jit(solution)/shard_map/ppermute | solution.py:699
  39.6 4.3 %copy-start.6 = (f32[152,128]{1,0:T(8,128)}, f32[152,128]{1,0:T(8,128)S(1)}, u32[]{:S(2)}) copy-start(f32[152,128]{1,0:T(8,128)S(1)} %collective-permute-done.1.p1) | copy-start | bytes 233476
  43.2 0.7 copy-start.7
  43.9 0.6 copy-start.8
  43.9 1.1 copy-start
  45.0 77.7 %copy-start.9 = (s32[2,34]{1,0:T(2,128)S(1)}, s32[2,34]{1,0:T(2,128)}, u32[]{:S(2)}) copy-start(s32[2,34]{1,0:T(2,128)} %get-tuple-element.17.meta_ref) | copy-start | bytes 820
  119.4 3.3 %collective-permute-start.4 = (f32[256,1280]{1,0:T(8,128)}, f32[256,1280]{1,0:T(8,128)S(1)}, u32[]{:S(2)}, u32[]{:S(2)}) collective-permute-start(f32[256,1280]{1,0:T(8,128)} %get-tuple-element.20), channel_id=1, source_target_pairs={{0,1},{1,0},{2,3},{3,2},{4,5},{5,4},{6,7},{7,6}} | collective-permute-start | bytes 3932168 | tf_op jit(solution)/shard_map/ppermute | solution.py:699
  119.9 6.6 %collective-permute-start.8 = (f32[256,128]{1,0:T(8,128)}, f32[256,128]{1,0:T(8,128)S(1)}, u32[]{:S(2)}, u32[]{:S(2)}) collective-permute-start(f32[256,128]{1,0:T(8,128)} %get-tuple-element.24), channel_id=1, source_target_pairs={{0,4},{4,0},{1,5},{5,1},{2,6},{6,2},{3,7},{7,3}} | collective-permute-start | bytes 393224 | tf_op jit(solution)/shard_map/ppermute | solution.py:705
  120.4 6.0 %collective-permute-start.5 = (f32[16,128]{1,0:T(8,128)}, f32[16,128]{1,0:T(8,128)S(1)}, u32[]{:S(2)}, u32[]{:S(2)}) collective-permute-start(f32[16,128]{1,0:T(8,128)} %get-tuple-element.23.st0), channel_id=1, source_target_pairs={{0,1},{1,0},{2,3},{3,2},{4,5},{5,4},{6,7},{7,6}} | collective-permute-start | bytes 24584 | tf_op jit(solution)/shard_map/ppermute | solution.py:699
  120.4 6.0 %collective-permute-start.6 = (f32[16,128]{1,0:T(8,128)}, f32[16,128]{1,0:T(8,128)S(1)}, u32[]{:S(2)}, u32[]{:S(2)}) collective-permute-start(f32[16,128]{1,0:T(8,128)} %get-tuple-element.23.st0), channel_id=1, source_target_pairs={{0,2},{1,3},{2,0},{3,1},{4,6},{5,7},{6,4},{7,5}} | collective-permute-start | bytes 24584 | tf_op jit(solution)/shard_map/ppermute | solution.py:699
  120.4 6.0 %collective-permute-start.7 = (f32[16,128]{1,0:T(8,128)}, f32[16,128]{1,0:T(8,128)S(1)}, u32[]{:S(2)}, u32[]{:S(2)}) collective-permute-start(f32[16,128]{1,0:T(8,128)} %get-tuple-element.23.st0), channel_id=1, source_target_pairs={{0,3},{1,2},{2,1},{3,0},{4,7},{5,6},{6,5},{7,4}} | collective-permute-start | bytes 24584 | tf_op jit(solution)/shard_map/ppermute | solution.py:699
  122.7 3.6 %collective-permute-start.9 = (s32[2,34]{1,0:T(2,128)S(1)}, s32[2,34]{1,0:T(2,128)S(1)}, u32[]{:S(2)}, u32[]{:S(2)}) collective-permute-start(s32[2,34]{1,0:T(2,128)S(1)} %copy-done.9), channel_id=1, source_target_pairs={{0,4},{4,0},{1,5},{5,1},{2,6},{6,2},{3,7},{7,3}} | collective-permute-start | bytes 824 | tf_op jit(solution)/shard_map/ppermute | solution.py:705
  126.3 0.5 copy-start.5
  126.3 37.8 %collective-permute-start.10 = (f32[256,1280]{1,0:T(8,128)S(1)}, f32[256,1280]{1,0:T(8,128)S(1)}, u32[]{:S(2)}, u32[]{:S(2)}) collective-permute-start(f32[256,1280]{1,0:T(8,128)S(1)} %add.6), channel_id=1, source_target_pairs={{0,2},{1,3},{2,0},{3,1},{4,6},{5,7},{6,4},{7,5}} | collective-permute-start | bytes 3932168 | tf_op jit(solution)/shard_map/ppermute | solution.py:699
  126.4 0.6 copy-start.2
  126.4 0.6 copy-start.3
  126.4 0.6 copy-start.4
  126.4 0.6 copy-start.1
  164.2 3.1 %collective-permute-start.11 = (f32[256,1280]{1,0:T(8,128)S(1)}, f32[256,1280]{1,0:T(8,128)S(1)}, u32[]{:S(2)}, u32[]{:S(2)}) collective-permute-start(f32[256,1280]{1,0:T(8,128)S(1)} %add.7), channel_id=1, source_target_pairs={{0,1},{1,0},{2,3},{3,2},{4,5},{5,4},{6,7},{7,6}} | collective-permute-start | bytes 3932168 | tf_op jit(solution)/shard_map/ppermute | solution.py:699

commit v6 on v5

--- a/solution.py
+++ b/solution.py
@@ -14,6 +14,7 @@
 ALONG = dict(axis=1, keepdims=True)
 BF16 = jnp.bfloat16
 TILE = 512
+W_PARTS = 5
 LANES = 128
 HALF = LANES // 2
 MIB = 1 << 20
@@ -84,13 +85,27 @@
     lax.while_loop(lambda i: i >= 0, body, head[tile])
 
 
+class SplitCopy:
+    def __init__(self, src, dst, sem, parts):
+        n = src.shape[0] // parts
+        self.copies = [pltpu.make_async_copy(src.at[pl.ds(p * n, n)], dst.at[pl.ds(p * n, n)], sem) for p in range(parts)]
+
+    def start(self):
+        for p, c in enumerate(self.copies):
+            c.start(priority=p % 2)
+
+    def wait(self):
+        for c in self.copies:
+            c.wait()
+
+
 class TileStream:
-    def __init__(self, src, buf, sem, depth, n_tiles, view):
-        self.src, self.buf, self.sem, self.depth, self.n, self.view = src, buf, sem, depth, n_tiles, view
+    def __init__(self, src, buf, sem, depth, n_tiles, view, parts):
+        self.src, self.buf, self.sem, self.depth, self.n, self.view, self.parts = src, buf, sem, depth, n_tiles, view, parts
 
     def copy(self, j):
         slot = lax.rem(j, self.depth)
-        return pltpu.make_async_copy(self.view(self.src, j), self.buf.at[slot], self.sem.at[slot])
+        return SplitCopy(self.view(self.src, j), self.buf.at[slot], self.sem.at[slot], self.parts)
 
     def prime(self):
         for j in range(min(self.depth - 1, self.n)):
@@ -183,7 +198,7 @@
         meta_ref[q, n_lab] = in_len_ref[q]
         meta_ref[q, n_lab + 1] = lab_len_ref[q]
     group = zbuf.shape[1]
-    stream = TileStream(w_hbm, wbuf, wsem, wbuf.shape[0], n_tiles // group, lambda src, j: w_view(src, j, group))
+    stream = TileStream(w_hbm, wbuf, wsem, wbuf.shape[0], n_tiles // group, lambda src, j: w_view(src, j, group), W_PARTS)
     stream.prime()
     col_start = build_lists([meta_ref], n_tiles * TILE, head, nxt)
     m_ref[...] = jnp.full(m_ref.shape, NEG_BIG, F32)
@@ -196,7 +211,7 @@
 
     def out_copy(j):
         slot = lax.rem(j, zbuf.shape[0])
-        return pltpu.make_async_copy(zbuf.at[slot], z_view(z_hbm, j, group), zsem.at[slot])
+        return SplitCopy(zbuf.at[slot], z_view(z_hbm, j, group), zsem.at[slot], group)
 
     def step(j, c):
         slot = stream.get(j)
@@ -248,12 +263,12 @@
 def z_oth_loop(lo, hi, join, h_ref, w_hbm, z_hbm, wbuf, wsem, zbuf, zsem, m_ref, s_ref, sections):
     group = zbuf.shape[1]
     lo, n_groups = lo // group, (hi - lo) // group
-    stream = TileStream(w_hbm, wbuf, wsem, wbuf.shape[0], n_groups, lambda src, j: w_view(src, lo + j, group))
+    stream = TileStream(w_hbm, wbuf, wsem, wbuf.shape[0], n_groups, lambda src, j: w_view(src, lo + j, group), W_PARTS)
     stream.prime()
 
     def out_copy(j):
         slot = lax.rem(j, zbuf.shape[0])
-        return pltpu.make_async_copy(zbuf.at[slot], z_view(z_hbm, lo + j, group), zsem.at[slot])
+        return SplitCopy(zbuf.at[slot], z_view(z_hbm, lo + j, group), zsem.at[slot], group)
 
     base = 0
     join.wait()
@@ -515,8 +530,8 @@
     meta_refs = [meta_ref]
     group = zbuf.shape[1]
     n_groups = n_tiles // group
-    stream = TileStream(w_hbm, wbuf, wsem, wbuf.shape[0], n_groups, lambda src, j: w_view(src, j, group))
-    zs = TileStream(z_hbm, zbuf, zsem, zbuf.shape[0], n_groups, lambda src, j: z_view(src, j, group))
+    stream = TileStream(w_hbm, wbuf, wsem, wbuf.shape[0], n_groups, lambda src, j: w_view(src, j, group), W_PARTS)
+    zs = TileStream(z_hbm, zbuf, zsem, zbuf.shape[0], n_groups, lambda src, j: z_view(src, j, group), group)
     zs.prime()
     yield stream.prime
     col_start = build_lists(meta_refs, n_tiles * TILE, head, nxt)
@@ -605,7 +620,7 @@
     d_loc = ht.shape[0]
     group = zbuf.shape[1]
     n_groups = n_tiles // group
-    zs = TileStream(z_hbm, zbuf, zsem, zbuf.shape[0], n_groups, lambda src, j: z_view(src, j, group))
+    zs = TileStream(z_hbm, zbuf, zsem, zbuf.shape[0], n_groups, lambda src, j: z_view(src, j, group), group)
 
     def g_copy(j, g, k):
         return pltpu.make_async_copy(g_hbm.at[j], g.at[0:rows, :], gsem.at[k])
@@ -640,7 +655,7 @@
 
     def out_copy(j):
         slot = lax.rem(j, obuf.shape[0])
-        return pltpu.make_async_copy(obuf.at[slot], w_view(gw_hbm, j, group), osem.at[slot])
+        return SplitCopy(obuf.at[slot], w_view(gw_hbm, j, group), osem.at[slot], W_PARTS)
 
     slot0 = zs.get(0)
     for u in range(n_units):

time: 169 us -> 170 us (level)
  no operation moved by 1% of the time
where the time goes in v6:
time: 170 us; the launch traced here: 169 us
  Pallas kernels  145 us (85%)
  starting transfers between devices  9.15 us (5%)
  waiting for transfers between devices  7.69 us (5%)
  other arithmetic  3.28 us (2%)
  local copies, waits for them, and re-layouts  2.9 us (2%)
    pallas_call x1, Pallas kernels, local_body(): kernel_call(functools.partial(mid_kernel, 0, n_tiles, n_lat, lat_steps, n...  73.6 us
    pallas_call x1, Pallas kernels, local_body(): kernel_call(functools.partial(grad_w_kernel, n_slots), out_shape=jax.Shap...  37.2 us
    pallas_call x1, Pallas kernels, local_body(): kernel_call(functools.partial(z_own_kernel, n_slots), out_shape=(z_type,...  34.6 us
    ppermute x9, waiting for transfers between devices, tp_xor(): return lax.ppermute(x, 'tp', [(i, i ^ mask) for i in range(n_tp)])  6.62 us
    ppermute x3, starting transfers between devices, swap_dp(): return lax.ppermute(x, 'dp', dp_swap)  4.9 us
    ppermute x9, starting transfers between devices, tp_xor(): return lax.ppermute(x, 'tp', [(i, i ^ mask) for i in range(n_tp)])  4.25 us
  transfers between devices with their start and end apart: 12, of which 5 were waited for; matrix products, arithmetic and copies ran while one was open for 2% of the time, Pallas kernels for 42%

profile of v6, /device:TPU:0, one launch (start us, length us, event | category | flops | bytes accessed | tf_op | source)
XLA Modules:
  0.0 169.2 jit_solution(5191289745428280091)
XLA Ops:
  0.6 3.4 %collective-permute-start = (bf16[512,1280]{1,0:T(8,128)(2,1)}, bf16[512,1280]{1,0:T(8,128)(2,1)S(1)}, u32[]{:S(2)}, u32[]{:S(2)}) collective-permute-start(bf16[512,1280]{1,0:T(8,128)(2,1)} %bitcast.7), channel_id=1, source_target_pairs={{0,4},{4,0},{1,5},{5,1},{2,6},{6,2},{3,7},{7,3}} | collective-permute-start | bytes 3932168 | tf_op jit(solution)/shard_map/ppermute | solution.py:720
  4.0 34.6 %shard_map.76 = (f32[32,512,512]{2,1,0:T(8,128)}, f32[152,128]{1,0:T(8,128)}, s32[2,34]{1,0:T(2,128)}) custom-call(bf16[512,1280]{1,0:T(8,128)(2,1)} %bitcast.8, bf16[1280,16384]{1,0:T(8,128)(2,1)} %w_hbm.3, s32[2,32]{1,0:T(2,128)} %labels_ref.1, s32[2]{0:T(128)} %in_len_ref.1, s32[2]{0:T(128)} %lab_len_ref.1), custom_call_target="tpu_custom_call" | custom-call | flops 21474836480 | bytes 75497472 | tf_op jit(solution)/shard_map/pallas_call | solution.py:758
  38.6 0.9 collective-permute-start.2
  39.5 1.0 collective-permute-start.3
  40.5 3.6 %collective-permute-done.2.p2 = f32[152,128]{1,0:T(8,128)S(1)} collective-permute-done((f32[152,128]{1,0:T(8,128)}, f32[152,128]{1,0:T(8,128)S(1)}, u32[]{:S(2)}, u32[]{:S(2)}) %collective-permute-start.2) | collective-permute-done | bytes 77856 | tf_op jit(solution)/shard_map/ppermute | solution.py:714
  44.1 0.7 collective-permute-done.3.p3
  44.8 0.6 copy-done.8
  45.4 0.5 copy-done
  45.9 73.6 %shard_map.77 = (f32[32,512,512]{2,1,0:T(8,128)}, f32[16,128]{1,0:T(8,128)}, f32[256,128]{1,0:T(8,128)}, f32[256,1280]{1,0:T(8,128)}, f32[256,1280]{1,0:T(8,128)...) custom-call(bf16[512,1280]{1,0:T(8,128)(2,1)} %copy-done, bf16[1280,16384]{1,0:T(8,128)(2,1)} %w_hbm.3, ...), custom_call_target="tpu_custom_call" | custom-call | flops 42949672960 | bytes 150994944 | tf_op jit(solution)/shard_map/pallas_call | solution.py:775
  119.5 0.5 collective-permute-start.4
  119.9 0.5 collective-permute-start.8
  120.5 1.9 %collective-permute-start.7 = (f32[16,128]{1,0:T(8,128)}, f32[16,128]{1,0:T(8,128)S(1)}, u32[]{:S(2)}, u32[]{:S(2)}) collective-permute-start(f32[16,128]{1,0:T(8,128)} %get-tuple-element.23.st0), channel_id=1, source_target_pairs={{0,3},{1,2},{2,1},{3,0},{4,7},{5,6},{6,5},{7,4}} | collective-permute-start | bytes 24584 | tf_op jit(solution)/shard_map/ppermute | solution.py:714
  122.3 0.5 collective-permute-done.4
  122.8 1.0 collective-permute-start.9
  123.8 1.5 add.6
  125.3 1.1 collective-permute-done.9.meta_ref
  126.5 0.5 copy-done.5
  126.9 0.1 copy-done.2
  127.0 0.1 copy-done.1
  127.1 37.2 %shard_map.78 = f32[640,16384]{1,0:T(8,128)} custom-call(bf16[16,512,1024]{2,1,0:T(8,128)(2,1)} %get-tuple-element.21.g_hbm, f32[32,512,512]{2,1,0:T(8,128)} %get-tuple-element.22.z_hbm, bf16[512,1280]{1,0:T(8,128)(2,1)} %bitcast.9, bf16[512,1280]{1,0:T(8,128)(2,1)} %copy-done, f32[16,128]{1,0:T(8,128)} %get-tuple-element.23.st0, f32[16,128]{1,0:T(8,128)} %copy-done.2, ...), custom_call_target="tpu_custom_call" | custom-call | flops 21474836480 | bytes 109051904 | tf_op jit(solution)/shard_map/pallas_call | solution.py:795
  164.4 0.1 add.7
  164.5 1.2 slice_bitcast_fusion
  165.7 1.8 %collective-permute-done.11 = f32[256,1280]{1,0:T(8,128)S(1)} collective-permute-done((f32[256,1280]{1,0:T(8,128)S(1)}, f32[256,1280]{1,0:T(8,128)S(1)}, u32[]{:S(2)}, u32[]{:S(2)}) %collective-permute-start.11) | collective-permute-done | bytes 1310752 | tf_op jit(solution)/shard_map/ppermute | solution.py:714
  167.6 1.7 maximum_select_fusion
  (27 shorter events, 0.1 us)
Async XLA Ops:
  0.6 44.1 %collective-permute-start = (bf16[512,1280]{1,0:T(8,128)(2,1)}, bf16[512,1280]{1,0:T(8,128)(2,1)S(1)}, u32[]{:S(2)}, u32[]{:S(2)}) collective-permute-start(bf16[512,1280]{1,0:T(8,128)(2,1)} %bitcast.7), channel_id=1, source_target_pairs={{0,4},{4,0},{1,5},{5,1},{2,6},{6,2},{3,7},{7,3}} | collective-permute-start | bytes 3932168 | tf_op jit(solution)/shard_map/ppermute | solution.py:720
  38.6 1.9 %collective-permute-start.1 = (f32[152,128]{1,0:T(8,128)}, f32[152,128]{1,0:T(8,128)S(1)}, u32[]{:S(2)}, u32[]{:S(2)}) collective-permute-start(f32[152,128]{1,0:T(8,128)} %get-tuple-element.15.p0), channel_id=1, source_target_pairs={{0,1},{1,0},{2,3},{3,2},{4,5},{5,4},{6,7},{7,6}} | collective-permute-start | bytes 233480 | tf_op jit(solution)/shard_map/ppermute | solution.py:714
  38.6 5.5 %collective-permute-start.2 = (f32[152,128]{1,0:T(8,128)}, f32[152,128]{1,0:T(8,128)S(1)}, u32[]{:S(2)}, u32[]{:S(2)}) collective-permute-start(f32[152,128]{1,0:T(8,128)} %get-tuple-element.15.p0), channel_id=1, source_target_pairs={{0,2},{1,3},{2,0},{3,1},{4,6},{5,7},{6,4},{7,5}} | collective-permute-start | bytes 233480 | tf_op jit(solution)/shard_map/ppermute | solution.py:714
  39.5 5.3 %collective-permute-start.3 = (f32[152,128]{1,0:T(8,128)}, f32[152,128]{1,0:T(8,128)S(1)}, u32[]{:S(2)}, u32[]{:S(2)}) collective-permute-start(f32[152,128]{1,0:T(8,128)} %get-tuple-element.15.p0), channel_id=1, source_target_pairs={{0,3},{1,2},{2,1},{3,0},{4,7},{5,6},{6,5},{7,4}} | collective-permute-start | bytes 233480 | tf_op jit(solution)/shard_map/ppermute | solution.py:714
  40.5 4.3 %copy-start.6 = (f32[152,128]{1,0:T(8,128)}, f32[152,128]{1,0:T(8,128)S(1)}, u32[]{:S(2)}) copy-start(f32[152,128]{1,0:T(8,128)S(1)} %collective-permute-done.1.p1) | copy-start | bytes 233476
  44.1 0.7 copy-start.7
  44.8 0.6 copy-start.8
  44.8 1.1 copy-start
  45.8 77.0 %copy-start.9 = (s32[2,34]{1,0:T(2,128)S(1)}, s32[2,34]{1,0:T(2,128)}, u32[]{:S(2)}) copy-start(s32[2,34]{1,0:T(2,128)} %get-tuple-element.17.meta_ref) | copy-start | bytes 820
  119.5 3.3 %collective-permute-start.4 = (f32[256,1280]{1,0:T(8,128)}, f32[256,1280]{1,0:T(8,128)S(1)}, u32[]{:S(2)}, u32[]{:S(2)}) collective-permute-start(f32[256,1280]{1,0:T(8,128)} %get-tuple-element.20), channel_id=1, source_target_pairs={{0,1},{1,0},{2,3},{3,2},{4,5},{5,4},{6,7},{7,6}} | collective-permute-start | bytes 3932168 | tf_op jit(solution)/shard_map/ppermute | solution.py:714
  119.9 6.5 %collective-permute-start.8 = (f32[256,128]{1,0:T(8,128)}, f32[256,128]{1,0:T(8,128)S(1)}, u32[]{:S(2)}, u32[]{:S(2)}) collective-permute-start(f32[256,128]{1,0:T(8,128)} %get-tuple-element.24), channel_id=1, source_target_pairs={{0,4},{4,0},{1,5},{5,1},{2,6},{6,2},{3,7},{7,3}} | collective-permute-start | bytes 393224 | tf_op jit(solution)/shard_map/ppermute | solution.py:720
  120.5 5.9 %collective-permute-start.5 = (f32[16,128]{1,0:T(8,128)}, f32[16,128]{1,0:T(8,128)S(1)}, u32[]{:S(2)}, u32[]{:S(2)}) collective-permute-start(f32[16,128]{1,0:T(8,128)} %get-tuple-element.23.st0), channel_id=1, source_target_pairs={{0,1},{1,0},{2,3},{3,2},{4,5},{5,4},{6,7},{7,6}} | collective-permute-start | bytes 24584 | tf_op jit(solution)/shard_map/ppermute | solution.py:714
  120.5 6.0 %collective-permute-start.6 = (f32[16,128]{1,0:T(8,128)}, f32[16,128]{1,0:T(8,128)S(1)}, u32[]{:S(2)}, u32[]{:S(2)}) collective-permute-start(f32[16,128]{1,0:T(8,128)} %get-tuple-element.23.st0), channel_id=1, source_target_pairs={{0,2},{1,3},{2,0},{3,1},{4,6},{5,7},{6,4},{7,5}} | collective-permute-start | bytes 24584 | tf_op jit(solution)/shard_map/ppermute | solution.py:714
  120.5 6.0 %collective-permute-start.7 = (f32[16,128]{1,0:T(8,128)}, f32[16,128]{1,0:T(8,128)S(1)}, u32[]{:S(2)}, u32[]{:S(2)}) collective-permute-start(f32[16,128]{1,0:T(8,128)} %get-tuple-element.23.st0), channel_id=1, source_target_pairs={{0,3},{1,2},{2,1},{3,0},{4,7},{5,6},{6,5},{7,4}} | collective-permute-start | bytes 24584 | tf_op jit(solution)/shard_map/ppermute | solution.py:714
  122.8 3.6 %collective-permute-start.9 = (s32[2,34]{1,0:T(2,128)S(1)}, s32[2,34]{1,0:T(2,128)S(1)}, u32[]{:S(2)}, u32[]{:S(2)}) collective-permute-start(s32[2,34]{1,0:T(2,128)S(1)} %copy-done.9), channel_id=1, source_target_pairs={{0,4},{4,0},{1,5},{5,1},{2,6},{6,2},{3,7},{7,3}} | collective-permute-start | bytes 824 | tf_op jit(solution)/shard_map/ppermute | solution.py:720
  126.4 0.5 copy-start.5
  126.4 38.0 %collective-permute-start.10 = (f32[256,1280]{1,0:T(8,128)S(1)}, f32[256,1280]{1,0:T(8,128)S(1)}, u32[]{:S(2)}, u32[]{:S(2)}) collective-permute-start(f32[256,1280]{1,0:T(8,128)S(1)} %add.6), channel_id=1, source_target_pairs={{0,2},{1,3},{2,0},{3,1},{4,6},{5,7},{6,4},{7,5}} | collective-permute-start | bytes 3932168 | tf_op jit(solution)/shard_map/ppermute | solution.py:714
  126.4 0.6 copy-start.2
  126.4 0.6 copy-start.3
  126.4 0.6 copy-start.4
  126.5 0.6 copy-start.1
  164.5 3.1 %collective-permute-start.11 = (f32[256,1280]{1,0:T(8,128)S(1)}, f32[256,1280]{1,0:T(8,128)S(1)}, u32[]{:S(2)}, u32[]{:S(2)}) collective-permute-start(f32[256,1280]{1,0:T(8,128)S(1)} %add.7), channel_id=1, source_target_pairs={{0,1},{1,0},{2,3},{3,2},{4,5},{5,4},{6,7},{7,6}} | collective-permute-start | bytes 3932168 | tf_op jit(solution)/shard_map/ppermute | solution.py:714

commit v7 on v6

--- a/solution.py
+++ b/solution.py
@@ -167,7 +167,7 @@
             lhs = after(h_ref[rows, :], zeros[-2] if len(zeros) >= 2 else None)
             z = jnp.dot(lhs, w[:, t * TILE:(t + 1) * TILE], preferred_element_type=F32)
             z_out[t, rows, :] = z
-            zeros.append(unit_stats(z, m_ref, s_ref, r * n))
+            zeros.append(None if m_ref is None else unit_stats(z, m_ref, s_ref, r * n))
 
 
 def emit_stats(m_ref, s_ref, out_ref, base):
@@ -260,7 +260,7 @@
         out_copy(j).wait()
 
 
-def z_oth_loop(lo, hi, join, h_ref, w_hbm, z_hbm, wbuf, wsem, zbuf, zsem, m_ref, s_ref, sections):
+def z_oth_loop(lo, hi, join, h_ref, w_hbm, z_hbm, wbuf, wsem, zbuf, zsem, sections):
     group = zbuf.shape[1]
     lo, n_groups = lo // group, (hi - lo) // group
     stream = TileStream(w_hbm, wbuf, wsem, wbuf.shape[0], n_groups, lambda src, j: w_view(src, lo + j, group), W_PARTS)
@@ -283,7 +283,7 @@
             def _():
                 out_copy(j - 3).wait()
 
-            z_group(h_ref, wbuf.at[slot], zbuf.at[lax.rem(j, zbuf.shape[0])], m_ref, s_ref)
+            z_group(h_ref, wbuf.at[slot], zbuf.at[lax.rem(j, zbuf.shape[0])], None, None)
             c = side(k, c)
             out_copy(j).start()
             return c
@@ -296,14 +296,12 @@
 
 
 def z_lattice_part(lo, hi, n_lat, per_group, n_lab, before_tail, h_oth, w_hbm, p0, p1, p2, p3, meta_ref,
-                     z_hbm, stats_ref, occ_ref, loss_ref, m_ref, s_ref,
+                     z_hbm, occ_ref, loss_ref,
                      h_ref, hsem, wbuf, wsem, zbuf, zsem, e_lab, e_blk, s_lab, s_blk, r_lab, r_blk, o_t):
     join = pltpu.make_async_copy(h_oth, h_ref, hsem.at[0])
     join.start()
     n_blk = e_lab.shape[0]
     frames = n_blk * HALF
-    m_ref[...] = jnp.full(m_ref.shape, NEG_BIG, F32)
-    s_ref[...] = jnp.zeros(s_ref.shape, F32)
     lane128 = lax.broadcasted_iota(jnp.int32, (LANES, LANES), 1)
     row32 = lax.broadcasted_iota(jnp.int32, (n_lab, LANES), 0)
     row8 = lax.broadcasted_iota(jnp.int32, (8, LANES), 0)
@@ -419,7 +417,7 @@
     n_occ = (hi - lo - n_lat) // group
     occ_group = frames // n_occ // HALF
     seq_of8 = jnp.where(lane8 >= HALF, 1, 0)
-    run = z_oth_loop(lo, hi, join, h_ref, w_hbm, z_hbm, wbuf, wsem, zbuf, zsem, m_ref, s_ref,
+    run = z_oth_loop(lo, hi, join, h_ref, w_hbm, z_hbm, wbuf, wsem, zbuf, zsem,
                      [(n_lat_groups, lattice_side, lambda: (neg32, first_b, first_t)),
                       (n_occ, lambda k, c: occ_side(k, c), lambda: 0)])
     al, ab, at = next(run)
@@ -459,7 +457,6 @@
     before_tail()
     for _ in run:
         pass
-    emit_stats(m_ref, s_ref, stats_ref, 0)
     row128 = lax.broadcasted_iota(jnp.int32, (LANES, LANES), 0)
     same = []
     for s in range(n_seq):
@@ -477,10 +474,13 @@
             jnp.dot(y[HALF * q:HALF * (q + 1), :], same[q], precision=lax.Precision.HIGHEST, preferred_element_type=F32) for q in range(n_seq)])
 
 
-def spread_lse(refs, base, meta_ref, lse_ref, r0, frames):
+def combine_lse(refs, base):
     m = functools.reduce(jnp.maximum, [r[base:base + 8, :] for r in refs])
     tot = functools.reduce(jnp.add, [r[base + 8:base + 16, :] * jnp.exp(r[base:base + 8, :] - m) for r in refs])
-    lse = m + jnp.log(tot)
+    return m + jnp.log(tot)
+
+
+def spread_lse(lse, meta_ref, lse_ref, r0, frames):
     t = lax.broadcasted_iota(jnp.int32, (LANES, LANES), 0)
     n_part = frames // LANES
     sums = []
@@ -505,7 +505,7 @@
     zb = z_block(seq, c0)
     slot_lane = jnp.where(item == 0, n_slots - 1, item - 1) + HALF * seq
     at = off - blk * LANES
-    occ = pltpu.roll(occ_ref[...], lax.rem(at - slot_lane + LANES, LANES), 1)
+    occ = pltpu.roll(occ_ref[0:frames, :], lax.rem(at - slot_lane + LANES, LANES), 1)
     fresh = jnp.exp(zb - lse_ref[pl.ds(r0, frames), :]) - occ
     gc = pl.multiple_of(g_col + c0, LANES)
     old = g_ref[pl.ds(r0, frames), pl.ds(gc, LANES)].astype(F32)
@@ -535,7 +535,9 @@
     zs.prime()
     yield stream.prime
     col_start = build_lists(meta_refs, n_tiles * TILE, head, nxt)
-    sums = spread_lse([st0, st1, st2, st3], frames // 2, meta_ref, lse_ref, 0, frames)
+    lse = combine_lse([st0, st1, st2, st3], frames // 2)
+    occ_ref[frames:frames + 8, :] = lse
+    sums = spread_lse(lse, meta_ref, lse_ref, 0, frames)
     lane1 = lax.broadcasted_iota(jnp.int32, (8, LANES), 1)
     loss_ref[...] = part_loss[...] + jnp.where(lane1 == 0, sums[0], sums[1])
     lane = lax.broadcasted_iota(jnp.int32, (frames, LANES), 1)
@@ -600,20 +602,20 @@
 
 
 def mid_kernel(lo, hi, n_lat, per_group, n_lab, h_oth, w_hbm, p0, p1, p2, p3, z_own, meta_ref,
-               z_hbm, stats_ref, occ_ref, keep_ref, send_ref, loss_ref, g_hbm,
-               part_loss, m_ref, s_ref, h_ref, hsem, wbuf, wsem, zbuf, zsem, e_lab, e_blk, s_lab, s_blk, r_lab, r_blk, o_t,
+               z_hbm, occ_ref, keep_ref, send_ref, loss_ref, g_hbm,
+               part_loss, h_ref, hsem, wbuf, wsem, zbuf, zsem, e_lab, e_blk, s_lab, s_blk, r_lab, r_blk, o_t,
                zin_buf, zin_sem, acc, lse_ref, g0, g1, gsem, head, nxt):
     second = grad_h_part(n_lab + 1, z_own, w_hbm, p0, p1, p2, p3, occ_ref, part_loss, meta_ref, keep_ref, send_ref, loss_ref, g_hbm,
                          wbuf, wsem, zin_buf, zin_sem, acc, lse_ref, g0, g1, gsem, head, nxt)
     prime_w = next(second)
     z_lattice_part(lo, hi, n_lat, per_group, n_lab, prime_w, h_oth, w_hbm, p0, p1, p2, p3, meta_ref,
-                   z_hbm, stats_ref, occ_ref, part_loss, m_ref, s_ref,
+                   z_hbm, occ_ref, part_loss,
                    h_ref, hsem, wbuf, wsem, zbuf, zsem, e_lab, e_blk, s_lab, s_blk, r_lab, r_blk, o_t)
     for _ in second:
         pass
 
 
-def grad_w_kernel(n_slots, g_hbm, z_hbm, h_own_hbm, h_oth, st0, st1, st2, st3, occ_ref, meta_ref, gw_hbm,
+def grad_w_kernel(n_slots, g_hbm, z_hbm, h_own_hbm, h_oth, occ_ref, meta_ref, gw_hbm,
                   h_ref, hsem, h_own_ref, zbuf, zsem, gsem, obuf, osem, ht, lse_ref, g0, g1, head, nxt):
     n_tiles, rows = z_hbm.shape[0], z_hbm.shape[1]
     frames = rows // meta_ref.shape[0]
@@ -635,7 +637,7 @@
     d0 = pl.multiple_of(lax.axis_index("dp") * d_loc, LANES)
     own_copy.wait()
     ht[:, 0:rows] = h_own_ref[:, pl.ds(d0, d_loc)].T
-    spread_lse([st0, st1, st2, st3], 0, meta_ref, lse_ref, 0, frames)
+    spread_lse(occ_ref[frames:frames + 8, :], meta_ref, lse_ref, 0, frames)
     join.wait()
     ht[:, rows:2 * rows] = h_ref[:, pl.ds(d0, d_loc)].T
     lane = lax.broadcasted_iota(jnp.int32, (frames, LANES), 1)
@@ -740,7 +742,6 @@
         pick_type = jax.ShapeDtypeStruct((frames // 2 + 24, LANES), F32)
         meta_type = jax.ShapeDtypeStruct((batch_loc, n_slots + 1), i32)
         g_type = jax.ShapeDtypeStruct((n_tiles // 2, rows, 2 * TILE), BF16)
-        stat_type = jax.ShapeDtypeStruct((16, LANES), F32)
         g_scratch = [pltpu.VMEM((rows, 2 * TILE), BF16)] * 2
 
         def w_scratch(n):
@@ -770,14 +771,14 @@
 
         n_blk = frames // HALF
         half_type = jax.ShapeDtypeStruct((rows // 2, model_dim), F32)
-        occ_type = jax.ShapeDtypeStruct((frames, LANES), F32)
+        occ_type = jax.ShapeDtypeStruct((frames + 8, LANES), F32)
         loss_type = jax.ShapeDtypeStruct((8, LANES), F32)
-        z_oth, stats_oth, occ, keep, send, loss, g_own = kernel_call(
+        z_oth, occ, keep, send, loss, g_own = kernel_call(
             functools.partial(mid_kernel, 0, n_tiles, n_lat, lat_steps, n_lab),
-            out_shape=(z_type, stat_type, occ_type, half_type, half_type, loss_type, g_type),
+            out_shape=(z_type, occ_type, half_type, half_type, loss_type, g_type),
             in_specs=[any_spec()] * 2 + [vmem_spec()] * 4 + [any_spec(), smem_spec()],
-            out_specs=(any_spec(),) + (vmem_spec(),) * 5 + (any_spec(),),
-            scratch_shapes=[pltpu.VMEM((8, LANES), F32)] + run_scratch + h_scratch + w_scratch(2) + z_scratch(2) + [
+            out_specs=(any_spec(),) + (vmem_spec(),) * 4 + (any_spec(),),
+            scratch_shapes=[pltpu.VMEM((8, LANES), F32)] + h_scratch + w_scratch(2) + z_scratch(2) + [
                 pltpu.VMEM((n_blk, n_lab, LANES), F32), pltpu.VMEM((n_blk, 8, LANES), F32),
                 *[pltpu.VMEM((frames + lat_pad, n, LANES), F32) for n in (n_lab, n_lab + 8) * 2],
                 pltpu.VMEM((n_blk, LANES, LANES), F32)] + z_scratch(2) + [
@@ -785,7 +786,6 @@
             compiler_params=params(),
             cost_estimate=cost((2 * n_tiles) * flops, (2 * n_tiles) * (wbytes + zbytes)),
         )(h_oth, w_loc, *picks, z_own, meta)
-        st_oth = [stats_oth] + [tp_xor(stats_oth, k) for k in others]
         occ_oth = swap_dp(occ)
         meta_oth = swap_dp(meta)
         recv = tp_xor(send, 1)
@@ -795,7 +795,7 @@
         grad_weight = kernel_call(
             functools.partial(grad_w_kernel, n_slots),
             out_shape=jax.ShapeDtypeStruct((d_loc, vocab_loc), F32),
-            in_specs=[any_spec(), any_spec(), any_spec(), any_spec()] + [vmem_spec()] * 5 + [smem_spec()],
+            in_specs=[any_spec(), any_spec(), any_spec(), any_spec(), vmem_spec(), smem_spec()],
             out_specs=any_spec(),
             scratch_shapes=h_scratch + h_scratch[:1] + z_scratch(2) + [
                 dma((2,)), pltpu.VMEM((3, d_loc, 2 * TILE), F32), dma((3,)),
@@ -803,7 +803,7 @@
                 pltpu.VMEM((2 * rows, 2 * TILE), BF16), pltpu.VMEM((2 * rows, 2 * TILE), BF16)] + lists(1),
             compiler_params=params(),
             cost_estimate=cost(n_tiles * flops, n_tiles * (2 * zbytes + d_loc * TILE * 4)),
-        )(g_own, z_oth, in_hbm(h_own), h_oth, *st_oth, occ_oth, meta_oth)
+        )(g_own, z_oth, in_hbm(h_own), h_oth, occ_oth, meta_oth)
 
         chip_sum, grad_weight = lax.optimization_barrier((chip_sum, grad_weight))
         full_half = chip_sum + across

time: 170 us -> 163 us (0.959)
  Pallas kernels: 145 us -> 140 us
    pallas_call x1, Pallas kernels: 73.6 us -> 68.1 us  [local_body(): kernel_call(functools.partial(mid_kernel, 0, n_tiles, n_lat, lat_steps, n...]
    ppermute x9 -> x6, starting transfers between devices: 4.25 us -> 2.43 us  [tp_xor(): return lax.ppermute(x, 'tp', [(i, i ^ mask) for i in range(n_tp)])]
    ppermute x9 -> x6, waiting for transfers between devices: 6.62 us -> 6.96 us  [tp_xor(): return lax.ppermute(x, 'tp', [(i, i ^ mask) for i in range(n_tp)])]
  transfers between devices with their start and end apart: 12 -> 9, of which waited for: 5 -> 5; matrix products, arithmetic and copies ran while one was open for 2% -> 2% of each run, Pallas kernels for 42% -> 44%
where the time goes in v7:
time: 163 us
  Pallas kernels  140 us (86%)
  waiting for transfers between devices  8.37 us (5%)
  starting transfers between devices  7.82 us (5%)
  other arithmetic  3.28 us (2%)
  local copies, waits for them, and re-layouts  2.9 us (2%)
    pallas_call x1, Pallas kernels, local_body(): kernel_call(functools.partial(mid_kernel, 0, n_tiles, n_lat, lat_steps, n...  68.1 us
    pallas_call x1, Pallas kernels, local_body(): kernel_call(functools.partial(grad_w_kernel, n_slots), out_shape=jax.Shap...  37.2 us
    pallas_call x1, Pallas kernels, local_body(): kernel_call(functools.partial(z_own_kernel, n_slots), out_shape=(z_type,...  34.6 us
    ppermute x6, waiting for transfers between devices, tp_xor(): return lax.ppermute(x, 'tp', [(i, i ^ mask) for i in range(n_tp)])  6.96 us
    ppermute x3, starting transfers between devices, swap_dp(): return lax.ppermute(x, 'dp', dp_swap)  5.38 us
  transfers between devices with their start and end apart: 9, of which 5 were waited for; matrix products, arithmetic and copies ran while one was open for 2% of the time, Pallas kernels for 44%

profile of v7, /device:TPU:0, one launch (start us, length us, event | category | flops | bytes accessed | tf_op | source)
XLA Modules:
  0.0 163.0 jit_solution(2089983510499462943)
XLA Ops:
  0.6 3.4 %collective-permute-start = (bf16[512,1280]{1,0:T(8,128)(2,1)}, bf16[512,1280]{1,0:T(8,128)(2,1)S(1)}, u32[]{:S(2)}, u32[]{:S(2)}) collective-permute-start(bf16[512,1280]{1,0:T(8,128)(2,1)} %bitcast.7), channel_id=1, source_target_pairs={{0,4},{4,0},{1,5},{5,1},{2,6},{6,2},{3,7},{7,3}} | collective-permute-start | bytes 3932168 | tf_op jit(solution)/shard_map/ppermute | solution.py:722
  4.0 34.6 %shard_map.76 = (f32[32,512,512]{2,1,0:T(8,128)}, f32[152,128]{1,0:T(8,128)}, s32[2,34]{1,0:T(2,128)}) custom-call(bf16[512,1280]{1,0:T(8,128)(2,1)} %bitcast.8, bf16[1280,16384]{1,0:T(8,128)(2,1)} %w_hbm.3, s32[2,32]{1,0:T(2,128)} %labels_ref.1, s32[2]{0:T(128)} %in_len_ref.1, s32[2]{0:T(128)} %lab_len_ref.1), custom_call_target="tpu_custom_call" | custom-call | flops 21474836480 | bytes 75497472 | tf_op jit(solution)/shard_map/pallas_call | solution.py:759
  38.6 0.9 collective-permute-start.2
  39.5 1.0 collective-permute-start.3
  40.5 3.6 %collective-permute-done.2.p2 = f32[152,128]{1,0:T(8,128)S(1)} collective-permute-done((f32[152,128]{1,0:T(8,128)}, f32[152,128]{1,0:T(8,128)S(1)}, u32[]{:S(2)}, u32[]{:S(2)}) %collective-permute-start.2) | collective-permute-done | bytes 77856 | tf_op jit(solution)/shard_map/ppermute | solution.py:716
  44.1 0.7 collective-permute-done.3.p3
  44.8 0.6 copy-done.5
  45.4 0.4 copy-done
  45.9 68.1 %shard_map.77 = (f32[32,512,512]{2,1,0:T(8,128)}, f32[264,128]{1,0:T(8,128)}, f32[256,1280]{1,0:T(8,128)}, f32[256,1280]{1,0:T(8,128)}, f32[8,128]{1,0:T(8,128)}, /*index=5*/bf16[16,512,1024]{2,1,0:T(8,128)(2,1)}) custom-call(bf16[512,1280]{1,0:T(8,128)(2,1)} %copy-done, bf16[1280,16384]{1,0:T(8,128)(2,1)} %w_hbm.3, f32[152,128]{1,0:T(8,128)} %get-tuple-element.14.p0, ...), custom_call_target="tpu_custom_call" | custom-call | flops 42949672960 | bytes 150994944 | tf_op jit(solution)/shard_map/pallas_call | solution.py:776
  114.0 0.5 collective-permute-start.4
  114.5 0.5 collective-permute-start.5
  115.0 1.5 collective-permute-start.6
  116.5 0.8 collective-permute-done.4
  117.4 1.5 add.6
  118.9 0.0 collective-permute-start.7
  118.9 1.4 collective-permute-done.6.meta_ref
  120.3 0.5 copy-done.2
  120.8 0.1 copy-done.1
  120.9 37.2 %shard_map.78 = f32[640,16384]{1,0:T(8,128)} custom-call(bf16[16,512,1024]{2,1,0:T(8,128)(2,1)} %get-tuple-element.20.g_hbm, f32[32,512,512]{2,1,0:T(8,128)} %get-tuple-element.21.z_hbm, bf16[512,1280]{1,0:T(8,128)(2,1)} %bitcast.9, bf16[512,1280]{1,0:T(8,128)(2,1)} %copy-done, f32[264,128]{1,0:T(8,128)} %copy-done.1, s32[2,34]{1,0:T(2,128)} %copy-done.2), custom_call_target="tpu_custom_call" | custom-call | flops 21474836480 | bytes 109051904 | tf_op jit(solution)/shard_map/pallas_call | solution.py:795
  158.1 0.1 add.7
  158.3 0.0 collective-permute-start.8
  158.3 1.2 slice_bitcast_fusion
  159.5 1.8 %collective-permute-done.8 = f32[256,1280]{1,0:T(8,128)S(1)} collective-permute-done((f32[256,1280]{1,0:T(8,128)S(1)}, f32[256,1280]{1,0:T(8,128)S(1)}, u32[]{:S(2)}, u32[]{:S(2)}) %collective-permute-start.8) | collective-permute-done | bytes 1310752 | tf_op jit(solution)/shard_map/ppermute | solution.py:716
  161.3 1.7 %maximum_select_fusion = f32[2,256,1280]{2,1,0:T(8,128)} fusion(f32[1,256,1280]{2,1,0:T(8,128)S(1)} %bitcast.6, f32[1,256,1280]{2,1,0:T(8,128)S(1)} %bitcast.5, pred[]{:T(512)S(6)} %eq.3), kind=kLoop, calls=%fused_computation | loop fusion | flops 1966080 | bytes 5242881 | tf_op jit(solution)/shard_map/jit(_where)/select_n | solution.py:811
  (15 shorter events, 0.1 us)
Async XLA Ops:
  0.6 44.1 %collective-permute-start = (bf16[512,1280]{1,0:T(8,128)(2,1)}, bf16[512,1280]{1,0:T(8,128)(2,1)S(1)}, u32[]{:S(2)}, u32[]{:S(2)}) collective-permute-start(bf16[512,1280]{1,0:T(8,128)(2,1)} %bitcast.7), channel_id=1, source_target_pairs={{0,4},{4,0},{1,5},{5,1},{2,6},{6,2},{3,7},{7,3}} | collective-permute-start | bytes 3932168 | tf_op jit(solution)/shard_map/ppermute | solution.py:722
  38.6 1.9 %collective-permute-start.1 = (f32[152,128]{1,0:T(8,128)}, f32[152,128]{1,0:T(8,128)S(1)}, u32[]{:S(2)}, u32[]{:S(2)}) collective-permute-start(f32[152,128]{1,0:T(8,128)} %get-tuple-element.14.p0), channel_id=1, source_target_pairs={{0,1},{1,0},{2,3},{3,2},{4,5},{5,4},{6,7},{7,6}} | collective-permute-start | bytes 233480 | tf_op jit(solution)/shard_map/ppermute | solution.py:716
  38.6 5.5 %collective-permute-start.2 = (f32[152,128]{1,0:T(8,128)}, f32[152,128]{1,0:T(8,128)S(1)}, u32[]{:S(2)}, u32[]{:S(2)}) collective-permute-start(f32[152,128]{1,0:T(8,128)} %get-tuple-element.14.p0), channel_id=1, source_target_pairs={{0,2},{1,3},{2,0},{3,1},{4,6},{5,7},{6,4},{7,5}} | collective-permute-start | bytes 233480 | tf_op jit(solution)/shard_map/ppermute | solution.py:716
  39.5 5.3 %collective-permute-start.3 = (f32[152,128]{1,0:T(8,128)}, f32[152,128]{1,0:T(8,128)S(1)}, u32[]{:S(2)}, u32[]{:S(2)}) collective-permute-start(f32[152,128]{1,0:T(8,128)} %get-tuple-element.14.p0), channel_id=1, source_target_pairs={{0,3},{1,2},{2,1},{3,0},{4,7},{5,6},{6,5},{7,4}} | collective-permute-start | bytes 233480 | tf_op jit(solution)/shard_map/ppermute | solution.py:716
  40.5 4.3 %copy-start.3 = (f32[152,128]{1,0:T(8,128)}, f32[152,128]{1,0:T(8,128)S(1)}, u32[]{:S(2)}) copy-start(f32[152,128]{1,0:T(8,128)S(1)} %collective-permute-done.1.p1) | copy-start | bytes 233476
  44.1 0.7 copy-start.4
  44.8 0.6 copy-start.5
  44.8 1.1 copy-start
  45.9 69.2 %copy-start.6 = (s32[2,34]{1,0:T(2,128)S(1)}, s32[2,34]{1,0:T(2,128)}, u32[]{:S(2)}) copy-start(s32[2,34]{1,0:T(2,128)} %get-tuple-element.16.meta_ref) | copy-start | bytes 820
  114.0 3.4 %collective-permute-start.4 = (f32[256,1280]{1,0:T(8,128)}, f32[256,1280]{1,0:T(8,128)S(1)}, u32[]{:S(2)}, u32[]{:S(2)}) collective-permute-start(f32[256,1280]{1,0:T(8,128)} %get-tuple-element.19), channel_id=1, source_target_pairs={{0,1},{1,0},{2,3},{3,2},{4,5},{5,4},{6,7},{7,6}} | collective-permute-start | bytes 3932168 | tf_op jit(solution)/shard_map/ppermute | solution.py:716
  114.5 5.8 %collective-permute-start.5 = (f32[264,128]{1,0:T(8,128)}, f32[264,128]{1,0:T(8,128)S(1)}, u32[]{:S(2)}, u32[]{:S(2)}) collective-permute-start(f32[264,128]{1,0:T(8,128)} %get-tuple-element.22), channel_id=1, source_target_pairs={{0,4},{4,0},{1,5},{5,1},{2,6},{6,2},{3,7},{7,3}} | collective-permute-start | bytes 405512 | tf_op jit(solution)/shard_map/ppermute | solution.py:722
  115.0 5.3 %collective-permute-start.6 = (s32[2,34]{1,0:T(2,128)S(1)}, s32[2,34]{1,0:T(2,128)S(1)}, u32[]{:S(2)}, u32[]{:S(2)}) collective-permute-start(s32[2,34]{1,0:T(2,128)S(1)} %copy-done.6), channel_id=1, source_target_pairs={{0,4},{4,0},{1,5},{5,1},{2,6},{6,2},{3,7},{7,3}} | collective-permute-start | bytes 824 | tf_op jit(solution)/shard_map/ppermute | solution.py:722
  118.9 39.3 %collective-permute-start.7 = (f32[256,1280]{1,0:T(8,128)S(1)}, f32[256,1280]{1,0:T(8,128)S(1)}, u32[]{:S(2)}, u32[]{:S(2)}) collective-permute-start(f32[256,1280]{1,0:T(8,128)S(1)} %add.6), channel_id=1, source_target_pairs={{0,2},{1,3},{2,0},{3,1},{4,6},{5,7},{6,4},{7,5}} | collective-permute-start | bytes 3932168 | tf_op jit(solution)/shard_map/ppermute | solution.py:716
  120.3 0.5 copy-start.2
  120.3 0.6 copy-start.1
  158.3 3.1 %collective-permute-start.8 = (f32[256,1280]{1,0:T(8,128)S(1)}, f32[256,1280]{1,0:T(8,128)S(1)}, u32[]{:S(2)}, u32[]{:S(2)}) collective-permute-start(f32[256,1280]{1,0:T(8,128)S(1)} %add.7), channel_id=1, source_target_pairs={{0,1},{1,0},{2,3},{3,2},{4,5},{5,4},{6,7},{7,6}} | collective-permute-start | bytes 3932168 | tf_op jit(solution)/shard_map/ppermute | solution.py:716

commit v8 on v7

--- a/solution.py
+++ b/solution.py
@@ -161,13 +161,17 @@
     n_tiles = z_out.shape[0]
     n = h_ref.shape[0] // 2
     zeros = []
+    if m_ref is None:
+        for t in range(n_tiles):
+            z_out[t] = jnp.dot(h_ref[...], w[:, t * TILE:(t + 1) * TILE], preferred_element_type=F32)
+        return
     for t in range(n_tiles):
         for r in range(2):
             rows = slice(r * n, (r + 1) * n)
             lhs = after(h_ref[rows, :], zeros[-2] if len(zeros) >= 2 else None)
             z = jnp.dot(lhs, w[:, t * TILE:(t + 1) * TILE], preferred_element_type=F32)
             z_out[t, rows, :] = z
-            zeros.append(None if m_ref is None else unit_stats(z, m_ref, s_ref, r * n))
+            zeros.append(unit_stats(z, m_ref, s_ref, r * n))
 
 
 def emit_stats(m_ref, s_ref, out_ref, base):

time: 163 us -> 162 us (level)
  no operation moved by 1% of the time
where the time goes in v8:
time: 162 us
  Pallas kernels  139 us (86%)
  waiting for transfers between devices  8.37 us (5%)
  starting transfers between devices  7.82 us (5%)
  other arithmetic  3.28 us (2%)
  local copies, waits for them, and re-layouts  2.9 us (2%)
    pallas_call x1, Pallas kernels, local_body(): kernel_call(functools.partial(mid_kernel, 0, n_tiles, n_lat, lat_steps, n...  67.1 us
    pallas_call x1, Pallas kernels, local_body(): kernel_call(functools.partial(grad_w_kernel, n_slots), out_shape=jax.Shap...  37.2 us
    pallas_call x1, Pallas kernels, local_body(): kernel_call(functools.partial(z_own_kernel, n_slots), out_shape=(z_type,...  34.6 us
    ppermute x6, waiting for transfers between devices, tp_xor(): return lax.ppermute(x, 'tp', [(i, i ^ mask) for i in range(n_tp)])  6.96 us
    ppermute x3, starting transfers between devices, swap_dp(): return lax.ppermute(x, 'dp', dp_swap)  5.38 us
  transfers between devices with their start and end apart: 9, of which 5 were waited for; matrix products, arithmetic and copies ran while one was open for 2% of the time, Pallas kernels for 44%

profile of v8, /device:TPU:0, one launch (start us, length us, event | category | flops | bytes accessed | tf_op | source)
XLA Modules:
  0.0 161.9 jit_solution(6551245576806635204)
XLA Ops:
  0.6 3.4 %collective-permute-start = (bf16[512,1280]{1,0:T(8,128)(2,1)}, bf16[512,1280]{1,0:T(8,128)(2,1)S(1)}, u32[]{:S(2)}, u32[]{:S(2)}) collective-permute-start(bf16[512,1280]{1,0:T(8,128)(2,1)} %bitcast.7), channel_id=1, source_target_pairs={{0,4},{4,0},{1,5},{5,1},{2,6},{6,2},{3,7},{7,3}} | collective-permute-start | bytes 3932168 | tf_op jit(solution)/shard_map/ppermute | solution.py:726
  4.0 34.6 %shard_map.76 = (f32[32,512,512]{2,1,0:T(8,128)}, f32[152,128]{1,0:T(8,128)}, s32[2,34]{1,0:T(2,128)}) custom-call(bf16[512,1280]{1,0:T(8,128)(2,1)} %bitcast.8, bf16[1280,16384]{1,0:T(8,128)(2,1)} %w_hbm.3, s32[2,32]{1,0:T(2,128)} %labels_ref.1, s32[2]{0:T(128)} %in_len_ref.1, s32[2]{0:T(128)} %lab_len_ref.1), custom_call_target="tpu_custom_call" | custom-call | flops 21474836480 | bytes 75497472 | tf_op jit(solution)/shard_map/pallas_call | solution.py:763
  38.6 0.9 collective-permute-start.2
  39.5 1.0 collective-permute-start.3
  40.5 3.6 %collective-permute-done.2.p2 = f32[152,128]{1,0:T(8,128)S(1)} collective-permute-done((f32[152,128]{1,0:T(8,128)}, f32[152,128]{1,0:T(8,128)S(1)}, u32[]{:S(2)}, u32[]{:S(2)}) %collective-permute-start.2) | collective-permute-done | bytes 77856 | tf_op jit(solution)/shard_map/ppermute | solution.py:720
  44.1 0.7 collective-permute-done.3.p3
  44.8 0.6 copy-done.5
  45.4 0.4 copy-done
  45.9 67.1 %shard_map.77 = (f32[32,512,512]{2,1,0:T(8,128)}, f32[264,128]{1,0:T(8,128)}, f32[256,1280]{1,0:T(8,128)}, f32[256,1280]{1,0:T(8,128)}, f32[8,128]{1,0:T(8,128)}, /*index=5*/bf16[16,512,1024]{2,1,0:T(8,128)(2,1)}) custom-call(bf16[512,1280]{1,0:T(8,128)(2,1)} %copy-done, bf16[1280,16384]{1,0:T(8,128)(2,1)} %w_hbm.3, f32[152,128]{1,0:T(8,128)} %get-tuple-element.14.p0, ...), custom_call_target="tpu_custom_call" | custom-call | flops 42949672960 | bytes 150994944 | tf_op jit(solution)/shard_map/pallas_call | solution.py:780
  112.9 0.5 collective-permute-start.4
  113.4 0.6 collective-permute-start.5
  114.0 1.5 collective-permute-start.6
  115.4 0.8 collective-permute-done.4
  116.3 1.5 add.6
  117.8 0.0 collective-permute-start.7
  117.8 1.4 collective-permute-done.6.meta_ref
  119.2 0.5 copy-done.2
  119.7 0.1 copy-done.1
  119.9 37.2 %shard_map.78 = f32[640,16384]{1,0:T(8,128)} custom-call(bf16[16,512,1024]{2,1,0:T(8,128)(2,1)} %get-tuple-element.20.g_hbm, f32[32,512,512]{2,1,0:T(8,128)} %get-tuple-element.21.z_hbm, bf16[512,1280]{1,0:T(8,128)(2,1)} %bitcast.9, bf16[512,1280]{1,0:T(8,128)(2,1)} %copy-done, f32[264,128]{1,0:T(8,128)} %copy-done.1, s32[2,34]{1,0:T(2,128)} %copy-done.2), custom_call_target="tpu_custom_call" | custom-call | flops 21474836480 | bytes 109051904 | tf_op jit(solution)/shard_map/pallas_call | solution.py:799
  157.1 0.1 add.7
  157.2 0.0 collective-permute-start.8
  157.2 1.2 slice_bitcast_fusion
  158.4 1.8 %collective-permute-done.8 = f32[256,1280]{1,0:T(8,128)S(1)} collective-permute-done((f32[256,1280]{1,0:T(8,128)S(1)}, f32[256,1280]{1,0:T(8,128)S(1)}, u32[]{:S(2)}, u32[]{:S(2)}) %collective-permute-start.8) | collective-permute-done | bytes 1310752 | tf_op jit(solution)/shard_map/ppermute | solution.py:720
  160.3 1.7 %maximum_select_fusion = f32[2,256,1280]{2,1,0:T(8,128)} fusion(f32[1,256,1280]{2,1,0:T(8,128)S(1)} %bitcast.6, f32[1,256,1280]{2,1,0:T(8,128)S(1)} %bitcast.5, pred[]{:T(512)S(6)} %eq.3), kind=kLoop, calls=%fused_computation | loop fusion | flops 1966080 | bytes 5242881 | tf_op jit(solution)/shard_map/jit(_where)/select_n | solution.py:815
  (15 shorter events, 0.1 us)
Async XLA Ops:
  0.6 44.1 %collective-permute-start = (bf16[512,1280]{1,0:T(8,128)(2,1)}, bf16[512,1280]{1,0:T(8,128)(2,1)S(1)}, u32[]{:S(2)}, u32[]{:S(2)}) collective-permute-start(bf16[512,1280]{1,0:T(8,128)(2,1)} %bitcast.7), channel_id=1, source_target_pairs={{0,4},{4,0},{1,5},{5,1},{2,6},{6,2},{3,7},{7,3}} | collective-permute-start | bytes 3932168 | tf_op jit(solution)/shard_map/ppermute | solution.py:726
  38.6 1.9 %collective-permute-start.1 = (f32[152,128]{1,0:T(8,128)}, f32[152,128]{1,0:T(8,128)S(1)}, u32[]{:S(2)}, u32[]{:S(2)}) collective-permute-start(f32[152,128]{1,0:T(8,128)} %get-tuple-element.14.p0), channel_id=1, source_target_pairs={{0,1},{1,0},{2,3},{3,2},{4,5},{5,4},{6,7},{7,6}} | collective-permute-start | bytes 233480 | tf_op jit(solution)/shard_map/ppermute | solution.py:720
  38.6 5.5 %collective-permute-start.2 = (f32[152,128]{1,0:T(8,128)}, f32[152,128]{1,0:T(8,128)S(1)}, u32[]{:S(2)}, u32[]{:S(2)}) collective-permute-start(f32[152,128]{1,0:T(8,128)} %get-tuple-element.14.p0), channel_id=1, source_target_pairs={{0,2},{1,3},{2,0},{3,1},{4,6},{5,7},{6,4},{7,5}} | collective-permute-start | bytes 233480 | tf_op jit(solution)/shard_map/ppermute | solution.py:720
  39.5 5.3 %collective-permute-start.3 = (f32[152,128]{1,0:T(8,128)}, f32[152,128]{1,0:T(8,128)S(1)}, u32[]{:S(2)}, u32[]{:S(2)}) collective-permute-start(f32[152,128]{1,0:T(8,128)} %get-tuple-element.14.p0), channel_id=1, source_target_pairs={{0,3},{1,2},{2,1},{3,0},{4,7},{5,6},{6,5},{7,4}} | collective-permute-start | bytes 233480 | tf_op jit(solution)/shard_map/ppermute | solution.py:720
  40.5 4.3 %copy-start.3 = (f32[152,128]{1,0:T(8,128)}, f32[152,128]{1,0:T(8,128)S(1)}, u32[]{:S(2)}) copy-start(f32[152,128]{1,0:T(8,128)S(1)} %collective-permute-done.1.p1) | copy-start | bytes 233476
  44.1 0.7 copy-start.4
  44.8 0.6 copy-start.5
  44.8 1.1 copy-start
  45.9 68.1 %copy-start.6 = (s32[2,34]{1,0:T(2,128)S(1)}, s32[2,34]{1,0:T(2,128)}, u32[]{:S(2)}) copy-start(s32[2,34]{1,0:T(2,128)} %get-tuple-element.16.meta_ref) | copy-start | bytes 820
  112.9 3.4 %collective-permute-start.4 = (f32[256,1280]{1,0:T(8,128)}, f32[256,1280]{1,0:T(8,128)S(1)}, u32[]{:S(2)}, u32[]{:S(2)}) collective-permute-start(f32[256,1280]{1,0:T(8,128)} %get-tuple-element.19), channel_id=1, source_target_pairs={{0,1},{1,0},{2,3},{3,2},{4,5},{5,4},{6,7},{7,6}} | collective-permute-start | bytes 3932168 | tf_op jit(solution)/shard_map/ppermute | solution.py:720
  113.4 5.8 %collective-permute-start.5 = (f32[264,128]{1,0:T(8,128)}, f32[264,128]{1,0:T(8,128)S(1)}, u32[]{:S(2)}, u32[]{:S(2)}) collective-permute-start(f32[264,128]{1,0:T(8,128)} %get-tuple-element.22), channel_id=1, source_target_pairs={{0,4},{4,0},{1,5},{5,1},{2,6},{6,2},{3,7},{7,3}} | collective-permute-start | bytes 405512 | tf_op jit(solution)/shard_map/ppermute | solution.py:726
  114.0 5.3 %collective-permute-start.6 = (s32[2,34]{1,0:T(2,128)S(1)}, s32[2,34]{1,0:T(2,128)S(1)}, u32[]{:S(2)}, u32[]{:S(2)}) collective-permute-start(s32[2,34]{1,0:T(2,128)S(1)} %copy-done.6), channel_id=1, source_target_pairs={{0,4},{4,0},{1,5},{5,1},{2,6},{6,2},{3,7},{7,3}} | collective-permute-start | bytes 824 | tf_op jit(solution)/shard_map/ppermute | solution.py:726
  117.8 39.3 %collective-permute-start.7 = (f32[256,1280]{1,0:T(8,128)S(1)}, f32[256,1280]{1,0:T(8,128)S(1)}, u32[]{:S(2)}, u32[]{:S(2)}) collective-permute-start(f32[256,1280]{1,0:T(8,128)S(1)} %add.6), channel_id=1, source_target_pairs={{0,2},{1,3},{2,0},{3,1},{4,6},{5,7},{6,4},{7,5}} | collective-permute-start | bytes 3932168 | tf_op jit(solution)/shard_map/ppermute | solution.py:720
  119.2 0.5 copy-start.2
  119.2 0.6 copy-start.1
  157.2 3.1 %collective-permute-start.8 = (f32[256,1280]{1,0:T(8,128)S(1)}, f32[256,1280]{1,0:T(8,128)S(1)}, u32[]{:S(2)}, u32[]{:S(2)}) collective-permute-start(f32[256,1280]{1,0:T(8,128)S(1)} %add.7), channel_id=1, source_target_pairs={{0,1},{1,0},{2,3},{3,2},{4,5},{5,4},{6,7},{7,6}} | collective-permute-start | bytes 3932168 | tf_op jit(solution)/shard_map/ppermute | solution.py:720
